TPU v7x, 32 devices: a whole 2x2x4 slice. The times are simulated.
32 devices in a mesh: data: 32 (over z, y, x, core).
Axes of the slice: x: 2, y: 2, z: 4, core: 2. Of those that a mesh axis runs over, the one named last changes fastest.
Arguments:
- h_a: bfloat16 [16384, 512], P('data')
- h_b: bfloat16 [16384, 512], P('data')
- w_one: bfloat16 [512, 2048], replicated
- w_two: bfloat16 [2048, 2048], replicated
- w_three: bfloat16 [2048, 2048], replicated
- gain_one: float32 [2048], replicated
- bias_one: float32 [2048], replicated
- gain_two: float32 [2048], replicated
- bias_two: float32 [2048], replicated
Outputs:
- output 1: float32 [], replicated
- output 2: float32 [512, 2048], replicated
- output 3: float32 [2048, 2048], replicated
- output 4: float32 [2048, 2048], replicated
- output 5: float32 [2048], replicated
- output 6: float32 [2048], replicated
- output 7: float32 [2048], replicated
- output 8: float32 [2048], replicated
All inputs are finite; a program needn't handle non-finite values.
Results may differ from a plain program's by a relative error of at most 0.00114.
Values are sent between devices in bfloat16 or wider.
A program may use at most 1 GiB of HBM per device.

v0:
```python
import jax
import jax.numpy as jnp
from jax import lax
from jax.sharding import PartitionSpec as P

BN_EPS = 1e-5
STD_EPS = 1e-4
INV_WEIGHT = 2.0
VAR_WEIGHT = 1.0
COV_WEIGHT = 2.0


def layer_forward(x_in, weight, gain_vec, bias_vec, all_rows):
    pre_act = jnp.einsum('vnk,kd->vnd', x_in, weight, preferred_element_type=jnp.float32)
    moments = lax.psum(jnp.stack([jnp.sum(pre_act, axis=1), jnp.sum(pre_act * pre_act, axis=1)]), 'data')
    col_mean = moments[0] / all_rows
    col_var = moments[1] / all_rows - col_mean * col_mean
    inv_std = lax.rsqrt(col_var + BN_EPS)[:, None, :]
    normed = (pre_act - col_mean[:, None, :]) * inv_std
    act_val = gain_vec * normed + bias_vec
    return jnp.maximum(act_val, 0.0).astype(jnp.bfloat16), normed, act_val, inv_std


def layer_backward(d_out, normed, act_val, inv_std, gain_vec, all_rows):
    d_act = jnp.where(act_val > 0.0, d_out, 0.0)
    stat_sums = lax.psum(jnp.stack([jnp.sum(d_act, axis=1), jnp.sum(d_act * normed, axis=1)]), 'data')
    d_pre = inv_std * gain_vec * (d_act - stat_sums[0][:, None, :] / all_rows - normed * (stat_sums[1][:, None, :] / all_rows))
    return d_pre.astype(jnp.bfloat16), jnp.sum(stat_sums[1], axis=0), jnp.sum(stat_sums[0], axis=0)


def loss_from_stats(z_views, z_diff, col_sum, gram_mat, sq_sum, all_rows):
    col_mu = col_sum / all_rows
    cov_mat = (gram_mat - all_rows * col_mu[:, :, None] * col_mu[:, None, :]) / (all_rows - 1)
    diag_var = jnp.diagonal(cov_mat, axis1=1, axis2=2)
    std_vec = jnp.sqrt(diag_var + STD_EPS)
    hinge_on = (std_vec < 1.0).astype(jnp.float32)
    loss_val = (INV_WEIGHT * sq_sum / all_rows
                + VAR_WEIGHT * jnp.sum(jnp.maximum(1.0 - std_vec, 0.0))
                + COV_WEIGHT * (jnp.sum(cov_mat * cov_mat) - jnp.sum(diag_var * diag_var)))
    proj_dim = cov_mat.shape[-1]
    eye_mask = lax.broadcasted_iota(jnp.int32, (proj_dim, proj_dim), 0) == lax.broadcasted_iota(jnp.int32, (proj_dim, proj_dim), 1)
    grad_cov = jnp.where(eye_mask, (-VAR_WEIGHT * hinge_on / (2.0 * std_vec))[:, None, :], (2.0 * COV_WEIGHT) * cov_mat)
    g_hat = grad_cov.astype(jnp.bfloat16)
    row_part = jnp.einsum('woe,wef->wof', z_views, g_hat, preferred_element_type=jnp.float32)
    mean_part = jnp.einsum('vd,vde->ve', col_mu, g_hat.astype(jnp.float32), precision=lax.Precision.HIGHEST)
    d_inv = (2.0 * INV_WEIGHT / all_rows) * z_diff
    d_z = ((2.0 / (all_rows - 1)) * (row_part - mean_part[:, None, :]) + jnp.stack([d_inv, -d_inv])).astype(jnp.bfloat16)
    return loss_val, d_z


def solution(mesh):
    group_devs = mesh.shape['data']

    def local_step(h_a, h_b, w_one, w_two, w_three, gain_one, bias_one, gain_two, bias_two):
        all_rows = h_a.shape[0] * group_devs
        view_feats = jnp.stack([h_a, h_b])
        hidden_one, normed_one, act_one, inv_one = layer_forward(view_feats, w_one, gain_one, bias_one, all_rows)
        hidden_two, normed_two, act_two, inv_two = layer_forward(hidden_one, w_two, gain_two, bias_two, all_rows)
        z_views = jnp.einsum('vnk,kd->vnd', hidden_two, w_three, preferred_element_type=jnp.float32).astype(jnp.bfloat16)
        z_diff = z_views[0].astype(jnp.float32) - z_views[1].astype(jnp.float32)
        col_sum, gram_mat, sq_sum = lax.psum(
            (jnp.sum(z_views, axis=1, dtype=jnp.float32),
             jnp.einsum('woe,wof->wef', z_views, z_views, preferred_element_type=jnp.float32),
             jnp.sum(z_diff * z_diff)), 'data')
        loss_val, d_z = loss_from_stats(z_views, z_diff, col_sum, gram_mat, sq_sum, all_rows)
        grad_three = jnp.einsum('vnk,vnd->kd', hidden_two, d_z, preferred_element_type=jnp.float32)
        d_hidden_two = jnp.einsum('vnd,kd->vnk', d_z, w_three, preferred_element_type=jnp.float32)
        d_pre_two, gain_grad_two, bias_grad_two = layer_backward(d_hidden_two, normed_two, act_two, inv_two, gain_two, all_rows)
        grad_two = jnp.einsum('vnk,vnd->kd', hidden_one, d_pre_two, preferred_element_type=jnp.float32)
        d_hidden_one = jnp.einsum('vnd,kd->vnk', d_pre_two, w_two, preferred_element_type=jnp.float32)
        d_pre_one, gain_grad_one, bias_grad_one = layer_backward(d_hidden_one, normed_one, act_one, inv_one, gain_one, all_rows)
        grad_one = jnp.einsum('vnf,vnd->fd', view_feats, d_pre_one, preferred_element_type=jnp.float32)
        grad_one, grad_two, grad_three = lax.psum((grad_one, grad_two, grad_three), 'data')
        return loss_val, grad_one, grad_two, grad_three, gain_grad_one, bias_grad_one, gain_grad_two, bias_grad_two

    row_spec = P('data', None)
    return jax.shard_map(local_step, mesh=mesh,
                         in_specs=(row_spec, row_spec, P(), P(), P(), P(), P(), P(), P()),
                         out_specs=(P(), P(), P(), P(), P(), P(), P(), P()),
                         check_vma=False)
```

profile of v0, /device:TPU:0, one launch (start us, length us, event | category | flops | bytes accessed | tf_op | source)
XLA Modules:
  0.0 1526.8 jit_solution(472760815865279904)
XLA Ops:
  7.2 0.0 copy-start
  7.2 0.0 all-reduce.5.cloned.1.call-start
  7.2 1.5 copy-done
  8.8 6.9 fusion.50
  15.7 42.1 %psum.70 = f32[2,2,2048]{2,1,0:T(2,128)S(1)} all-reduce(f32[2,2,2048]{2,1,0:T(2,128)S(1)} %pad_maximum_fusion.3), channel_id=1, replica_groups=mesh['data'=32] {'data'}, use_global_device_ids=true, to_apply=%region_2.0 | all-reduce | flops 8192 | bytes 65536 | tf_op jit(solution)/shard_map/psum | solution.py:15
  57.8 0.0 copy-done.12
  57.8 0.0 copy-start.5
  57.8 0.6 fusion.38
  58.5 0.0 copy-done.15
  58.5 15.9 %fusion.49 = (f32[2,2048]{1,0:T(2,128)S(1)}, f32[2,2048]{1,0:T(2,128)S(1)}, f32[2,512,2048]{2,1,0:T(8,128)}) fusion(bf16[2048,2048]{1,0:T(8,128)(2,1)} %param.12, f32[2,512,2048]{2,1,0:T(8,128)} %get-tuple-element.42, f32[2048]{0:T(1024)S(1)} %copy-done.15, f32[2,2048]{1,0:T(2,128)S(1)} %get-tuple-element.37, f32[2,2048]{1,0:T(2,128)S(1)} %fusion.39, ...), kind=kOutput, calls=%fused_computation.92 | convolution fusion | flops 8608800768 | bytes 25247744 | tf_op jit(solution)/shard_map/vnk,kd->vnd/dot_general | solution.py:14
  74.3 0.0 copy-done.5
  74.3 0.0 copy-done.8
  74.4 40.9 %psum.71 = f32[2,2,2048]{2,1,0:T(2,128)S(1)} all-reduce(f32[2,2,2048]{2,1,0:T(2,128)S(1)} %pad_maximum_fusion.4), channel_id=1, replica_groups=mesh['data'=32] {'data'}, use_global_device_ids=true, to_apply=%region_5.0 | all-reduce | flops 8192 | bytes 65536 | tf_op jit(solution)/shard_map/psum | solution.py:15
  115.3 0.0 copy-done.11
  115.3 0.6 fusion.32
  115.9 0.0 copy-done.14
  115.9 13.8 convert_reduce_fusion
  129.7 0.0 copy-start.2
  129.7 2.0 copy-done.2
  131.7 15.3 %fusion.52 = f32[2,2048,2048]{2,1,0:T(8,128)} fusion(bf16[2,512,2048]{2,1,0:T(8,128)(2,1)S(1)} %get-tuple-element.45), kind=kOutput, calls=%fused_computation.94 | convolution fusion | flops 8589934592 | bytes 37748736 | tf_op jit(solution)/shard_map/woe,wof->wef/dot_general | solution.py:63
  147.1 0.0 all-reduce.5.cloned.1.call-update
  147.1 0.0 all-reduce.7.cloned.1.call-start
  147.1 41.1 %psum.74 = f32[2,2048]{1,0:T(2,128)S(1)} all-reduce(f32[2,2048]{1,0:T(2,128)S(1)} %get-tuple-element.44), channel_id=1, replica_groups=mesh['data'=32] {'data'}, use_global_device_ids=true, to_apply=%region_10.0 | all-reduce | flops 4096 | bytes 32768 | tf_op jit(solution)/shard_map/psum | solution.py:61
  188.3 7.6 fusion.20
  195.9 4.1 iota_compare_fusion
  199.9 444.3 %all-reduce.5.cloned.1.call-done = f32[2,2048,2048]{2,1,0:T(8,128)} async-done(((f32[2,2048,2048]{2,1,0:T(8,128)}), f32[2,2048,2048]{2,1,0:T(8,128)}) %all-reduce.5.cloned.1.call-update) | async-done | bytes 33554448 | tf_op jit(solution)/shard_map/psum | solution.py:61
  644.2 23.5 %multiply_reduce_fusion = (f32[]{:T(128)}, f32[2,2048,2048]{2,1,0:T(8,128)}) fusion(f32[2,2048,2048]{2,1,0:T(8,128)} %all-reduce.5.cloned.1.call-done, f32[2,2048]{1,0:T(2,128)S(1)} %get-tuple-element.40, f32[2,2048]{1,0:T(2,128)S(1)} %psum.74), kind=kLoop, calls=%fused_computation.2 | loop fusion | flops 41943040 | bytes 67141632 | tf_op jit(solution)/shard_map/reduce_sum | solution.py:39
  667.7 55.0 %copy.23 = f32[2,2048,2048]{2,0,1:T(2,128)} copy(f32[2,2048,2048]{2,1,0:T(8,128)} %get-tuple-element.28) | data formatting | bytes 67108864 | tf_op jit(solution)/shard_map/div | solution.py:33
  722.7 24.1 %gather_fusion = f32[2048,2]{0,1:T(2,128)S(1)} fusion(f32[2,2048,2048]{2,0,1:T(2,128)} %copy.23, s32[2048]{0:T(1024)S(1)} %bitcast.100), kind=kCustom, calls=%fused_computation | custom fusion | bytes 49152 | tf_op jit(solution)/shard_map/jit(diagonal)/gather | solution.py:34
  746.8 16.9 %fusion.40 = f32[2,1,2048]{2,1,0:T(1,128)S(1)} fusion(f32[2,2048,1]{1,0,2:T(2,128)S(1)} %get-tuple-element.41, f32[2,2048,2048]{2,1,0:T(8,128)} %all-reduce.5.cloned.1.call-done, bf16[2,2048]{1,0:T(2,128)(2,1)S(1)} %fusion.42, f32[2,2048]{1,0:T(2,128)S(1)} %get-tuple-element.40, f32[2,2048]{1,0:T(2,128)S(1)} %psum.74, pred[2048,2048]{1,0:T(8,128)(4,1)} %iota_compare_fusion), kind=kOutput, calls=%fused_computation.70 | convolution fusion | flops 134217728 | bytes 37822464 | tf_op jit(solution)/shard_map/vd,vde->ve/dot_general | solution.py:45
  763.8 19.5 %fusion.1 = bf16[2,512,2048]{2,1,0:T(8,128)(2,1)S(1)} fusion(f32[1,512,2048]{2,1,0:T(8,128)} %get-tuple-element.30, f32[1,512,2048]{2,1,0:T(8,128)} %get-tuple-element.29, bf16[2,512,2048]{2,1,0:T(8,128)(2,1)} %copy-done.2, f32[2,2048]{1,0:T(2,128)S(1)} %bitcast.109, f32[2,2048,2048]{2,1,0:T(8,128)} %all-reduce.5.cloned.1.call-done, ...), kind=kOutput, calls=%fused_computation.9 | convolution fusion | flops 8633974784 | bytes 54583296 | tf_op jit(solution)/shard_map/woe,wef->wof/dot_general | solution.py:44
  783.3 15.0 convolution_bitcast_fusion
  798.3 15.7 %fusion.48 = (f32[2,2048]{1,0:T(2,128)S(1)}, f32[2,2048]{1,0:T(2,128)S(1)}, f32[2,512,2048]{2,1,0:T(8,128)}) fusion(f32[2,2048]{1,0:T(2,128)S(1)} %get-tuple-element.39, f32[2,512,2048]{2,1,0:T(8,128)} %get-tuple-element.43, f32[2,2048]{1,0:T(2,128)S(1)} %fusion.33, bf16[2,512,2048]{2,1,0:T(8,128)(2,1)S(1)} %fusion.1, bf16[2048,2048]{1,0:T(8,128)(2,1)} %param.13, ...), kind=kOutput, calls=%fused_computation.91 | convolution fusion | flops 8608800768 | bytes 29442048 | tf_op jit(solution)/shard_map/vnd,kd->vnk/dot_general | solution.py:67
  814.0 40.2 %psum.75 = f32[2,2,2048]{2,1,0:T(2,128)S(1)} all-reduce(f32[2,2,2048]{2,1,0:T(2,128)S(1)} %pad_maximum_fusion.5), channel_id=1, replica_groups=mesh['data'=32] {'data'}, use_global_device_ids=true, to_apply=%region_16.17 | all-reduce | flops 8192 | bytes 65536 | tf_op jit(solution)/shard_map/psum | solution.py:26
  854.3 0.6 slice_reduce_fusion.3
  854.9 0.0 copy-done.10
  854.9 0.0 copy-start.16
  854.9 0.0 slice-start.4
  855.0 7.2 multiply_convert_fusion.1
  862.2 0.0 copy-done.6
  862.2 0.0 copy-done.9
  862.2 0.0 copy-done.13
  862.2 0.0 copy-done.16
  862.2 0.0 slice-start.5
  862.2 15.1 convolution_bitcast_fusion.1
  877.4 0.0 slice-done.4
  877.4 0.0 slice-done.5
  877.4 0.0 copy-start.4
  877.4 0.0 copy-start.7
  877.4 14.8 fusion.47
  892.2 40.1 %all-reduce = (f32[]{:T(128)}, f32[2,2,2048]{2,1,0:T(2,128)S(1)}) all-reduce(f32[]{:T(128)} %get-tuple-element.31, f32[2,2,2048]{2,1,0:T(2,128)S(1)} %pad_maximum_fusion.6), channel_id=1, replica_groups=mesh['data'=32] {'data'}, use_global_device_ids=true, to_apply=%region_7.0 | all-reduce | flops 8193 | bytes 65544 | tf_op jit(solution)/shard_map/psum | solution.py:61
  932.3 0.6 slice_reduce_fusion.1
  932.9 0.0 copy-done.3
  932.9 0.0 copy-done.7
  932.9 10.4 fusion.24
  943.4 0.0 all-reduce.7.cloned.1.call-update
  943.4 0.6 multiply_reduce_fusion.6
  946.4 545.7 %all-reduce.7.cloned.1.call-done = (f32[512,2048]{1,0:T(8,128)}, f32[2048,2048]{1,0:T(8,128)}, f32[2048,2048]{1,0:T(8,128)}) async-done(((f32[512,2048]{1,0:T(8,128)}, f32[2048,2048]{1,0:T(8,128)}, f32[2048,2048]{1,0:T(8,128)}), (f32[512,2048]{1,0:T(8,128)}, f32[2048,2048]{1,0:T(8,128)}, f32[2048,2048]{1,0:T(8,128)})) %all-reduce.7.cloned.1.call-update) | async-done | bytes 37748752 | tf_op jit(solution)/shard_map/psum | solution.py:73
  1492.1 4.8 copy.41
  1497.0 13.6 copy.42
  1510.6 0.0 slice-done.1
  1510.6 1.7 slice-done.3
  1512.3 6.3 copy.43
  1518.6 0.0 copy-done.1
  (30 shorter events, 0.2 us)
Async XLA Ops:
  7.2 1.6 copy-start
  7.2 637.0 %all-reduce.5.cloned.1.call-start = ((), (), s32[]{:S(2)}) async-start(), calls=%async_computation | async-start | bytes 67108864 | tf_op jit(solution)/shard_map/psum | solution.py:61
  8.8 49.0 %copy-start.12 = (f32[2048]{0:T(1024)S(1)}, f32[2048]{0:T(1024)}, u32[]{:S(2)}) copy-start(f32[2048]{0:T(1024)} %param.14) | copy-start | bytes 24580
  8.8 49.7 %copy-start.15 = (f32[2048]{0:T(1024)S(1)}, f32[2048]{0:T(1024)}, u32[]{:S(2)}) copy-start(f32[2048]{0:T(1024)} %param.15) | copy-start | bytes 24580
  57.8 16.5 %copy-start.5 = (f32[2,2048]{1,0:T(2,128)}, f32[2,2048]{1,0:T(2,128)S(1)}, u32[]{:S(2)}) copy-start(f32[2,2048]{1,0:T(2,128)S(1)} %fusion.39) | copy-start | bytes 49156
  58.4 15.9 %copy-start.8 = (f32[2,2048]{1,0:T(2,128)}, f32[2,2048]{1,0:T(2,128)S(1)}, u32[]{:S(2)}) copy-start(f32[2,2048]{1,0:T(2,128)S(1)} %get-tuple-element.37) | copy-start | bytes 49156
  58.5 56.8 %copy-start.11 = (f32[2048]{0:T(1024)S(1)}, f32[2048]{0:T(1024)}, u32[]{:S(2)}) copy-start(f32[2048]{0:T(1024)} %param.16) | copy-start | bytes 24580
  58.5 57.5 %copy-start.14 = (f32[2048]{0:T(1024)S(1)}, f32[2048]{0:T(1024)}, u32[]{:S(2)}) copy-start(f32[2048]{0:T(1024)} %param.17) | copy-start | bytes 24580
  129.7 2.0 copy-start.2
  147.1 1345.0 %all-reduce.7.cloned.1.call-start = ((), (), s32[]{:S(2)}) async-start(), calls=%async_computation.1 | async-start | bytes 75497472 | tf_op jit(solution)/shard_map/psum | solution.py:73
  798.3 56.6 %copy-start.10 = (f32[2,2048]{1,0:T(2,128)S(1)}, f32[2,2048]{1,0:T(2,128)}, u32[]{:S(2)}) copy-start(f32[2,2048]{1,0:T(2,128)} %get-tuple-element.38) | copy-start | bytes 49156
  854.9 7.3 copy-start.6
  854.9 7.3 copy-start.9
  854.9 7.3 copy-start.13
  854.9 7.3 copy-start.16
  854.9 22.4 %slice-start.4 = ((s8[8388608]{0:T(1024)(128)(4,1)}), s8[4194304]{0:T(1024)(128)(4,1)S(1)}, s32[]{:S(2)}) async-start(s8[8388608]{0:T(1024)(128)(4,1)} %bitcast.103), calls=%async_computation.6 | async-start | bytes 8388608
  862.2 15.1 slice-start.5
  877.4 55.6 %copy-start.3 = (bf16[512,512]{1,0:T(8,128)(2,1)S(1)}, bf16[512,512]{1,0:T(8,128)(2,1)}, u32[]{:S(2)}) copy-start(bf16[512,512]{1,0:T(8,128)(2,1)} %param.10) | copy-start | bytes 1572868
  877.4 55.6 %copy-start.4 = (bf16[512,512]{1,0:T(8,128)(2,1)S(1)}, bf16[512,512]{1,0:T(8,128)(2,1)}, u32[]{:S(2)}) copy-start(bf16[512,512]{1,0:T(8,128)(2,1)} %param.9) | copy-start | bytes 1572868
  877.4 55.6 %copy-start.7 = (f32[2,2048]{1,0:T(2,128)S(1)}, f32[2,2048]{1,0:T(2,128)}, u32[]{:S(2)}) copy-start(f32[2,2048]{1,0:T(2,128)} %get-tuple-element.36) | copy-start | bytes 49156
  1492.1 18.4 %slice-start = ((s8[16777216]{0:T(1024)(128)(4,1)}), s8[4194304]{0:T(1024)(128)(4,1)S(1)}, s32[]{:S(2)}) async-start(s8[16777216]{0:T(1024)(128)(4,1)} %bitcast.101), calls=%async_computation.2 | async-start | bytes 8388608
  1497.0 13.6 slice-start.1
  1497.0 13.6 slice-start.2
  1497.0 15.3 %slice-start.3 = ((s8[16777216]{0:T(1024)(128)(4,1)}), s8[4194304]{0:T(1024)(128)(4,1)S(1)}, s32[]{:S(2)}) async-start(s8[16777216]{0:T(1024)(128)(4,1)} %bitcast.101), calls=%async_computation.5 | async-start | bytes 8388608
  1512.3 6.3 copy-start.1
Sparse Core Ops, SparseCore 0:
  147.2 496.9 all-reduce.4
  943.5 548.5 all-reduce.6
where the time goes:
time: 1530 us
  waiting for transfers between devices  990 us (65%)
  blocking collectives  204 us (13%)
  matrix products  159 us (10%)
  local copies, waits for them, and re-layouts  109 us (7%)
  other arithmetic  45.7 us (3%)
  between operations  18.1 us (1%)
    psum x1, waiting for transfers between devices, local_step(): lax.psum((grad_one, grad_two, grad_three), 'data')  546 us
    psum x1, waiting for transfers between devices, local_step(): lax.psum((jnp.sum(z_views, axis=1, dtype=jnp.float32), jnp.einsum('woe,wo...  444 us
    psum x2, blocking collectives, layer_forward(): lax.psum(jnp.stack([jnp.sum(pre_act, axis=1), jnp.sum(pre_act * pre_act,...  83 us
    psum x2, blocking collectives, local_step(): lax.psum((jnp.sum(z_views, axis=1, dtype=jnp.float32), jnp.einsum('woe,wo...  81.2 us
    div x1, local copies, waits for them, and re-layouts, loss_from_stats(): (gram_mat - all_rows * col_mu[:, :, None] * col_mu[:, None, :]) / (all_ro...  55 us
    psum x1, blocking collectives, layer_backward(): lax.psum(jnp.stack([jnp.sum(d_act, axis=1), jnp.sum(d_act * normed, axis=...  40.2 us
  transfers between devices with their start and end apart: 2, of which 2 were waited for; matrix products, arithmetic and copies ran while one was open for 1% of the time, Pallas kernels for 0%

commit v1 on v0

v1 whole, which is shorter than its diff:
```python
import functools

import jax
import jax.numpy as jnp
from jax import lax
from jax.experimental import pallas as pl
from jax.experimental.pallas import tpu as pltpu
from jax.sharding import PartitionSpec as P

BN_EPS = 1e-5
STD_EPS = 1e-4
INV_WEIGHT = 2.0
VAR_WEIGHT = 1.0
COV_WEIGHT = 2.0

F32 = jnp.float32
BF16 = jnp.bfloat16
MESH = pl.DeviceIdType.MESH
VMEM_LIMIT = 67043328

ROWS = 1024
HALF = 512
FEAT = 512
DIM = 2048
NB = 8
BLK = 256
LAG = 2
RING = 4
ALL_ROWS = 16384


def sds(shape, dtype):
    return jax.ShapeDtypeStruct(shape, dtype)


ANY = pl.BlockSpec(memory_space=pl.ANY)
INV = pl.BlockSpec(memory_space=pltpu.VMEM)


class Place:
    def __init__(self):
        i = lax.axis_index('data')
        self.c = lax.rem(i, 2)
        x = lax.rem(i // 2, 2)
        y = lax.rem(i // 4, 2)
        z = i // 8
        zl = lax.rem(z, 2)
        zh = z // 2
        self.pc = i + 1 - 2 * self.c
        px = i + 2 - 4 * x
        py = i + 4 - 8 * y
        p1 = i + 8 - 16 * zl
        p2 = i + 16 - 32 * zh
        self.ring = (px, py, p1, p2)
        self.bits = ((x, zl, y, zh), (y, zl, x, zh))
        self.peers = ((px, p1, py, p2), (py, p1, px, p2))
        self.keep = []
        self.send = []
        for k in range(2):
            keep = [0]
            send = [None]
            for s in range(1, 5):
                n = BLK >> s
                bit = self.bits[k][s - 1]
                send.append(keep[-1] + (1 - bit) * n)
                keep.append(keep[-1] + bit * n)
            self.keep.append(keep)
            self.send.append(send)

    def barrier(self):
        sem = pltpu.get_barrier_semaphore()
        for p in (self.pc,) + self.ring:
            pl.semaphore_signal(sem, inc=1, device_id=(p,), device_id_type=MESH)
        pl.semaphore_wait(sem, 5)


def rcopy(src, dst, ssem, rsem, dev):
    return pltpu.make_async_remote_copy(src_ref=src, dst_ref=dst, send_sem=ssem, recv_sem=rsem,
                                        device_id=(dev,), device_id_type=MESH)


def rows_at(off, n):
    return pl.ds(pl.multiple_of(off, n), n)


def nn(a, b):
    return jnp.dot(a, b, preferred_element_type=F32)


def nt(a, b):
    return lax.dot_general(a, b, (((1,), (1,)), ((), ())), preferred_element_type=F32)


def tn(a, b):
    return lax.dot_general(a, b, (((0,), (0,)), ((), ())), preferred_element_type=F32)


def cols(j):
    return pl.ds(pl.multiple_of(j * BLK, BLK), BLK)


class Scatter:
    def __init__(self, place, part, lands, ssem, rsem, n_units, slots):
        self.pl, self.part, self.lands = place, part, lands
        self.ssem, self.rsem, self.n, self.slots = ssem, rsem, n_units, slots

    def copy(self, u, s, k):
        n = BLK >> s
        r = lax.rem(u, RING)
        return rcopy(self.part.at[lax.rem(u, self.slots), k, rows_at(self.pl.send[k][s], n)],
                     self.lands[s - 1].at[r, k], self.ssem.at[s - 1, k, r], self.rsem.at[s - 1, k, r],
                     self.pl.peers[k][s - 1])

    def begin(self, u):
        for k in range(2):
            self.copy(u, 1, k).start()

    def advance(self, t, final):
        for s in (4, 3, 2, 1):
            u = t - LAG * s

            @pl.when((u >= 0) & (u < self.n))
            def _(s=s, u=u):
                n = BLK >> s
                p, r = lax.rem(u, self.slots), lax.rem(u, RING)
                for k in range(2):
                    cp = self.copy(u, s, k)
                    cp.wait_send()
                    cp.wait_recv()
                    rr = rows_at(self.pl.keep[k][s], n)
                    self.part[p, k, rr] = self.part[p, k, rr] + self.lands[s - 1][r, k]
                    if s < 4:
                        self.copy(u, s + 1, k).start()
                if s == 4:
                    final(u)


def scatter_scratch(slots):
    return [pltpu.VMEM((slots, 2, BLK, BLK), F32)] + \
        [pltpu.VMEM((RING, 2, BLK >> s, BLK), F32) for s in range(1, 5)] + \
        [pltpu.SemaphoreType.DMA((4, 2, RING)), pltpu.SemaphoreType.DMA((4, 2, RING))]


class SmallReduce:
    def __init__(self, place, val, land, ssem, rsem):
        self.pl, self.val, self.land, self.ssem, self.rsem = place, val, land, ssem, rsem

    def copy(self, k):
        return rcopy(self.val, self.land.at[k], self.ssem.at[k], self.rsem.at[k], self.pl.ring[k])

    def start(self, k):
        self.copy(k).start()

    def finish(self, k):
        self.copy(k).wait()
        self.val[...] = self.val[...] + self.land[k]

    def run(self):
        for k in range(4):
            self.start(k)
            self.finish(k)


def small_scratch(n):
    return [pltpu.VMEM((n, BLK), F32), pltpu.VMEM((4, n, BLK), F32),
            pltpu.SemaphoreType.DMA((4,)), pltpu.SemaphoreType.DMA((4,))]


def forward_kernel(ha, hb, w1, w2, w3, gb, n1_o, n2_o, x1_o, x2_o, z_o, r_o, h_o,
                   h, w1v, w2v, w3v, u1, u2, x1, x2, z, s1, l1, a1, b1, s2, l2, a2, b2, hsem, wsem, osem):
    me = Place()
    loads = [pltpu.make_async_copy(w1, w1v, wsem.at[0]), pltpu.make_async_copy(w2, w2v, wsem.at[1]),
             pltpu.make_async_copy(w3, w3v, wsem.at[2])]
    mine = pl.ds(pl.multiple_of(me.c * HALF, HALF), HALF)
    for c, own in ((0, ha), (1, hb)):
        @pl.when(me.c == c)
        def _(own=own):
            pltpu.make_async_copy(own, h.at[mine], hsem.at[0]).start()
    loads[0].start()
    me.barrier()

    def exchange(src):
        return rcopy(src, h.at[mine], hsem.at[1], hsem.at[2], me.pc)
    for c, other in ((0, hb), (1, ha)):
        @pl.when(me.c == c)
        def _(other=other):
            exchange(other).start()
    loads[1].start()
    loads[2].start()
    loads[0].wait()
    pltpu.make_async_copy(ha, h.at[mine], hsem.at[0]).wait()
    exchange(ha).wait()
    out = []

    def save(src, dst):
        cp = pltpu.make_async_copy(src, dst, osem.at[len(out)])
        cp.start()
        out.append(cp)

    save(h, h_o)

    def matmul(src, w, dst, st):
        def step(j, carry):
            res = nn(src[...], w[:, cols(j)])
            dst[:, cols(j)] = res
            st[pl.ds(j, 1)] = jnp.sum(res, axis=0, keepdims=True)
            st[pl.ds(NB + j, 1)] = jnp.sum(res * res, axis=0, keepdims=True)
            return carry
        lax.fori_loop(0, NB, step, 0)

    def norm(u, x, st, layer):
        mean = st[0:NB] * (1.0 / ALL_ROWS)
        var = st[NB:2 * NB] * (1.0 / ALL_ROWS) - mean * mean
        st[0:NB] = mean
        st[NB:2 * NB] = lax.rsqrt(var + BN_EPS)

        def step(j, carry):
            nrm = (u[:, cols(j)] - st[pl.ds(j, 1)]) * st[pl.ds(NB + j, 1)]
            act = gb[pl.ds(2 * NB * layer + j, 1)] * nrm + gb[pl.ds(2 * NB * layer + NB + j, 1)]
            u[:, cols(j)] = nrm
            x[:, cols(j)] = jnp.maximum(act, 0.0).astype(BF16)
            return carry
        lax.fori_loop(0, NB, step, 0)

    matmul(h, w1v, u1, s1)
    SmallReduce(me, s1, l1, a1, b1).run()
    norm(u1, x1, s1, 0)
    save(u1, n1_o)
    save(x1, x1_o)
    loads[1].wait()
    matmul(x1, w2v, u2, s2)
    SmallReduce(me, s2, l2, a2, b2).run()
    norm(u2, x2, s2, 1)
    save(u2, n2_o)
    save(x2, x2_o)
    r_o[0:NB] = s1[NB:2 * NB]
    r_o[NB:2 * NB] = s2[NB:2 * NB]
    loads[2].wait()

    def step(j, carry):
        z[:, cols(j)] = nn(x2[...], w3v[:, cols(j)]).astype(BF16)
        return carry
    lax.fori_loop(0, NB, step, 0)
    save(z, z_o)
    for cp in out:
        cp.wait()


def forward(ha, hb, w1, w2, w3, gb):
    return pl.pallas_call(
        forward_kernel,
        out_shape=(sds((ROWS, DIM), F32), sds((ROWS, DIM), F32), sds((ROWS, DIM), BF16), sds((ROWS, DIM), BF16),
                   sds((ROWS, DIM), BF16), sds((2 * NB, BLK), F32), sds((ROWS, FEAT), BF16)),
        in_specs=[ANY] * 5 + [INV],
        out_specs=(ANY,) * 5 + (INV, ANY),
        scratch_shapes=[pltpu.VMEM((ROWS, FEAT), BF16), pltpu.VMEM((FEAT, DIM), BF16), pltpu.VMEM((DIM, DIM), BF16),
                        pltpu.VMEM((DIM, DIM), BF16), pltpu.VMEM((ROWS, DIM), F32), pltpu.VMEM((ROWS, DIM), F32),
                        pltpu.VMEM((ROWS, DIM), BF16), pltpu.VMEM((ROWS, DIM), BF16), pltpu.VMEM((ROWS, DIM), BF16)]
        + small_scratch(2 * NB) + small_scratch(2 * NB)
        + [pltpu.SemaphoreType.DMA((3,)), pltpu.SemaphoreType.DMA((3,)), pltpu.SemaphoreType.DMA((6,))],
        compiler_params=pltpu.CompilerParams(collective_id=0, has_side_effects=True, vmem_limit_bytes=VMEM_LIMIT),
        name='forward',
    )(ha, hb, w1, w2, w3, gb)


GRAM_UNITS = 18
GRAM_SLOTS = 4 * LAG + 2


def block_of(q):
    p, r = q // 9, lax.rem(q, 9)
    first = r < NB - p
    return jnp.where(first, p, NB - 1 - p), jnp.where(first, p + r, r - 1)


def gram_kernel(z_i, dz_o, loss_o, z, zo, part, r1, r2, r3, r4, ssem, rsem, gh, gfull, mut, dz,
                sv, sl, sa, sb, asem, bsem, csem):
    me = Place()
    load = pltpu.make_async_copy(z_i, z.at[pl.ds(0, ROWS)], csem.at[0])
    load.start()
    me.barrier()
    swap = rcopy(z_i, zo, csem.at[1], csem.at[2], me.pc)
    swap.start()
    load.wait()
    loss_o[...] = jnp.zeros_like(loss_o)

    def col_sum(j, carry):
        sv[pl.ds(j, 1)] = jnp.sum(z[0:ROWS, cols(j)].astype(F32), axis=0, keepdims=True)
        return carry
    lax.fori_loop(0, NB, col_sum, 0)
    red = SmallReduce(me, sv, sl, sa, sb)
    sc = Scatter(me, part, (r1, r2, r3, r4), ssem, rsem, GRAM_UNITS, GRAM_SLOTS)

    def compute(u):
        for k in range(2):
            i, j = block_of(2 * u + k)
            part[lax.rem(u, GRAM_SLOTS), k] = tn(z[0:ROWS, cols(i)], z[0:ROWS, cols(j)])

    def spread(u, s, k):
        rr = rows_at(me.keep[k][s], BLK >> s)
        r = lax.rem(u, RING)
        buf = gh.at[2 * u + k, rr]
        return rcopy(buf, buf, asem.at[s - 1, k, r], bsem.at[s - 1, k, r], me.peers[k][s - 1])

    def final(u):
        for k in range(2):
            i, j = block_of(2 * u + k)
            rr = rows_at(me.keep[k][4], 16)
            gram = part[lax.rem(u, GRAM_SLOTS), k, rr]
            mu_r = mut[pl.ds(pl.multiple_of(i * BLK + me.keep[k][4], 16), 16)]
            mu_c = sv[pl.ds(j, 1)]
            cov = (gram - ALL_ROWS * jnp.concatenate([mu_r, mu_r], axis=1) * mu_c) * (1.0 / (ALL_ROWS - 1))
            row = lax.broadcasted_iota(jnp.int32, (16, BLK), 0) + (i * BLK + me.keep[k][4])
            col = lax.broadcasted_iota(jnp.int32, (16, BLK), 1) + j * BLK
            diag = row == col
            std = jnp.sqrt(jnp.where(diag, cov, 1.0) + STD_EPS)
            hinge = jnp.where(std < 1.0, VAR_WEIGHT / (2.0 * std), 0.0)
            weight = jnp.where(i == j, COV_WEIGHT, 2.0 * COV_WEIGHT)
            term = jnp.where(diag, VAR_WEIGHT * jnp.maximum(1.0 - std, 0.0), weight * cov * cov)
            loss_o[...] = loss_o[...] + term[0:8] + term[8:16]
            gh[2 * u + k, rr] = jnp.where(diag, -hinge, (2.0 * COV_WEIGHT) * cov).astype(BF16)
            spread(u, 4, k).start()

    compute(0)

    def slot(t, carry):
        for s in range(4):
            @pl.when(t == s + 1)
            def _(s=s):
                red.finish(s)

            @pl.when(t == s)
            def _(s=s):
                red.start(s)

        @pl.when(t == 5)
        def _():
            mean = sv[...] * (1.0 / ALL_ROWS)
            sv[...] = mean
            hi = mean.astype(BF16)
            mid = (mean - hi.astype(F32)).astype(BF16)
            low = (mean - hi.astype(F32) - mid.astype(F32)).astype(BF16)
            for j in range(NB):
                for h in range(2):
                    lanes = slice(128 * h, 128 * h + 128)
                    dst = slice(j * BLK + 128 * h, j * BLK + 128 * h + 128)
                    mut[dst] = jnp.broadcast_to(mean[j:j + 1, lanes], (128, 128)).T
                z[ROWS:ROWS + 16, j * BLK:(j + 1) * BLK] = jnp.concatenate(
                    [hi[j:j + 1], mid[j:j + 1], low[j:j + 1], jnp.zeros((13, BLK), BF16)], axis=0)

        for s in (1, 2, 3, 4):
            u = t - LAG * (9 - s)

            @pl.when((u >= 0) & (u < GRAM_UNITS))
            def _(s=s, u=u):
                for k in range(2):
                    cp = spread(u, s, k)
                    cp.wait_send()
                    cp.wait_recv()
                    if s > 1:
                        spread(u, s - 1, k).start()
                if s == 1:
                    for k in range(2):
                        i, j = block_of(2 * u + k)
                        blk = gh[2 * u + k]
                        gfull[rows_at(i * BLK, BLK), cols(j)] = blk

                        @pl.when(i != j)
                        def _():
                            gfull[rows_at(j * BLK, BLK), cols(i)] = blk.T

        sc.advance(t, final)

        @pl.when(t < GRAM_UNITS)
        def _():
            sc.begin(t)

        @pl.when(t + 1 < GRAM_UNITS)
        def _():
            compute(t + 1)
        return carry
    lax.fori_loop(0, GRAM_UNITS + 8 * LAG, slot, 0)
    swap.wait()
    pull = 2.0 * INV_WEIGHT / ALL_ROWS

    def dz_block(j, carry):
        acc = nn(z[...], gfull[:, cols(j)])
        mean = acc[ROWS:ROWS + 1] + acc[ROWS + 1:ROWS + 2] + acc[ROWS + 2:ROWS + 3]
        diff = z[0:ROWS, cols(j)].astype(F32) - zo[:, cols(j)].astype(F32)
        sq = jnp.sum((diff * diff).reshape(ROWS // 8, 8, BLK), axis=0)
        loss_o[...] = loss_o[...] + (0.5 * INV_WEIGHT / ALL_ROWS) * sq
        dz[:, cols(j)] = (pull * diff + (2.0 / (ALL_ROWS - 1)) * (acc[0:ROWS] - mean)).astype(BF16)
        return carry
    lax.fori_loop(0, NB, dz_block, 0)
    store = pltpu.make_async_copy(dz, dz_o, csem.at[0])
    store.start()
    store.wait()


def gram(z):
    return pl.pallas_call(
        gram_kernel,
        out_shape=(sds((ROWS, DIM), BF16), sds((8, BLK), F32)),
        in_specs=[ANY],
        out_specs=(ANY, INV),
        scratch_shapes=[pltpu.VMEM((ROWS + 16, DIM), BF16), pltpu.VMEM((ROWS, DIM), BF16)]
        + scatter_scratch(GRAM_SLOTS)
        + [pltpu.VMEM((2 * GRAM_UNITS, BLK, BLK), BF16), pltpu.VMEM((DIM, DIM), BF16), pltpu.VMEM((DIM, 128), F32),
           pltpu.VMEM((ROWS, DIM), BF16)]
        + small_scratch(NB)
        + [pltpu.SemaphoreType.DMA((4, 2, RING)), pltpu.SemaphoreType.DMA((4, 2, RING)), pltpu.SemaphoreType.DMA((3,))],
        compiler_params=pltpu.CompilerParams(collective_id=1, has_side_effects=True, vmem_limit_bytes=VMEM_LIMIT),
        name='gram',
    )(z)


GRAD_UNITS = 36
GRAD_SLOTS = 5 * LAG + 2


def grad_kernel(dz_i, x2_i, x1_i, h_i, n2_i, n1_i, w3, w2, gb, rs_i, loss_i, g_o, st2_o, st1_o,
                dz, dzo, du2, du2o, x2h, x2o, x1h, x1o, hh, ho, wv, nv, da,
                part, r1, r2, r3, r4, ssem, rsem, s2, l2, a2, b2, s1, l1, a1, b1, e2, e1,
                asem, bsem, lsem, csem, dsem, esem):
    me = Place()
    c = me.c
    half = pl.ds(pl.multiple_of(c * 1024, 1024), 1024)
    ohalf = pl.ds(pl.multiple_of((1 - c) * 1024, 1024), 1024)
    hhalf = pl.ds(pl.multiple_of(c * 256, 256), 256)
    hohalf = pl.ds(pl.multiple_of((1 - c) * 256, 256), 256)
    loads = [pltpu.make_async_copy(dz_i, dz, csem.at[0]), pltpu.make_async_copy(x2_i.at[:, half], x2h, csem.at[1]),
             pltpu.make_async_copy(w3, wv, csem.at[2]), pltpu.make_async_copy(n2_i, nv, csem.at[3]),
             pltpu.make_async_copy(x1_i.at[:, half], x1h, csem.at[4]),
             pltpu.make_async_copy(h_i.at[:, hhalf], hh, csem.at[5])]
    load_w2 = pltpu.make_async_copy(w2, wv, csem.at[6])
    load_n1 = pltpu.make_async_copy(n1_i, nv, csem.at[7])
    swaps = [rcopy(dz_i, dzo, dsem.at[0], esem.at[0], me.pc),
             rcopy(x2_i.at[:, ohalf], x2o, dsem.at[1], esem.at[1], me.pc),
             rcopy(x1_i.at[:, ohalf], x1o, dsem.at[2], esem.at[2], me.pc),
             rcopy(h_i.at[:, hohalf], ho, dsem.at[3], esem.at[3], me.pc)]
    swap_du2 = rcopy(du2, du2o, dsem.at[4], esem.at[4], me.pc)
    swap_du1 = rcopy(dz, dzo, dsem.at[5], esem.at[5], me.pc)
    swap_s2 = rcopy(s2, e2, dsem.at[6], esem.at[6], me.pc)
    swap_s1 = rcopy(s1, e1, dsem.at[7], esem.at[7], me.pc)
    for cp in loads[:2]:
        cp.start()
    me.barrier()
    for cp in swaps[:2]:
        cp.start()
    for cp in loads[2:]:
        cp.start()
    for cp in swaps[2:]:
        cp.start()
    for cp in loads:
        cp.wait()
    for cp in swaps:
        cp.wait()
    s2[2 * NB:3 * NB] = loss_i[...]
    red2 = SmallReduce(me, s2, l2, a2, b2)
    red1 = SmallReduce(me, s1, l1, a1, b1)
    sc = Scatter(me, part, (r1, r2, r3, r4), ssem, rsem, GRAD_UNITS, GRAD_SLOTS)

    def compute(u):
        p = lax.rem(u, GRAD_SLOTS)
        v = lax.rem(u, 16)
        rb, cb = cols(v // 4), pl.ds(pl.multiple_of(lax.rem(v, 4) * 512, 512), 512)
        for w, (la, lb, ra, rb_) in enumerate(((x2h, x2o, dz, dzo), (x1h, x1o, du2, du2o), (hh, ho, dz, dzo))):
            @pl.when(u // 16 == w)
            def _(w=w, la=la, lb=lb, ra=ra, rb_=rb_):
                lc = slice(None) if w == 2 else rb
                res = tn(la[:, lc], ra[:, cb]) + tn(lb[:, lc], rb_[:, cb])
                part[p, 0] = res[:, 0:BLK]
                part[p, 1] = res[:, BLK:2 * BLK]

    def base(u):
        w, v = u // 16, lax.rem(u, 16)
        own = jnp.where(w == 2, 256, 1024)
        return w * 2048 + c * own + (v // 4) * 256, lax.rem(v, 4) * 512

    def region(u, k, off, n):
        r0, c0 = base(u)
        return g_o.at[rows_at(r0 + off, n), pl.ds(pl.multiple_of(c0 + k * BLK, BLK), BLK)]

    def keep_copy(u, k):
        return pltpu.make_async_copy(part.at[lax.rem(u, GRAD_SLOTS), k, rows_at(me.keep[k][4], 16)],
                                     region(u, k, me.keep[k][4], 16), lsem.at[k, lax.rem(u, RING)])

    def spread(u, s, k):
        n = BLK >> s
        r = lax.rem(u, RING)
        dst = region(u, k, me.keep[k][s], n)
        src = part.at[lax.rem(u, GRAD_SLOTS), k, rows_at(me.keep[k][4], 16)] if s == 4 else dst
        return rcopy(src, dst, asem.at[s, k, r], bsem.at[s, k, r], me.peers[k][s - 1])

    def cross(u):
        r = lax.rem(u, RING)
        r0, c0 = base(u)
        reg = g_o.at[rows_at(r0, BLK), pl.ds(pl.multiple_of(c0, 512), 512)]
        return rcopy(reg, reg, asem.at[0, 0, r], bsem.at[0, 0, r], me.pc)

    def final(u):
        for k in range(2):
            spread(u, 4, k).start()
            keep_copy(u, k).start()

    def back_block(j, grad, st, layer):
        dx = nt(grad[...], wv[cols(j)])
        nrm = nv[:, cols(j)]
        act = gb[pl.ds(2 * NB * layer + j, 1)] * nrm + gb[pl.ds(2 * NB * layer + NB + j, 1)]
        d_act = jnp.where(act > 0.0, dx, 0.0)
        da[:, cols(j)] = d_act
        st[pl.ds(j, 1)] = jnp.sum(d_act, axis=0, keepdims=True)
        st[pl.ds(NB + j, 1)] = jnp.sum(d_act * nrm, axis=0, keepdims=True)

    def back_pre(dst, st, layer):
        def step(j, carry):
            scale = gb[pl.ds(2 * NB * layer + j, 1)] * rs_i[pl.ds(NB * layer + j, 1)]
            m0 = st[pl.ds(j, 1)] * (1.0 / ALL_ROWS)
            m1 = st[pl.ds(NB + j, 1)] * (1.0 / ALL_ROWS)
            dst[:, cols(j)] = (scale * (da[:, cols(j)] - m0 - nv[:, cols(j)] * m1)).astype(BF16)
            return carry
        lax.fori_loop(0, NB, step, 0)

    compute(0)

    def slot(t, carry):
        u = t - LAG * 9

        @pl.when((u >= 0) & (u < GRAD_UNITS))
        def _(u=u):
            cross(u).wait()

        for s in (1, 2, 3, 4):
            u = t - LAG * (9 - s)

            @pl.when((u >= 0) & (u < GRAD_UNITS))
            def _(s=s, u=u):
                for k in range(2):
                    cp = spread(u, s, k)
                    cp.wait_send()
                    cp.wait_recv()
                    if s == 4:
                        keep_copy(u, k).wait()
                    if s > 1:
                        spread(u, s - 1, k).start()
                if s == 1:
                    cross(u).start()

        sc.advance(t, final)

        @pl.when(t < GRAD_UNITS)
        def _():
            sc.begin(t)

        for first, grad, st, layer, red, dst, swap_d, swap_s, nxt in (
                (0, dz, s2, 1, red2, du2, swap_du2, swap_s2, load_n1),
                (13, du2, s1, 0, red1, dz, swap_du1, swap_s1, None)):
            @pl.when((t >= first) & (t < first + NB))
            def _(first=first, grad=grad, st=st, layer=layer):
                back_block(t - first, grad, st, layer)

            if nxt is not None:
                @pl.when(t == first + NB - 1)
                def _():
                    load_w2.start()
            for k in range(4):
                @pl.when(t == first + NB + k + 1)
                def _(red=red, k=k):
                    red.finish(k)

                @pl.when(t == first + NB + k)
                def _(red=red, k=k):
                    red.start(k)

            @pl.when(t == first + NB + 4)
            def _(st=st, layer=layer, dst=dst, swap_d=swap_d, swap_s=swap_s, nxt=nxt):
                back_pre(dst, st, layer)
                swap_d.start()
                swap_s.start()
                if nxt is not None:
                    nxt.start()
                    load_w2.wait()
                    nxt.wait()

        @pl.when(t == 15)
        def _():
            swap_du2.wait()

        @pl.when(t == 31)
        def _():
            swap_du1.wait()

        @pl.when(t + 1 < GRAD_UNITS)
        def _():
            compute(t + 1)
        return carry
    lax.fori_loop(0, GRAD_UNITS + 9 * LAG, slot, 0)
    swap_s2.wait()
    swap_s1.wait()
    st2_o[...] = s2[...] + e2[...]
    st1_o[...] = s1[...] + e1[...]


def gradients(dz, x2, x1, h, n2, n1, w3, w2, gb, rs, loss):
    act = pltpu.VMEM((ROWS, DIM), BF16)
    part = pltpu.VMEM((ROWS, 1024), BF16)
    dma = pltpu.SemaphoreType.DMA
    return pl.pallas_call(
        grad_kernel,
        out_shape=(sds((2 * DIM + FEAT, DIM), F32), sds((3 * NB, BLK), F32), sds((2 * NB, BLK), F32)),
        in_specs=[ANY] * 8 + [INV] * 3,
        out_specs=(ANY, INV, INV),
        scratch_shapes=[act, act, act, act, part, part, part, part, pltpu.VMEM((ROWS, 256), BF16),
                        pltpu.VMEM((ROWS, 256), BF16), pltpu.VMEM((DIM, DIM), BF16), pltpu.VMEM((ROWS, DIM), F32),
                        pltpu.VMEM((ROWS, DIM), F32)]
        + scatter_scratch(GRAD_SLOTS) + small_scratch(3 * NB) + small_scratch(2 * NB)
        + [pltpu.VMEM((3 * NB, BLK), F32), pltpu.VMEM((2 * NB, BLK), F32),
           dma((5, 2, RING)), dma((5, 2, RING)), dma((2, RING)), dma((8,)), dma((8,)), dma((8,))],
        compiler_params=pltpu.CompilerParams(collective_id=2, has_side_effects=True, vmem_limit_bytes=VMEM_LIMIT),
        name='gradients',
    )(dz, x2, x1, h, n2, n1, w3, w2, gb, rs, loss)


def solution(mesh):
    def local_step(h_a, h_b, w_one, w_two, w_three, gain_one, bias_one, gain_two, bias_two):
        gb = jnp.stack([gain_one, bias_one, gain_two, bias_two]).reshape(4 * NB, BLK)
        n1, n2, x1, x2, z, rs, h = forward(h_a, h_b, w_one, w_two, w_three, gb)
        dz, loss_part = gram(z)
        grads, st2, st1 = gradients(dz, x2, x1, h, n2, n1, w_three, w_two, gb, rs, loss_part)
        loss = jnp.sum(st2[2 * NB:])
        return (loss, grads[2 * DIM:], grads[DIM:2 * DIM], grads[:DIM],
                st1[NB:2 * NB].reshape(DIM), st1[:NB].reshape(DIM),
                st2[NB:2 * NB].reshape(DIM), st2[:NB].reshape(DIM))

    row_spec = P('data', None)
    return jax.shard_map(local_step, mesh=mesh,
                         in_specs=(row_spec, row_spec, P(), P(), P(), P(), P(), P(), P()),
                         out_specs=(P(), P(), P(), P(), P(), P(), P(), P()),
                         check_vma=False)
```

time: 1530 us -> 523 us (0.34)
  waiting for transfers between devices: 990 us -> 0 us
  Pallas kernels: 0 us -> 490 us
  blocking collectives: 204 us -> 0 us
  matrix products: 159 us -> 0 us
  local copies, waits for them, and re-layouts: 109 us -> 29.7 us
  other arithmetic: 45.7 us -> 2.12 us
  between operations: 18.1 us -> 0.66 us
    psum x2 -> x0, waiting for transfers between devices: 990 us -> none  [the longest x1 546 us: local_step(): lax.psum((grad_one, grad_two, grad_three), 'data')]
    pallas_call x0 -> x3, Pallas kernels: none -> 490 us  [the longest x1 296 us: gradients(): pl.pallas_call(grad_kernel, out_shape=(sds((2 * DIM + FEAT, DIM), F32), s...]
    psum x5 -> x0, blocking collectives: 204 us -> none  [the longest x2 83 us: layer_forward(): lax.psum(jnp.stack([jnp.sum(pre_act, axis=1), jnp.sum(pre_act * pre_act,...]
    dot_general x11 -> x0, matrix products: 159 us -> none  [the longest x2 22.8 us: layer_forward(): jnp.einsum('vnk,kd->vnd', x_in, weight, preferred_element_type=jnp.float32)]
    div x1 -> x0, local copies, waits for them, and re-layouts: 55 us -> none  [loss_from_stats(): (gram_mat - all_rows * col_mu[:, :, None] * col_mu[:, None, :]) / (all_ro...]
    unnamed x49 -> x5, local copies, waits for them, and re-layouts: 30.1 us -> 3.13 us
    slice x0 -> x2, local copies, waits for them, and re-layouts: none -> 25.9 us  [the longest x1 21.2 us: local_step(): grads[:DIM]]
    reduce_sum x4 -> x0, other arithmetic: 25.5 us -> none  [the longest x1 23.5 us: loss_from_stats(): jnp.sum(cov_mat * cov_mat) - jnp.sum(diag_var * diag_var)]
  transfers between devices with their start and end apart: 2 -> 0, of which waited for: 2 -> 0; matrix products, arithmetic and copies ran while one was open for 1% -> 0% of each run, Pallas kernels for 0% -> 0%
where the time goes in v1:
time: 523 us; the launch traced here: 522 us
  Pallas kernels  490 us (94%)
  local copies, waits for them, and re-layouts  29.7 us (6%)
    pallas_call x1, Pallas kernels, gradients(): pl.pallas_call(grad_kernel, out_shape=(sds((2 * DIM + FEAT, DIM), F32), s...  296 us
    pallas_call x1, Pallas kernels, gram(): pl.pallas_call(gram_kernel, out_shape=(sds((ROWS, DIM), BF16), sds((8, BL...  134 us
    pallas_call x1, Pallas kernels, forward(): pl.pallas_call(forward_kernel, out_shape=(sds((ROWS, DIM), F32), sds((ROW...  60.3 us
    slice x1, local copies, waits for them, and re-layouts, local_step(): grads[:DIM]  21.2 us

profile of v1, /device:TPU:0, one launch (start us, length us, event | category | flops | bytes accessed | tf_op | source)
XLA Modules:
  0.0 522.4 jit_solution(7569619864168450949)
XLA Ops:
  0.6 0.8 pad_maximum_fusion
  1.4 0.6 reshape.31.gb
  2.1 60.3 %forward.1 = (f32[1024,2048]{1,0:T(8,128)}, f32[1024,2048]{1,0:T(8,128)}, bf16[1024,2048]{1,0:T(8,128)(2,1)}, bf16[1024,2048]{1,0:T(8,128)(2,1)}, bf16[1024,2048...) custom-call(bf16[512,512]{1,0:T(8,128)(2,1)} %ha.1, bf16[512,512]{1,0:T(8,128)(2,1)} %hb.1, ...), custom_call_target="tpu_custom_call" | custom-call | tf_op jit(solution)/shard_map/forward/pallas_call | solution.py:250
  62.4 133.6 %gram.1 = (bf16[1024,2048]{1,0:T(8,128)(2,1)}, f32[8,256]{1,0:T(8,128)}) custom-call(bf16[1024,2048]{1,0:T(8,128)(2,1)} %get-tuple-element.20.z_i), custom_call_target="tpu_custom_call" | custom-call | tf_op jit(solution)/shard_map/gram/pallas_call | solution.py:401
  196.0 296.0 %gradients.1 = (f32[4608,2048]{1,0:T(8,128)}, f32[24,256]{1,0:T(8,128)}, f32[16,256]{1,0:T(8,128)}) custom-call(bf16[1024,2048]{1,0:T(8,128)(2,1)} %get-tuple-element.21.dz_i, bf16[1024,2048]{1,0:T(8,128)(2,1)} %get-tuple-element.22.x2_i, bf16[1024,2048]{1,0:T(8,128)(2,1)} %get-tuple-element.23.x1_i, bf16[1024,512]{1,0:T(8,128)(2,1)} %get-tuple-element.24.h_i, ...), custom_call_target="tpu_custom_call" | custom-call | tf_op jit(solution)/shard_map/gradients/pallas_call | solution.py:608
  492.0 1.3 slice_bitcast_fusion
  493.4 0.6 copy.20
  494.0 0.6 copy.19
  494.6 0.7 slice_bitcast_fusion.2
  495.3 0.6 copy.18
  495.9 0.6 copy.17
  496.5 4.7 slice.25
  501.2 21.2 %fusion = (f32[2048,2048]{1,0:T(8,128)}, f32[2048,2048]{1,0:T(8,128)}) fusion(f32[4608,2048]{1,0:T(8,128)} %get-tuple-element.30), kind=kLoop, calls=%fused_computation.6 | loop fusion | bytes 67108864 | tf_op jit(solution)/shard_map/slice | solution.py:631

commit v2 on v1

v2 whole, which is shorter than its diff:
```python
import functools

import jax
import jax.numpy as jnp
from jax import lax
from jax.experimental import pallas as pl
from jax.experimental.pallas import tpu as pltpu
from jax.sharding import PartitionSpec as P

BN_EPS = 1e-5
STD_EPS = 1e-4
INV_WEIGHT = 2.0
VAR_WEIGHT = 1.0
COV_WEIGHT = 2.0

F32 = jnp.float32
BF16 = jnp.bfloat16
MESH = pl.DeviceIdType.MESH
VMEM_LIMIT = 67043328

ROWS = 1024
HALF = 512
FEAT = 512
DIM = 2048
NB = 8
BLK = 256
LAG = 2
RING = 4
ALL_ROWS = 16384


def sds(shape, dtype):
    return jax.ShapeDtypeStruct(shape, dtype)


ANY = pl.BlockSpec(memory_space=pl.ANY)
INV = pl.BlockSpec(memory_space=pltpu.VMEM)


class Place:
    def __init__(self):
        i = lax.axis_index('data')
        self.c = lax.rem(i, 2)
        x = lax.rem(i // 2, 2)
        y = lax.rem(i // 4, 2)
        z = i // 8
        zl = lax.rem(z, 2)
        zh = z // 2
        self.pc = i + 1 - 2 * self.c
        px = i + 2 - 4 * x
        py = i + 4 - 8 * y
        p1 = i + 8 - 16 * zl
        p2 = i + 16 - 32 * zh
        self.ring = (px, py, p1, p2)
        self.bits = ((x, zl, y, zh), (y, zl, x, zh))
        self.peers = ((px, p1, py, p2), (py, p1, px, p2))
        self.keep = []
        self.send = []
        for k in range(2):
            keep = [0]
            send = [None]
            for s in range(1, 5):
                n = BLK >> s
                bit = self.bits[k][s - 1]
                send.append(keep[-1] + (1 - bit) * n)
                keep.append(keep[-1] + bit * n)
            self.keep.append(keep)
            self.send.append(send)

    def barrier(self):
        sem = pltpu.get_barrier_semaphore()
        for p in (self.pc,) + self.ring:
            pl.semaphore_signal(sem, inc=1, device_id=(p,), device_id_type=MESH)
        pl.semaphore_wait(sem, 5)


def rcopy(src, dst, ssem, rsem, dev):
    return pltpu.make_async_remote_copy(src_ref=src, dst_ref=dst, send_sem=ssem, recv_sem=rsem,
                                        device_id=(dev,), device_id_type=MESH)


def rows_at(off, n):
    return pl.ds(pl.multiple_of(off, n), n)


def nn(a, b):
    return jnp.dot(a, b, preferred_element_type=F32)


def nt(a, b):
    return lax.dot_general(a, b, (((1,), (1,)), ((), ())), preferred_element_type=F32)


def tn(a, b):
    return lax.dot_general(a, b, (((0,), (0,)), ((), ())), preferred_element_type=F32)


def cols(j):
    return pl.ds(pl.multiple_of(j * BLK, BLK), BLK)


class Scatter:
    def __init__(self, place, part, lands, ssem, rsem):
        self.pl, self.part, self.lands, self.ssem, self.rsem = place, part, lands, ssem, rsem

    def copy(self, u, s, k):
        n = BLK >> s
        r = lax.rem(u, RING)
        return rcopy(self.part.at[lax.rem(u, SLOTS), k, rows_at(self.pl.send[k][s], n)],
                     self.lands[s - 1].at[r, k], self.ssem.at[s - 1, k, r], self.rsem.at[s - 1, k, r],
                     self.pl.peers[k][s - 1])

    def begin(self, u):
        for k in range(2):
            self.copy(u, 1, k).start()

    def advance(self, t, final):
        for s in (4, 3, 2, 1):
            u, ok = unit_at(t - LAG * s)

            @pl.when(ok)
            def _(s=s, u=u):
                n = BLK >> s
                p, r = lax.rem(u, SLOTS), lax.rem(u, RING)
                for k in range(2):
                    cp = self.copy(u, s, k)
                    cp.wait_send()
                    cp.wait_recv()
                    rr = rows_at(self.pl.keep[k][s], n)
                    self.part[p, k, rr] = self.part[p, k, rr] + self.lands[s - 1][r, k]
                    if s < 4:
                        self.copy(u, s + 1, k).start()
                if s == 4:
                    final(u)


def scatter_scratch(slots):
    return [pltpu.VMEM((slots, 2, BLK, BLK), F32)] + \
        [pltpu.VMEM((RING, 2, BLK >> s, BLK), F32) for s in range(1, 5)] + \
        [pltpu.SemaphoreType.DMA((4, 2, RING)), pltpu.SemaphoreType.DMA((4, 2, RING))]


class SmallReduce:
    def __init__(self, place, val, land, ssem, rsem):
        self.pl, self.val, self.land, self.ssem, self.rsem = place, val, land, ssem, rsem

    def copy(self, k):
        return rcopy(self.val, self.land.at[k], self.ssem.at[k], self.rsem.at[k], self.pl.ring[k])

    def start(self, k):
        self.copy(k).start()

    def finish(self, k):
        self.copy(k).wait()
        self.val[...] = self.val[...] + self.land[k]

    def run(self):
        for k in range(4):
            self.start(k)
            self.finish(k)


def small_scratch(n):
    return [pltpu.VMEM((n, BLK), F32), pltpu.VMEM((4, n, BLK), F32),
            pltpu.SemaphoreType.DMA((4,)), pltpu.SemaphoreType.DMA((4,))]


def forward_kernel(ha, hb, w1, w2, w3, gb, n1_o, n2_o, x1_o, x2_o, z_o, r_o, h_o,
                   h, w1v, w2v, w3v, u1, u2, x1, x2, z, s1, l1, a1, b1, s2, l2, a2, b2, hsem, wsem, osem):
    me = Place()
    loads = [pltpu.make_async_copy(w1, w1v, wsem.at[0]), pltpu.make_async_copy(w2, w2v, wsem.at[1]),
             pltpu.make_async_copy(w3, w3v, wsem.at[2])]
    mine = pl.ds(pl.multiple_of(me.c * HALF, HALF), HALF)
    for c, own in ((0, ha), (1, hb)):
        @pl.when(me.c == c)
        def _(own=own):
            pltpu.make_async_copy(own, h.at[mine], hsem.at[0]).start()
    loads[0].start()
    me.barrier()

    def exchange(src):
        return rcopy(src, h.at[mine], hsem.at[1], hsem.at[2], me.pc)
    for c, other in ((0, hb), (1, ha)):
        @pl.when(me.c == c)
        def _(other=other):
            exchange(other).start()
    loads[1].start()
    loads[2].start()
    loads[0].wait()
    pltpu.make_async_copy(ha, h.at[mine], hsem.at[0]).wait()
    exchange(ha).wait()
    out = []

    def save(src, dst):
        cp = pltpu.make_async_copy(src, dst, osem.at[len(out)])
        cp.start()
        out.append(cp)

    save(h, h_o)

    def matmul(src, w, dst, st):
        def step(j, carry):
            res = nn(src[...], w[:, cols(j)])
            dst[:, cols(j)] = res
            st[pl.ds(j, 1)] = jnp.sum(res, axis=0, keepdims=True)
            st[pl.ds(NB + j, 1)] = jnp.sum(res * res, axis=0, keepdims=True)
            return carry
        lax.fori_loop(0, NB, step, 0)

    def norm(u, x, st, layer):
        mean = st[0:NB] * (1.0 / ALL_ROWS)
        var = st[NB:2 * NB] * (1.0 / ALL_ROWS) - mean * mean
        st[0:NB] = mean
        st[NB:2 * NB] = lax.rsqrt(var + BN_EPS)

        def step(j, carry):
            nrm = (u[:, cols(j)] - st[pl.ds(j, 1)]) * st[pl.ds(NB + j, 1)]
            act = gb[pl.ds(2 * NB * layer + j, 1)] * nrm + gb[pl.ds(2 * NB * layer + NB + j, 1)]
            u[:, cols(j)] = nrm
            x[:, cols(j)] = jnp.maximum(act, 0.0).astype(BF16)
            return carry
        lax.fori_loop(0, NB, step, 0)

    matmul(h, w1v, u1, s1)
    SmallReduce(me, s1, l1, a1, b1).run()
    norm(u1, x1, s1, 0)
    save(u1, n1_o)
    save(x1, x1_o)
    loads[1].wait()
    matmul(x1, w2v, u2, s2)
    SmallReduce(me, s2, l2, a2, b2).run()
    norm(u2, x2, s2, 1)
    save(u2, n2_o)
    save(x2, x2_o)
    r_o[0:NB] = s1[NB:2 * NB]
    r_o[NB:2 * NB] = s2[NB:2 * NB]
    loads[2].wait()

    def step(j, carry):
        z[:, cols(j)] = nn(x2[...], w3v[:, cols(j)]).astype(BF16)
        return carry
    lax.fori_loop(0, NB, step, 0)
    save(z, z_o)
    for cp in out:
        cp.wait()


def forward(ha, hb, w1, w2, w3, gb):
    return pl.pallas_call(
        forward_kernel,
        out_shape=(sds((ROWS, DIM), F32), sds((ROWS, DIM), F32), sds((ROWS, DIM), BF16), sds((ROWS, DIM), BF16),
                   sds((ROWS, DIM), BF16), sds((2 * NB, BLK), F32), sds((ROWS, FEAT), BF16)),
        in_specs=[ANY] * 5 + [INV],
        out_specs=(ANY,) * 5 + (INV, ANY),
        scratch_shapes=[pltpu.VMEM((ROWS, FEAT), BF16), pltpu.VMEM((FEAT, DIM), BF16), pltpu.VMEM((DIM, DIM), BF16),
                        pltpu.VMEM((DIM, DIM), BF16), pltpu.VMEM((ROWS, DIM), F32), pltpu.VMEM((ROWS, DIM), F32),
                        pltpu.VMEM((ROWS, DIM), BF16), pltpu.VMEM((ROWS, DIM), BF16), pltpu.VMEM((ROWS, DIM), BF16)]
        + small_scratch(2 * NB) + small_scratch(2 * NB)
        + [pltpu.SemaphoreType.DMA((3,)), pltpu.SemaphoreType.DMA((3,)), pltpu.SemaphoreType.DMA((6,))],
        compiler_params=pltpu.CompilerParams(collective_id=0, has_side_effects=True, vmem_limit_bytes=VMEM_LIMIT),
        name='forward',
    )(ha, hb, w1, w2, w3, gb)


GRAM_UNITS = 18
UNITS = 54
SLOTS = 5 * LAG + 2
START_3 = 26
START_2 = 46
END = START_2 + 20 + 9 * LAG
DZ_SLOTS = (23, 28, 32, 34)
PASS_2 = 35
PASS_1 = 45


def block_of(q):
    i = jnp.int32(0)
    for first in (8, 15, 21, 26, 30, 33, 35):
        i = i + jnp.where(q >= first, 1, 0)
    return i, i + q - (17 * i - i * i) // 2


def unit_at(t):
    u = jnp.where(t < START_3, t, jnp.where(t < START_2, t - (START_3 - 18), t - (START_2 - 34)))
    ok = ((t >= 0) & (t < 18)) | ((t >= START_3) & (t < START_3 + 16)) | ((t >= START_2) & (t < START_2 + 20))
    return jnp.where(ok, u, 0), ok


def back_kernel(z_i, x2_i, x1_i, h_i, n2_i, n1_i, w3, w2, gb, rs_i, g_o, st2_o, st1_o,
                zd, zod, dz, dzo, gw, x2h, x2o, x1h, x1o, hh, ho, nv, da, mut, lacc,
                part, r1, r2, r3, r4, ssem, rsem, sv, sl, sa, sb, s2, l2, a2, b2, s1, l1, a1, b1, e2, e1,
                gasem, gbsem, asem, bsem, lsem, csem, dsem, esem):
    me = Place()
    c = me.c
    half = pl.ds(pl.multiple_of(c * 1024, 1024), 1024)
    ohalf = pl.ds(pl.multiple_of((1 - c) * 1024, 1024), 1024)
    hhalf = pl.ds(pl.multiple_of(c * 256, 256), 256)
    hohalf = pl.ds(pl.multiple_of((1 - c) * 256, 256), 256)
    body = pl.ds(0, ROWS)
    load_z = pltpu.make_async_copy(z_i, zd.at[body], csem.at[0])
    loads = [pltpu.make_async_copy(x2_i.at[:, half], x2h, csem.at[1]),
             pltpu.make_async_copy(n2_i, nv, csem.at[2]),
             pltpu.make_async_copy(x1_i.at[:, half], x1h, csem.at[3]),
             pltpu.make_async_copy(h_i.at[:, hhalf], hh, csem.at[4])]
    load_w3 = pltpu.make_async_copy(w3, gw, csem.at[5])
    load_w2 = pltpu.make_async_copy(w2, gw, csem.at[6])
    load_n1 = pltpu.make_async_copy(n1_i, nv, csem.at[7])
    swap_z = rcopy(z_i, zod, dsem.at[0], esem.at[0], me.pc)
    swaps = [rcopy(x2_i.at[:, ohalf], x2o, dsem.at[1], esem.at[1], me.pc),
             rcopy(x1_i.at[:, ohalf], x1o, dsem.at[2], esem.at[2], me.pc),
             rcopy(h_i.at[:, hohalf], ho, dsem.at[3], esem.at[3], me.pc)]
    swap_du2 = rcopy(zd.at[body], zod, dsem.at[4], esem.at[4], me.pc)
    swap_du1 = rcopy(dz, dzo, dsem.at[5], esem.at[5], me.pc)
    swap_s2 = rcopy(s2, e2, dsem.at[6], esem.at[6], me.pc)
    swap_s1 = rcopy(s1, e1, dsem.at[7], esem.at[7], me.pc)

    def swap_dz(p):
        part_cols = pl.ds(512 * p, 512)
        return rcopy(dz.at[:, part_cols], dzo.at[:, part_cols], dsem.at[8 + p], esem.at[8 + p], me.pc)

    load_z.start()
    me.barrier()
    swap_z.start()
    load_z.wait()
    for cp in swaps + loads:
        cp.start()
    lacc[...] = jnp.zeros_like(lacc)

    def col_sum(j, carry):
        sv[pl.ds(j, 1)] = jnp.sum(zd[0:ROWS, cols(j)].astype(F32), axis=0, keepdims=True)
        return carry
    lax.fori_loop(0, NB, col_sum, 0)
    red0 = SmallReduce(me, sv, sl, sa, sb)
    red2 = SmallReduce(me, s2, l2, a2, b2)
    red1 = SmallReduce(me, s1, l1, a1, b1)
    sc = Scatter(me, part, (r1, r2, r3, r4), ssem, rsem)

    def compute(u):
        p = lax.rem(u, SLOTS)

        @pl.when(u < GRAM_UNITS)
        def _():
            for k in range(2):
                i, j = block_of(2 * u + k)
                part[p, k] = tn(zd[0:ROWS, cols(i)], zd[0:ROWS, cols(j)])

        w, rb, cb = grad_unit(u)
        for w_, la, lb, ra, rb_ in ((0, x2h, x2o, dz, dzo), (1, x1h, x1o, zd, zod), (2, hh, ho, dz, dzo)):
            @pl.when((u >= GRAM_UNITS) & (w == w_))
            def _(w_=w_, la=la, lb=lb, ra=ra, rb_=rb_):
                lc = slice(None) if w_ == 2 else cols(rb)
                rc = pl.ds(pl.multiple_of(cb * 512, 512), 512)
                res = tn(la[:, lc], ra[0:ROWS, rc]) + tn(lb[:, lc], rb_[:, rc])
                part[p, 0] = res[:, 0:BLK]
                part[p, 1] = res[:, BLK:2 * BLK]

    def grad_unit(u):
        v = u - GRAM_UNITS
        w = v // 16
        q = lax.rem(v, 16)
        return w, jnp.where(w == 2, 0, lax.rem(q, 4)), jnp.where(w == 2, q, q // 4)

    def base(u):
        w, rb, cb = grad_unit(u)
        return w * 2048 + c * jnp.where(w == 2, 256, 1024) + rb * 256, cb * 512

    def region(u, k, off, n):
        r0, c0 = base(u)
        return g_o.at[rows_at(r0 + off, n), pl.ds(pl.multiple_of(c0 + k * BLK, BLK), BLK)]

    def keep_copy(u, k):
        return pltpu.make_async_copy(part.at[lax.rem(u, SLOTS), k, rows_at(me.keep[k][4], 16)],
                                     region(u, k, me.keep[k][4], 16), lsem.at[k, lax.rem(u, RING)])

    def spread(u, s, k):
        r = lax.rem(u, RING)
        dst = region(u, k, me.keep[k][s], BLK >> s)
        src = part.at[lax.rem(u, SLOTS), k, rows_at(me.keep[k][4], 16)] if s == 4 else dst
        return rcopy(src, dst, asem.at[s, k, r], bsem.at[s, k, r], me.peers[k][s - 1])

    def cross(u):
        r = lax.rem(u, RING)
        r0, c0 = base(u)
        reg = g_o.at[rows_at(r0, BLK), pl.ds(pl.multiple_of(c0, 512), 512)]
        return rcopy(reg, reg, asem.at[0, 0, r], bsem.at[0, 0, r], me.pc)

    def spread_gram(u, s, k):
        i, j = block_of(2 * u + k)
        r = lax.rem(u, RING)
        buf = gw.at[rows_at(i * BLK + me.keep[k][s], BLK >> s), cols(j)]
        return rcopy(buf, buf, gasem.at[s - 1, k, r], gbsem.at[s - 1, k, r], me.peers[k][s - 1])

    def final(u):
        @pl.when(u >= GRAM_UNITS)
        def _():
            for k in range(2):
                spread(u, 4, k).start()
                keep_copy(u, k).start()

        @pl.when(u < GRAM_UNITS)
        def _():
            for k in range(2):
                i, j = block_of(2 * u + k)
                own = rows_at(me.keep[k][4], 16)
                row0 = rows_at(i * BLK + me.keep[k][4], 16)
                mu_r = mut[row0]
                mu_c = sv[pl.ds(j, 1)]
                mm = ALL_ROWS * jnp.concatenate([mu_r, mu_r], axis=1) * mu_c
                cov = (part[lax.rem(u, SLOTS), k, own] - mm) * (1.0 / (ALL_ROWS - 1))
                row = lax.broadcasted_iota(jnp.int32, (16, BLK), 0) + (i * BLK + me.keep[k][4])
                col = lax.broadcasted_iota(jnp.int32, (16, BLK), 1) + j * BLK
                diag = row == col
                std = jnp.sqrt(jnp.where(diag, cov, 1.0) + STD_EPS)
                hinge = jnp.where(std < 1.0, VAR_WEIGHT / (2.0 * std), 0.0)
                weight = jnp.where(i == j, COV_WEIGHT, 2.0 * COV_WEIGHT)
                term = jnp.where(diag, VAR_WEIGHT * jnp.maximum(1.0 - std, 0.0), weight * cov * cov)
                lacc[...] = lacc[...] + term[0:8] + term[8:16]
                gw[row0, cols(j)] = jnp.where(diag, -hinge, (2.0 * COV_WEIGHT) * cov).astype(BF16)
                spread_gram(u, 4, k).start()

    def dz_block(j):
        acc = nn(zd[...], gw[:, cols(j)])
        mean = acc[ROWS:ROWS + 1] + acc[ROWS + 1:ROWS + 2] + acc[ROWS + 2:ROWS + 3]
        diff = zd[0:ROWS, cols(j)].astype(F32) - zod[:, cols(j)].astype(F32)
        sq = jnp.sum((diff * diff).reshape(ROWS // 8, 8, BLK), axis=0)
        lacc[...] = lacc[...] + (0.5 * INV_WEIGHT / ALL_ROWS) * sq
        dz[:, cols(j)] = ((2.0 * INV_WEIGHT / ALL_ROWS) * diff
                          + (2.0 / (ALL_ROWS - 1)) * (acc[0:ROWS] - mean)).astype(BF16)

    def back_block(j, grad, st, layer):
        dx = nt(grad[0:ROWS, :], gw[cols(j)])
        nrm = nv[:, cols(j)]
        act = gb[pl.ds(2 * NB * layer + j, 1)] * nrm + gb[pl.ds(2 * NB * layer + NB + j, 1)]
        d_act = jnp.where(act > 0.0, dx, 0.0)
        da[:, cols(j)] = d_act
        st[pl.ds(j, 1)] = jnp.sum(d_act, axis=0, keepdims=True)
        st[pl.ds(NB + j, 1)] = jnp.sum(d_act * nrm, axis=0, keepdims=True)

    def back_pre(dst, st, layer):
        def step(j, carry):
            scale = gb[pl.ds(2 * NB * layer + j, 1)] * rs_i[pl.ds(NB * layer + j, 1)]
            m0 = st[pl.ds(j, 1)] * (1.0 / ALL_ROWS)
            m1 = st[pl.ds(NB + j, 1)] * (1.0 / ALL_ROWS)
            dst[0:ROWS, cols(j)] = (scale * (da[:, cols(j)] - m0 - nv[:, cols(j)] * m1)).astype(BF16)
            return carry
        lax.fori_loop(0, NB, step, 0)

    compute(jnp.int32(0))

    def slot(t, carry):
        u, ok = unit_at(t - 9 * LAG)

        @pl.when(ok & (u >= GRAM_UNITS))
        def _(u=u):
            cross(u).wait()

        for s in (1, 2, 3, 4):
            u, ok = unit_at(t - LAG * (9 - s))

            @pl.when(ok & (u >= GRAM_UNITS))
            def _(s=s, u=u):
                for k in range(2):
                    cp = spread(u, s, k)
                    cp.wait_send()
                    cp.wait_recv()
                    if s == 4:
                        keep_copy(u, k).wait()
                    if s > 1:
                        spread(u, s - 1, k).start()
                if s == 1:
                    cross(u).start()

            @pl.when(ok & (u < GRAM_UNITS))
            def _(s=s, u=u):
                for k in range(2):
                    cp = spread_gram(u, s, k)
                    cp.wait_send()
                    cp.wait_recv()
                    if s > 1:
                        spread_gram(u, s - 1, k).start()
                if s == 1:
                    for k in range(2):
                        i, j = block_of(2 * u + k)

                        @pl.when(i != j)
                        def _():
                            gw[rows_at(j * BLK, BLK), cols(i)] = gw[rows_at(i * BLK, BLK), cols(j)].T

        sc.advance(t, final)
        u, ok = unit_at(t)

        @pl.when(ok)
        def _(u=u):
            sc.begin(u)

        for first, red in ((0, red0), (PASS_2 + 4, red2), (PASS_1 + 4, red1)):
            for k in range(4):
                @pl.when(t == first + k + 1)
                def _(red=red, k=k):
                    red.finish(k)

                @pl.when(t == first + k)
                def _(red=red, k=k):
                    red.start(k)

        @pl.when(t == 5)
        def _():
            mean = sv[...] * (1.0 / ALL_ROWS)
            sv[...] = mean
            hi = mean.astype(BF16)
            mid = (mean - hi.astype(F32)).astype(BF16)
            low = (mean - hi.astype(F32) - mid.astype(F32)).astype(BF16)
            for j in range(NB):
                for h in range(2):
                    lanes = slice(128 * h, 128 * h + 128)
                    dst = slice(j * BLK + 128 * h, j * BLK + 128 * h + 128)
                    mut[dst] = jnp.broadcast_to(mean[j:j + 1, lanes], (128, 128)).T
                zd[ROWS:ROWS + 16, j * BLK:(j + 1) * BLK] = jnp.concatenate(
                    [hi[j:j + 1], mid[j:j + 1], low[j:j + 1], jnp.zeros((13, BLK), BF16)], axis=0)

        @pl.when(t == DZ_SLOTS[0] - 1)
        def _():
            swap_z.wait()
            for cp in swaps + loads:
                cp.wait()

        for p, first in enumerate(DZ_SLOTS):
            @pl.when(t == first + 1)
            def _(p=p):
                swap_dz(p).wait()

            @pl.when(t == first)
            def _(p=p):
                def step(j, carry):
                    dz_block(2 * p + j)
                    return carry
                lax.fori_loop(0, 2, step, 0)
                swap_dz(p).start()

        @pl.when(t == DZ_SLOTS[3])
        def _():
            load_w3.start()

        @pl.when(t == PASS_2)
        def _():
            s2[2 * NB:3 * NB] = lacc[...]
            load_w3.wait()

        @pl.when(t == PASS_1)
        def _():
            load_w2.wait()
            load_n1.wait()
            swap_du2.wait()

        @pl.when(t == START_2 + 14)
        def _():
            swap_du1.wait()

        for first, grad, st, layer, dst in ((PASS_2, dz, s2, 1, zd), (PASS_1, zd, s1, 0, dz)):
            @pl.when((t >= first) & (t < first + 4))
            def _(first=first, grad=grad, st=st, layer=layer):
                def step(j, carry):
                    back_block(2 * (t - first) + j, grad, st, layer)
                    return carry
                lax.fori_loop(0, 2, step, 0)

            @pl.when(t == first + 8)
            def _(st=st, layer=layer, dst=dst):
                back_pre(dst, st, layer)

        @pl.when(t == PASS_2 + 4)
        def _():
            load_w2.start()

        @pl.when(t == PASS_2 + 8)
        def _():
            load_n1.start()
            swap_du2.start()
            swap_s2.start()

        @pl.when(t == PASS_1 + 8)
        def _():
            swap_du1.start()
            swap_s1.start()

        u, ok = unit_at(t + 1)

        @pl.when(ok)
        def _(u=u):
            compute(u)
        return carry
    lax.fori_loop(0, END, slot, 0)
    swap_s2.wait()
    swap_s1.wait()
    st2_o[...] = s2[...] + e2[...]
    st1_o[...] = s1[...] + e1[...]


def backward(z, x2, x1, h, n2, n1, w3, w2, gb, rs):
    act = pltpu.VMEM((ROWS, DIM), BF16)
    piece = pltpu.VMEM((ROWS, 1024), BF16)
    feat = pltpu.VMEM((ROWS, 256), BF16)
    wide = pltpu.VMEM((ROWS, DIM), F32)
    dma = pltpu.SemaphoreType.DMA
    return pl.pallas_call(
        back_kernel,
        out_shape=(sds((2 * DIM + FEAT, DIM), F32), sds((3 * NB, BLK), F32), sds((2 * NB, BLK), F32)),
        in_specs=[ANY] * 8 + [INV] * 2,
        out_specs=(ANY, INV, INV),
        scratch_shapes=[pltpu.VMEM((ROWS + 16, DIM), BF16), act, act, act, pltpu.VMEM((DIM, DIM), BF16),
                        piece, piece, piece, piece, feat, feat, wide, wide, pltpu.VMEM((DIM, 128), F32),
                        pltpu.VMEM((NB, BLK), F32)]
        + scatter_scratch(SLOTS) + small_scratch(NB) + small_scratch(3 * NB) + small_scratch(2 * NB)
        + [pltpu.VMEM((3 * NB, BLK), F32), pltpu.VMEM((2 * NB, BLK), F32),
           dma((4, 2, RING)), dma((4, 2, RING)), dma((5, 2, RING)), dma((5, 2, RING)), dma((2, RING)),
           dma((8,)), dma((12,)), dma((12,))],
        compiler_params=pltpu.CompilerParams(collective_id=1, has_side_effects=True, vmem_limit_bytes=VMEM_LIMIT),
        name='backward',
    )(z, x2, x1, h, n2, n1, w3, w2, gb, rs)


def solution(mesh):
    def local_step(h_a, h_b, w_one, w_two, w_three, gain_one, bias_one, gain_two, bias_two):
        gb = jnp.stack([gain_one, bias_one, gain_two, bias_two]).reshape(4 * NB, BLK)
        n1, n2, x1, x2, z, rs, h = forward(h_a, h_b, w_one, w_two, w_three, gb)
        grads, st2, st1 = backward(z, x2, x1, h, n2, n1, w_three, w_two, gb, rs)
        loss = jnp.sum(st2[2 * NB:])
        return (loss, grads[2 * DIM:], grads[DIM:2 * DIM], grads[:DIM],
                st1[NB:2 * NB].reshape(DIM), st1[:NB].reshape(DIM),
                st2[NB:2 * NB].reshape(DIM), st2[:NB].reshape(DIM))

    row_spec = P('data', None)
    return jax.shard_map(local_step, mesh=mesh,
                         in_specs=(row_spec, row_spec, P(), P(), P(), P(), P(), P(), P()),
                         out_specs=(P(), P(), P(), P(), P(), P(), P(), P()),
                         check_vma=False)
```

time: 523 us -> 493 us (0.943)
  Pallas kernels: 490 us -> 460 us
    pallas_call x2 -> x1, Pallas kernels: 430 us -> 399 us  [backward(): pl.pallas_call(back_kernel, out_shape=(sds((2 * DIM + FEAT, DIM), F32), s...]
where the time goes in v2:
time: 493 us; the launch traced here: 492 us
  Pallas kernels  460 us (93%)
  local copies, waits for them, and re-layouts  29.7 us (6%)
    pallas_call x1, Pallas kernels, backward(): pl.pallas_call(back_kernel, out_shape=(sds((2 * DIM + FEAT, DIM), F32), s...  399 us
    pallas_call x1, Pallas kernels, forward(): pl.pallas_call(forward_kernel, out_shape=(sds((ROWS, DIM), F32), sds((ROW...  60.3 us
    slice x1, local copies, waits for them, and re-layouts, local_step(): grads[:DIM]  21.2 us

profile of v2, /device:TPU:0, one launch (start us, length us, event | category | flops | bytes accessed | tf_op | source)
XLA Modules:
  0.0 492.0 jit_solution(2696233677474684982)
XLA Ops:
  0.6 0.8 pad_maximum_fusion
  1.4 0.6 reshape.31.gb
  2.1 60.3 %forward.1 = (f32[1024,2048]{1,0:T(8,128)}, f32[1024,2048]{1,0:T(8,128)}, bf16[1024,2048]{1,0:T(8,128)(2,1)}, bf16[1024,2048]{1,0:T(8,128)(2,1)}, bf16[1024,2048...) custom-call(bf16[512,512]{1,0:T(8,128)(2,1)} %ha.1, bf16[512,512]{1,0:T(8,128)(2,1)} %hb.1, ...), custom_call_target="tpu_custom_call" | custom-call | tf_op jit(solution)/shard_map/forward/pallas_call | solution.py:249
  62.4 399.3 %backward.1 = (f32[4608,2048]{1,0:T(8,128)}, f32[24,256]{1,0:T(8,128)}, f32[16,256]{1,0:T(8,128)}) custom-call(bf16[1024,2048]{1,0:T(8,128)(2,1)} %get-tuple-element.18.z_i, bf16[1024,2048]{1,0:T(8,128)(2,1)} %get-tuple-element.19.x2_i, bf16[1024,2048]{1,0:T(8,128)(2,1)} %get-tuple-element.20.x1_i, bf16[1024,512]{1,0:T(8,128)(2,1)} %get-tuple-element.21.h_i, ...), custom_call_target="tpu_custom_call" | custom-call | tf_op jit(solution)/shard_map/backward/pallas_call | solution.py:605
  461.7 1.3 slice_bitcast_fusion
  463.0 0.6 copy.20
  463.6 0.6 copy.19
  464.2 0.7 slice_bitcast_fusion.2
  464.9 0.6 copy.18
  465.5 0.6 copy.17
  466.1 4.7 slice.25
  470.8 21.2 %fusion = (f32[2048,2048]{1,0:T(8,128)}, f32[2048,2048]{1,0:T(8,128)}) fusion(f32[4608,2048]{1,0:T(8,128)} %get-tuple-element.26), kind=kLoop, calls=%fused_computation.6 | loop fusion | bytes 67108864 | tf_op jit(solution)/shard_map/slice | solution.py:628

commit v3 on v2

--- a/solution.py
+++ b/solution.py
@@ -51,7 +51,9 @@
         py = i + 4 - 8 * y
         p1 = i + 8 - 16 * zl
         p2 = i + 16 - 32 * zh
-        self.ring = (px, py, p1, p2)
+        pd = px + py - i
+        p3 = p1 + p2 - i
+        self.phases = ((px, py, pd), (p1, p2, p3))
         self.bits = ((x, zl, y, zh), (y, zl, x, zh))
         self.peers = ((px, p1, py, p2), (py, p1, px, p2))
         self.keep = []
@@ -69,9 +71,9 @@
 
     def barrier(self):
         sem = pltpu.get_barrier_semaphore()
-        for p in (self.pc,) + self.ring:
+        for p in (self.pc,) + self.phases[0] + self.phases[1]:
             pl.semaphore_signal(sem, inc=1, device_id=(p,), device_id_type=MESH)
-        pl.semaphore_wait(sem, 5)
+        pl.semaphore_wait(sem, 7)
 
 
 def rcopy(src, dst, ssem, rsem, dev):
@@ -144,59 +146,108 @@
     def __init__(self, place, val, land, ssem, rsem):
         self.pl, self.val, self.land, self.ssem, self.rsem = place, val, land, ssem, rsem
 
-    def copy(self, k):
-        return rcopy(self.val, self.land.at[k], self.ssem.at[k], self.rsem.at[k], self.pl.ring[k])
-
-    def start(self, k):
-        self.copy(k).start()
-
-    def finish(self, k):
-        self.copy(k).wait()
-        self.val[...] = self.val[...] + self.land[k]
+    def copies(self, ph):
+        return [rcopy(self.val, self.land.at[ph, k], self.ssem.at[ph, k], self.rsem.at[ph, k], p)
+                for k, p in enumerate(self.pl.phases[ph])]
+
+    def start(self, ph):
+        for cp in self.copies(ph):
+            cp.start()
+
+    def finish(self, ph):
+        for cp in self.copies(ph):
+            cp.wait()
+        self.val[...] = (self.val[...] + self.land[ph, 0]) + (self.land[ph, 1] + self.land[ph, 2])
 
     def run(self):
-        for k in range(4):
-            self.start(k)
-            self.finish(k)
+        for ph in range(2):
+            self.start(ph)
+            self.finish(ph)
 
 
 def small_scratch(n):
-    return [pltpu.VMEM((n, BLK), F32), pltpu.VMEM((4, n, BLK), F32),
-            pltpu.SemaphoreType.DMA((4,)), pltpu.SemaphoreType.DMA((4,))]
-
-
-def forward_kernel(ha, hb, w1, w2, w3, gb, n1_o, n2_o, x1_o, x2_o, z_o, r_o, h_o,
-                   h, w1v, w2v, w3v, u1, u2, x1, x2, z, s1, l1, a1, b1, s2, l2, a2, b2, hsem, wsem, osem):
+    return [pltpu.VMEM((n, BLK), F32), pltpu.VMEM((2, 3, n, BLK), F32),
+            pltpu.SemaphoreType.DMA((2, 3)), pltpu.SemaphoreType.DMA((2, 3))]
+
+
+GRAM_UNITS = 18
+UNITS = 54
+SLOTS = 5 * LAG + 2
+START_3 = 26
+START_2 = 42
+END = START_2 + 20 + 9 * LAG
+DZ_SLOTS = (23, 28, 32, 34)
+PASS_2 = 35
+PASS_1 = 43
+
+
+def block_of(q):
+    i = jnp.int32(0)
+    for first in (8, 15, 21, 26, 30, 33, 35):
+        i = i + jnp.where(q >= first, 1, 0)
+    return i, i + q - (17 * i - i * i) // 2
+
+
+def unit_at(t):
+    u = jnp.where(t < START_3, t, jnp.where(t < START_2, t - (START_3 - 18), t - (START_2 - 34)))
+    ok = ((t >= 0) & (t < 18)) | ((t >= START_3) & (t < START_3 + 16)) | ((t >= START_2) & (t < START_2 + 20))
+    return jnp.where(ok, u, 0), ok
+
+
+def step_kernel(ha, hb, w1, w2, w3, gb, g_o, n1_o, st2_o, st1_o,
+                zd, zod, dz, dzo, gw, x2h, x2o, x1h, x1o, hv, ho, nv, da, mut, lacc, rs,
+                part, r1, r2, r3, r4, ssem, rsem, sv, sl, sa, sb, f1, fl1, fa1, fb1, f2, fl2, fa2, fb2,
+                s2, l2, a2, b2, s1, l1, a1, b1, e2, e1,
+                gasem, gbsem, asem, bsem, lsem, csem, dsem, esem):
     me = Place()
-    loads = [pltpu.make_async_copy(w1, w1v, wsem.at[0]), pltpu.make_async_copy(w2, w2v, wsem.at[1]),
-             pltpu.make_async_copy(w3, w3v, wsem.at[2])]
-    mine = pl.ds(pl.multiple_of(me.c * HALF, HALF), HALF)
-    for c, own in ((0, ha), (1, hb)):
-        @pl.when(me.c == c)
+    c = me.c
+    half = pl.ds(pl.multiple_of(c * 1024, 1024), 1024)
+    ohalf = pl.ds(pl.multiple_of((1 - c) * 1024, 1024), 1024)
+    hhalf = pl.ds(pl.multiple_of(c * 256, 256), 256)
+    hohalf = pl.ds(pl.multiple_of((1 - c) * 256, 256), 256)
+    mine = pl.ds(pl.multiple_of(c * HALF, HALF), HALF)
+    body = pl.ds(0, ROWS)
+    w1v = zod.at[pl.ds(0, FEAT)]
+    load_w1 = pltpu.make_async_copy(w1, w1v, csem.at[0])
+    load_w2a = pltpu.make_async_copy(w2, gw, csem.at[1])
+    load_w3a = pltpu.make_async_copy(w3, gw, csem.at[2])
+    load_w3 = pltpu.make_async_copy(w3, gw, csem.at[5])
+    load_w2 = pltpu.make_async_copy(w2, gw, csem.at[6])
+    load_n1 = pltpu.make_async_copy(n1_o, nv, csem.at[7])
+    save_n1 = pltpu.make_async_copy(da, n1_o, csem.at[8])
+    keep_x1 = pltpu.make_async_copy(dzo.at[:, half], x1h, csem.at[3])
+    keep_x2 = pltpu.make_async_copy(dz.at[:, half], x2h, csem.at[4])
+    swap_z = rcopy(zd.at[body], zod, dsem.at[0], esem.at[0], me.pc)
+    swap_x2 = rcopy(dz.at[:, ohalf], x2o, dsem.at[1], esem.at[1], me.pc)
+    swap_x1 = rcopy(dzo.at[:, ohalf], x1o, dsem.at[2], esem.at[2], me.pc)
+    swap_h = rcopy(hv.at[:, hohalf], ho, dsem.at[3], esem.at[3], me.pc)
+    swap_du2 = rcopy(zd.at[body], zod, dsem.at[4], esem.at[4], me.pc)
+    swap_du1 = rcopy(dz, dzo, dsem.at[5], esem.at[5], me.pc)
+    swap_s2 = rcopy(s2, e2, dsem.at[6], esem.at[6], me.pc)
+    swap_s1 = rcopy(s1, e1, dsem.at[7], esem.at[7], me.pc)
+
+    def load_h(src):
+        return pltpu.make_async_copy(src, hv.at[mine], csem.at[9])
+
+    def give_h(src):
+        return rcopy(src, hv.at[mine], dsem.at[12], esem.at[12], me.pc)
+
+    def swap_dz(p):
+        part_cols = pl.ds(512 * p, 512)
+        return rcopy(dz.at[:, part_cols], dzo.at[:, part_cols], dsem.at[8 + p], esem.at[8 + p], me.pc)
+
+    for k, own in ((0, ha), (1, hb)):
+        @pl.when(c == k)
         def _(own=own):
-            pltpu.make_async_copy(own, h.at[mine], hsem.at[0]).start()
-    loads[0].start()
+            load_h(own).start()
+    load_w1.start()
+    load_w2a.start()
     me.barrier()
-
-    def exchange(src):
-        return rcopy(src, h.at[mine], hsem.at[1], hsem.at[2], me.pc)
-    for c, other in ((0, hb), (1, ha)):
-        @pl.when(me.c == c)
+    for k, other in ((0, hb), (1, ha)):
+        @pl.when(c == k)
         def _(other=other):
-            exchange(other).start()
-    loads[1].start()
-    loads[2].start()
-    loads[0].wait()
-    pltpu.make_async_copy(ha, h.at[mine], hsem.at[0]).wait()
-    exchange(ha).wait()
-    out = []
-
-    def save(src, dst):
-        cp = pltpu.make_async_copy(src, dst, osem.at[len(out)])
-        cp.start()
-        out.append(cp)
-
-    save(h, h_o)
+            give_h(other).start()
+    lacc[...] = jnp.zeros_like(lacc)
 
     def matmul(src, w, dst, st):
         def step(j, carry):
@@ -210,8 +261,10 @@
     def norm(u, x, st, layer):
         mean = st[0:NB] * (1.0 / ALL_ROWS)
         var = st[NB:2 * NB] * (1.0 / ALL_ROWS) - mean * mean
+        inv = lax.rsqrt(var + BN_EPS)
         st[0:NB] = mean
-        st[NB:2 * NB] = lax.rsqrt(var + BN_EPS)
+        st[NB:2 * NB] = inv
+        rs[NB * layer:NB * layer + NB] = inv
 
         def step(j, carry):
             nrm = (u[:, cols(j)] - st[pl.ds(j, 1)]) * st[pl.ds(NB + j, 1)]
@@ -221,115 +274,38 @@
             return carry
         lax.fori_loop(0, NB, step, 0)
 
-    matmul(h, w1v, u1, s1)
-    SmallReduce(me, s1, l1, a1, b1).run()
-    norm(u1, x1, s1, 0)
-    save(u1, n1_o)
-    save(x1, x1_o)
-    loads[1].wait()
-    matmul(x1, w2v, u2, s2)
-    SmallReduce(me, s2, l2, a2, b2).run()
-    norm(u2, x2, s2, 1)
-    save(u2, n2_o)
-    save(x2, x2_o)
-    r_o[0:NB] = s1[NB:2 * NB]
-    r_o[NB:2 * NB] = s2[NB:2 * NB]
-    loads[2].wait()
-
-    def step(j, carry):
-        z[:, cols(j)] = nn(x2[...], w3v[:, cols(j)]).astype(BF16)
-        return carry
-    lax.fori_loop(0, NB, step, 0)
-    save(z, z_o)
-    for cp in out:
-        cp.wait()
-
-
-def forward(ha, hb, w1, w2, w3, gb):
-    return pl.pallas_call(
-        forward_kernel,
-        out_shape=(sds((ROWS, DIM), F32), sds((ROWS, DIM), F32), sds((ROWS, DIM), BF16), sds((ROWS, DIM), BF16),
-                   sds((ROWS, DIM), BF16), sds((2 * NB, BLK), F32), sds((ROWS, FEAT), BF16)),
-        in_specs=[ANY] * 5 + [INV],
-        out_specs=(ANY,) * 5 + (INV, ANY),
-        scratch_shapes=[pltpu.VMEM((ROWS, FEAT), BF16), pltpu.VMEM((FEAT, DIM), BF16), pltpu.VMEM((DIM, DIM), BF16),
-                        pltpu.VMEM((DIM, DIM), BF16), pltpu.VMEM((ROWS, DIM), F32), pltpu.VMEM((ROWS, DIM), F32),
-                        pltpu.VMEM((ROWS, DIM), BF16), pltpu.VMEM((ROWS, DIM), BF16), pltpu.VMEM((ROWS, DIM), BF16)]
-        + small_scratch(2 * NB) + small_scratch(2 * NB)
-        + [pltpu.SemaphoreType.DMA((3,)), pltpu.SemaphoreType.DMA((3,)), pltpu.SemaphoreType.DMA((6,))],
-        compiler_params=pltpu.CompilerParams(collective_id=0, has_side_effects=True, vmem_limit_bytes=VMEM_LIMIT),
-        name='forward',
-    )(ha, hb, w1, w2, w3, gb)
-
-
-GRAM_UNITS = 18
-UNITS = 54
-SLOTS = 5 * LAG + 2
-START_3 = 26
-START_2 = 46
-END = START_2 + 20 + 9 * LAG
-DZ_SLOTS = (23, 28, 32, 34)
-PASS_2 = 35
-PASS_1 = 45
-
-
-def block_of(q):
-    i = jnp.int32(0)
-    for first in (8, 15, 21, 26, 30, 33, 35):
-        i = i + jnp.where(q >= first, 1, 0)
-    return i, i + q - (17 * i - i * i) // 2
-
-
-def unit_at(t):
-    u = jnp.where(t < START_3, t, jnp.where(t < START_2, t - (START_3 - 18), t - (START_2 - 34)))
-    ok = ((t >= 0) & (t < 18)) | ((t >= START_3) & (t < START_3 + 16)) | ((t >= START_2) & (t < START_2 + 20))
-    return jnp.where(ok, u, 0), ok
-
-
-def back_kernel(z_i, x2_i, x1_i, h_i, n2_i, n1_i, w3, w2, gb, rs_i, g_o, st2_o, st1_o,
-                zd, zod, dz, dzo, gw, x2h, x2o, x1h, x1o, hh, ho, nv, da, mut, lacc,
-                part, r1, r2, r3, r4, ssem, rsem, sv, sl, sa, sb, s2, l2, a2, b2, s1, l1, a1, b1, e2, e1,
-                gasem, gbsem, asem, bsem, lsem, csem, dsem, esem):
-    me = Place()
-    c = me.c
-    half = pl.ds(pl.multiple_of(c * 1024, 1024), 1024)
-    ohalf = pl.ds(pl.multiple_of((1 - c) * 1024, 1024), 1024)
-    hhalf = pl.ds(pl.multiple_of(c * 256, 256), 256)
-    hohalf = pl.ds(pl.multiple_of((1 - c) * 256, 256), 256)
-    body = pl.ds(0, ROWS)
-    load_z = pltpu.make_async_copy(z_i, zd.at[body], csem.at[0])
-    loads = [pltpu.make_async_copy(x2_i.at[:, half], x2h, csem.at[1]),
-             pltpu.make_async_copy(n2_i, nv, csem.at[2]),
-             pltpu.make_async_copy(x1_i.at[:, half], x1h, csem.at[3]),
-             pltpu.make_async_copy(h_i.at[:, hhalf], hh, csem.at[4])]
-    load_w3 = pltpu.make_async_copy(w3, gw, csem.at[5])
-    load_w2 = pltpu.make_async_copy(w2, gw, csem.at[6])
-    load_n1 = pltpu.make_async_copy(n1_i, nv, csem.at[7])
-    swap_z = rcopy(z_i, zod, dsem.at[0], esem.at[0], me.pc)
-    swaps = [rcopy(x2_i.at[:, ohalf], x2o, dsem.at[1], esem.at[1], me.pc),
-             rcopy(x1_i.at[:, ohalf], x1o, dsem.at[2], esem.at[2], me.pc),
-             rcopy(h_i.at[:, hohalf], ho, dsem.at[3], esem.at[3], me.pc)]
-    swap_du2 = rcopy(zd.at[body], zod, dsem.at[4], esem.at[4], me.pc)
-    swap_du1 = rcopy(dz, dzo, dsem.at[5], esem.at[5], me.pc)
-    swap_s2 = rcopy(s2, e2, dsem.at[6], esem.at[6], me.pc)
-    swap_s1 = rcopy(s1, e1, dsem.at[7], esem.at[7], me.pc)
-
-    def swap_dz(p):
-        part_cols = pl.ds(512 * p, 512)
-        return rcopy(dz.at[:, part_cols], dzo.at[:, part_cols], dsem.at[8 + p], esem.at[8 + p], me.pc)
-
-    load_z.start()
-    me.barrier()
-    swap_z.start()
-    load_z.wait()
-    for cp in swaps + loads:
-        cp.start()
-    lacc[...] = jnp.zeros_like(lacc)
-
-    def col_sum(j, carry):
-        sv[pl.ds(j, 1)] = jnp.sum(zd[0:ROWS, cols(j)].astype(F32), axis=0, keepdims=True)
-        return carry
-    lax.fori_loop(0, NB, col_sum, 0)
+    load_w1.wait()
+    load_h(ha).wait()
+    give_h(ha).wait()
+    swap_h.start()
+    matmul(hv, w1v, da, f1)
+    SmallReduce(me, f1, fl1, fa1, fb1).run()
+    norm(da, dzo, f1, 0)
+    save_n1.start()
+    swap_x1.start()
+    keep_x1.start()
+    load_w2a.wait()
+    matmul(dzo, gw, nv, f2)
+    load_w3a.start()
+    SmallReduce(me, f2, fl2, fa2, fb2).run()
+    norm(nv, dz, f2, 1)
+    swap_x1.wait()
+    swap_x2.start()
+    keep_x2.start()
+    load_w3a.wait()
+
+    def z_block(j):
+        res = nn(dz[...], gw[:, cols(j)]).astype(BF16)
+        zd[0:ROWS, cols(j)] = res
+        sv[pl.ds(j, 1)] = jnp.sum(res.astype(F32), axis=0, keepdims=True)
+
+    def z_blocks(first):
+        def step(j, carry):
+            z_block(first + j)
+            return carry
+        lax.fori_loop(0, 2, step, 0)
+
+    z_blocks(0)
     red0 = SmallReduce(me, sv, sl, sa, sb)
     red2 = SmallReduce(me, s2, l2, a2, b2)
     red1 = SmallReduce(me, s1, l1, a1, b1)
@@ -345,12 +321,12 @@
                 part[p, k] = tn(zd[0:ROWS, cols(i)], zd[0:ROWS, cols(j)])
 
         w, rb, cb = grad_unit(u)
-        for w_, la, lb, ra, rb_ in ((0, x2h, x2o, dz, dzo), (1, x1h, x1o, zd, zod), (2, hh, ho, dz, dzo)):
+        for w_, la, lb, ra, rb_ in ((0, x2h, x2o, dz, dzo), (1, x1h, x1o, zd, zod), (2, hv, ho, dz, dzo)):
             @pl.when((u >= GRAM_UNITS) & (w == w_))
             def _(w_=w_, la=la, lb=lb, ra=ra, rb_=rb_):
-                lc = slice(None) if w_ == 2 else cols(rb)
+                lc, oc = (hhalf, slice(None)) if w_ == 2 else (cols(rb), cols(rb))
                 rc = pl.ds(pl.multiple_of(cb * 512, 512), 512)
-                res = tn(la[:, lc], ra[0:ROWS, rc]) + tn(lb[:, lc], rb_[:, rc])
+                res = tn(la[:, lc], ra[0:ROWS, rc]) + tn(lb[:, oc], rb_[:, rc])
                 part[p, 0] = res[:, 0:BLK]
                 part[p, 1] = res[:, BLK:2 * BLK]
 
@@ -438,7 +414,7 @@
 
     def back_pre(dst, st, layer):
         def step(j, carry):
-            scale = gb[pl.ds(2 * NB * layer + j, 1)] * rs_i[pl.ds(NB * layer + j, 1)]
+            scale = gb[pl.ds(2 * NB * layer + j, 1)] * rs[pl.ds(NB * layer + j, 1)]
             m0 = st[pl.ds(j, 1)] * (1.0 / ALL_ROWS)
             m1 = st[pl.ds(NB + j, 1)] * (1.0 / ALL_ROWS)
             dst[0:ROWS, cols(j)] = (scale * (da[:, cols(j)] - m0 - nv[:, cols(j)] * m1)).astype(BF16)
@@ -493,15 +469,15 @@
         def _(u=u):
             sc.begin(u)
 
-        for first, red in ((0, red0), (PASS_2 + 4, red2), (PASS_1 + 4, red1)):
-            for k in range(4):
-                @pl.when(t == first + k + 1)
-                def _(red=red, k=k):
-                    red.finish(k)
-
-                @pl.when(t == first + k)
-                def _(red=red, k=k):
-                    red.start(k)
+        for first, red in ((3, red0), (PASS_2 + 3, red2), (PASS_1 + 3, red1)):
+            for ph in range(2):
+                @pl.when(t == first + ph + 1)
+                def _(red=red, ph=ph):
+                    red.finish(ph)
+
+                @pl.when(t == first + ph)
+                def _(red=red, ph=ph):
+                    red.start(ph)
 
         @pl.when(t == 5)
         def _():
@@ -518,11 +494,22 @@
                 zd[ROWS:ROWS + 16, j * BLK:(j + 1) * BLK] = jnp.concatenate(
                     [hi[j:j + 1], mid[j:j + 1], low[j:j + 1], jnp.zeros((13, BLK), BF16)], axis=0)
 
+        @pl.when(t < 3)
+        def _():
+            z_blocks(2 * t + 2)
+
+        @pl.when(t == 3)
+        def _():
+            keep_x1.wait()
+            keep_x2.wait()
+            swap_x2.wait()
+            swap_h.wait()
+            save_n1.wait()
+            swap_z.start()
+
         @pl.when(t == DZ_SLOTS[0] - 1)
         def _():
             swap_z.wait()
-            for cp in swaps + loads:
-                cp.wait()
 
         for p, first in enumerate(DZ_SLOTS):
             @pl.when(t == first + 1)
@@ -550,6 +537,9 @@
         def _():
             load_w2.wait()
             load_n1.wait()
+
+        @pl.when(t == START_2 - 1)
+        def _():
             swap_du2.wait()
 
         @pl.when(t == START_2 + 14)
@@ -557,28 +547,29 @@
             swap_du1.wait()
 
         for first, grad, st, layer, dst in ((PASS_2, dz, s2, 1, zd), (PASS_1, zd, s1, 0, dz)):
-            @pl.when((t >= first) & (t < first + 4))
+            @pl.when((t >= first) & (t < first + 3))
             def _(first=first, grad=grad, st=st, layer=layer):
                 def step(j, carry):
-                    back_block(2 * (t - first) + j, grad, st, layer)
+                    back_block(j, grad, st, layer)
                     return carry
-                lax.fori_loop(0, 2, step, 0)
-
-            @pl.when(t == first + 8)
+                lo = 3 * (t - first)
+                lax.fori_loop(lo, jnp.minimum(lo + 3, NB), step, 0)
+
+            @pl.when(t == first + 5)
             def _(st=st, layer=layer, dst=dst):
                 back_pre(dst, st, layer)
 
-        @pl.when(t == PASS_2 + 4)
+        @pl.when(t == PASS_2 + 3)
         def _():
             load_w2.start()
 
-        @pl.when(t == PASS_2 + 8)
+        @pl.when(t == PASS_2 + 5)
         def _():
             load_n1.start()
             swap_du2.start()
             swap_s2.start()
 
-        @pl.when(t == PASS_1 + 8)
+        @pl.when(t == PASS_1 + 5)
         def _():
             swap_du1.start()
             swap_s1.start()
@@ -596,34 +587,35 @@
     st1_o[...] = s1[...] + e1[...]
 
 
-def backward(z, x2, x1, h, n2, n1, w3, w2, gb, rs):
+def train_step(ha, hb, w1, w2, w3, gb):
     act = pltpu.VMEM((ROWS, DIM), BF16)
     piece = pltpu.VMEM((ROWS, 1024), BF16)
-    feat = pltpu.VMEM((ROWS, 256), BF16)
     wide = pltpu.VMEM((ROWS, DIM), F32)
     dma = pltpu.SemaphoreType.DMA
     return pl.pallas_call(
-        back_kernel,
-        out_shape=(sds((2 * DIM + FEAT, DIM), F32), sds((3 * NB, BLK), F32), sds((2 * NB, BLK), F32)),
-        in_specs=[ANY] * 8 + [INV] * 2,
-        out_specs=(ANY, INV, INV),
+        step_kernel,
+        out_shape=(sds((2 * DIM + FEAT, DIM), F32), sds((ROWS, DIM), F32), sds((3 * NB, BLK), F32),
+                   sds((2 * NB, BLK), F32)),
+        in_specs=[ANY] * 5 + [INV],
+        out_specs=(ANY, ANY, INV, INV),
         scratch_shapes=[pltpu.VMEM((ROWS + 16, DIM), BF16), act, act, act, pltpu.VMEM((DIM, DIM), BF16),
-                        piece, piece, piece, piece, feat, feat, wide, wide, pltpu.VMEM((DIM, 128), F32),
-                        pltpu.VMEM((NB, BLK), F32)]
-        + scatter_scratch(SLOTS) + small_scratch(NB) + small_scratch(3 * NB) + small_scratch(2 * NB)
+                        piece, piece, piece, piece, pltpu.VMEM((ROWS, FEAT), BF16), pltpu.VMEM((ROWS, 256), BF16),
+                        wide, wide, pltpu.VMEM((DIM, 128), F32), pltpu.VMEM((NB, BLK), F32),
+                        pltpu.VMEM((2 * NB, BLK), F32)]
+        + scatter_scratch(SLOTS) + small_scratch(NB) + small_scratch(2 * NB) + small_scratch(2 * NB)
+        + small_scratch(3 * NB) + small_scratch(2 * NB)
         + [pltpu.VMEM((3 * NB, BLK), F32), pltpu.VMEM((2 * NB, BLK), F32),
            dma((4, 2, RING)), dma((4, 2, RING)), dma((5, 2, RING)), dma((5, 2, RING)), dma((2, RING)),
-           dma((8,)), dma((12,)), dma((12,))],
-        compiler_params=pltpu.CompilerParams(collective_id=1, has_side_effects=True, vmem_limit_bytes=VMEM_LIMIT),
-        name='backward',
-    )(z, x2, x1, h, n2, n1, w3, w2, gb, rs)
+           dma((10,)), dma((13,)), dma((13,))],
+        compiler_params=pltpu.CompilerParams(collective_id=0, has_side_effects=True, vmem_limit_bytes=VMEM_LIMIT),
+        name='train_step',
+    )(ha, hb, w1, w2, w3, gb)
 
 
 def solution(mesh):
     def local_step(h_a, h_b, w_one, w_two, w_three, gain_one, bias_one, gain_two, bias_two):
         gb = jnp.stack([gain_one, bias_one, gain_two, bias_two]).reshape(4 * NB, BLK)
-        n1, n2, x1, x2, z, rs, h = forward(h_a, h_b, w_one, w_two, w_three, gb)
-        grads, st2, st1 = backward(z, x2, x1, h, n2, n1, w_three, w_two, gb, rs)
+        grads, _, st2, st1 = train_step(h_a, h_b, w_one, w_two, w_three, gb)
         loss = jnp.sum(st2[2 * NB:])
         return (loss, grads[2 * DIM:], grads[DIM:2 * DIM], grads[:DIM],
                 st1[NB:2 * NB].reshape(DIM), st1[:NB].reshape(DIM),

time: 493 us -> 473 us (0.959)
  Pallas kernels: 460 us -> 440 us
    pallas_call x2 -> x1, Pallas kernels: 460 us -> 440 us  [train_step(): pl.pallas_call(step_kernel, out_shape=(sds((2 * DIM + FEAT, DIM), F32), s...]
where the time goes in v3:
time: 473 us
  Pallas kernels  440 us (93%)
  local copies, waits for them, and re-layouts  29.7 us (6%)
    pallas_call x1, Pallas kernels, train_step(): pl.pallas_call(step_kernel, out_shape=(sds((2 * DIM + FEAT, DIM), F32), s...  440 us
    slice x1, local copies, waits for them, and re-layouts, local_step(): grads[:DIM]  21.2 us

profile of v3, /device:TPU:0, one launch (start us, length us, event | category | flops | bytes accessed | tf_op | source)
XLA Modules:
  0.0 472.7 jit_solution(7755158809022170125)
XLA Ops:
  0.6 0.8 pad_maximum_fusion
  1.4 0.6 reshape.31.gb
  2.1 440.3 %train_step.1 = (f32[4608,2048]{1,0:T(8,128)}, f32[1024,2048]{1,0:T(8,128)}, f32[24,256]{1,0:T(8,128)}, f32[16,256]{1,0:T(8,128)}) custom-call(bf16[512,512]{1,0:T(8,128)(2,1)} %ha.1, bf16[512,512]{1,0:T(8,128)(2,1)} %hb.1, bf16[512,2048]{1,0:T(8,128)(2,1)} %w1.1, bf16[2048,2048]{1,0:T(8,128)(2,1)} %w2.1, bf16[2048,2048]{1,0:T(8,128)(2,1)} %w3.1, ...), custom_call_target="tpu_custom_call" | custom-call | tf_op jit(solution)/shard_map/train_step/pallas_call | solution.py:595
  442.4 1.3 slice_bitcast_fusion
  443.7 0.6 copy.20
  444.3 0.6 copy.19
  444.9 0.7 slice_bitcast_fusion.2
  445.6 0.6 copy.18
  446.2 0.6 copy.17
  446.8 4.7 slice.25
  451.5 21.2 %fusion = (f32[2048,2048]{1,0:T(8,128)}, f32[2048,2048]{1,0:T(8,128)}) fusion(f32[4608,2048]{1,0:T(8,128)} %get-tuple-element.12), kind=kLoop, calls=%fused_computation.6 | loop fusion | bytes 67108864 | tf_op jit(solution)/shard_map/slice | solution.py:620

commit v4 on v3

--- a/solution.py
+++ b/solution.py
@@ -97,6 +97,14 @@
     return lax.dot_general(a, b, (((0,), (0,)), ((), ())), preferred_element_type=F32)
 
 
+def lanes_at(off):
+    return pl.ds(pl.multiple_of(off, 128), 128)
+
+
+def cols_at(off):
+    return pl.ds(pl.multiple_of(off, BLK), BLK)
+
+
 def cols(j):
     return pl.ds(pl.multiple_of(j * BLK, BLK), BLK)
 
@@ -172,13 +180,13 @@
 
 GRAM_UNITS = 18
 UNITS = 54
-SLOTS = 5 * LAG + 2
-START_3 = 26
-START_2 = 42
-END = START_2 + 20 + 9 * LAG
-DZ_SLOTS = (23, 28, 32, 34)
+SLOTS = 4 * LAG + 1
+START_3 = 24
+START_2 = 41
+END = START_2 + 21 + 9 * LAG
+DZ_SLOTS = (20, 23, 26, 28, 30, 32, 33, 34)
 PASS_2 = 35
-PASS_1 = 43
+PASS_1 = 42
 
 
 def block_of(q):
@@ -194,13 +202,16 @@
     return jnp.where(ok, u, 0), ok
 
 
-def step_kernel(ha, hb, w1, w2, w3, gb, g_o, n1_o, st2_o, st1_o,
-                zd, zod, dz, dzo, gw, x2h, x2o, x1h, x1o, hv, ho, nv, da, mut, lacc, rs,
+def step_kernel(ha, hb, w1, w2, w3, g1, b1, g2, b2, g3_o, g2_o, g1_o, n1_o, st_o,
+                zd, zod, dz, dzo, gw, x2h, x2o, x1h, x1o, hh, ho, g2v, g1v, lacc, rs, stage,
                 part, r1, r2, r3, r4, ssem, rsem, sv, sl, sa, sb, f1, fl1, fa1, fb1, f2, fl2, fa2, fb2,
-                s2, l2, a2, b2, s1, l1, a1, b1, e2, e1,
-                gasem, gbsem, asem, bsem, lsem, csem, dsem, esem):
+                s2, l2, sa2, sb2, s1, l1, sa1, sb1, e2, e1,
+                gasem, gbsem, asem, bsem, lsem, psem, csem, dsem, esem):
     me = Place()
     c = me.c
+    nv, da = g2v.at[pl.ds(0, ROWS)], g2v.at[pl.ds(ROWS, ROWS)]
+    hv = x2o.at[:, pl.ds(0, FEAT)]
+    gains, biases = (g1, g2), (b1, b2)
     half = pl.ds(pl.multiple_of(c * 1024, 1024), 1024)
     ohalf = pl.ds(pl.multiple_of((1 - c) * 1024, 1024), 1024)
     hhalf = pl.ds(pl.multiple_of(c * 256, 256), 256)
@@ -211,11 +222,12 @@
     load_w1 = pltpu.make_async_copy(w1, w1v, csem.at[0])
     load_w2a = pltpu.make_async_copy(w2, gw, csem.at[1])
     load_w3a = pltpu.make_async_copy(w3, gw, csem.at[2])
-    load_w3 = pltpu.make_async_copy(w3, gw, csem.at[5])
+    load_w3 = pltpu.make_async_copy(w3, gw, csem.at[2])
     load_w2 = pltpu.make_async_copy(w2, gw, csem.at[6])
     load_n1 = pltpu.make_async_copy(n1_o, nv, csem.at[7])
     save_n1 = pltpu.make_async_copy(da, n1_o, csem.at[8])
     keep_x1 = pltpu.make_async_copy(dzo.at[:, half], x1h, csem.at[3])
+    keep_h = pltpu.make_async_copy(hv.at[:, hhalf], hh, csem.at[5])
     keep_x2 = pltpu.make_async_copy(dz.at[:, half], x2h, csem.at[4])
     swap_z = rcopy(zd.at[body], zod, dsem.at[0], esem.at[0], me.pc)
     swap_x2 = rcopy(dz.at[:, ohalf], x2o, dsem.at[1], esem.at[1], me.pc)
@@ -230,11 +242,10 @@
         return pltpu.make_async_copy(src, hv.at[mine], csem.at[9])
 
     def give_h(src):
-        return rcopy(src, hv.at[mine], dsem.at[12], esem.at[12], me.pc)
-
-    def swap_dz(p):
-        part_cols = pl.ds(512 * p, 512)
-        return rcopy(dz.at[:, part_cols], dzo.at[:, part_cols], dsem.at[8 + p], esem.at[8 + p], me.pc)
+        return rcopy(src, hv.at[mine], dsem.at[16], esem.at[16], me.pc)
+
+    def swap_dz(j):
+        return rcopy(dz.at[:, cols(j)], dzo.at[:, cols(j)], dsem.at[8 + j], esem.at[8 + j], me.pc)
 
     for k, own in ((0, ha), (1, hb)):
         @pl.when(c == k)
@@ -268,7 +279,7 @@
 
         def step(j, carry):
             nrm = (u[:, cols(j)] - st[pl.ds(j, 1)]) * st[pl.ds(NB + j, 1)]
-            act = gb[pl.ds(2 * NB * layer + j, 1)] * nrm + gb[pl.ds(2 * NB * layer + NB + j, 1)]
+            act = gains[layer][:, cols(j)] * nrm + biases[layer][:, cols(j)]
             u[:, cols(j)] = nrm
             x[:, cols(j)] = jnp.maximum(act, 0.0).astype(BF16)
             return carry
@@ -278,10 +289,13 @@
     load_h(ha).wait()
     give_h(ha).wait()
     swap_h.start()
+    keep_h.start()
     matmul(hv, w1v, da, f1)
     SmallReduce(me, f1, fl1, fa1, fb1).run()
     norm(da, dzo, f1, 0)
     save_n1.start()
+    keep_h.wait()
+    swap_h.wait()
     swap_x1.start()
     keep_x1.start()
     load_w2a.wait()
@@ -307,8 +321,8 @@
 
     z_blocks(0)
     red0 = SmallReduce(me, sv, sl, sa, sb)
-    red2 = SmallReduce(me, s2, l2, a2, b2)
-    red1 = SmallReduce(me, s1, l1, a1, b1)
+    red2 = SmallReduce(me, s2, l2, sa2, sb2)
+    red1 = SmallReduce(me, s1, l1, sa1, sb1)
     sc = Scatter(me, part, (r1, r2, r3, r4), ssem, rsem)
 
     def compute(u):
@@ -320,45 +334,65 @@
                 i, j = block_of(2 * u + k)
                 part[p, k] = tn(zd[0:ROWS, cols(i)], zd[0:ROWS, cols(j)])
 
-        w, rb, cb = grad_unit(u)
-        for w_, la, lb, ra, rb_ in ((0, x2h, x2o, dz, dzo), (1, x1h, x1o, zd, zod), (2, hv, ho, dz, dzo)):
+        w, q = grad_unit(u)
+        for w_, la, lb, ra, rb in ((0, x2h, x2o, dz, dzo), (1, x1h, x1o, zd, zod)):
             @pl.when((u >= GRAM_UNITS) & (w == w_))
-            def _(w_=w_, la=la, lb=lb, ra=ra, rb_=rb_):
-                lc, oc = (hhalf, slice(None)) if w_ == 2 else (cols(rb), cols(rb))
-                rc = pl.ds(pl.multiple_of(cb * 512, 512), 512)
-                res = tn(la[:, lc], ra[0:ROWS, rc]) + tn(lb[:, oc], rb_[:, rc])
-                part[p, 0] = res[:, 0:BLK]
-                part[p, 1] = res[:, BLK:2 * BLK]
+            def _(la=la, lb=lb, ra=ra, rb=rb):
+                lc = pl.ds(pl.multiple_of(lax.rem(q, 2) * 512, 512), 512)
+                rc = cols(q // 2)
+                res = tn(la[:, lc], ra[0:ROWS, rc]) + tn(lb[:, lc], rb[:, rc])
+                part[p, 0] = res[0:BLK]
+                part[p, 1] = res[BLK:2 * BLK]
+
+        @pl.when((u >= GRAM_UNITS) & (w == 2))
+        def _():
+            rc = pl.ds(pl.multiple_of(q * 512, 512), 512)
+            res = tn(hh[...], dz[:, rc]) + tn(ho[...], dzo[:, rc])
+            part[p, 0] = res[:, 0:BLK]
+            part[p, 1] = res[:, BLK:2 * BLK]
 
     def grad_unit(u):
-        v = u - GRAM_UNITS
-        w = v // 16
-        q = lax.rem(v, 16)
-        return w, jnp.where(w == 2, 0, lax.rem(q, 4)), jnp.where(w == 2, q, q // 4)
-
-    def base(u):
-        w, rb, cb = grad_unit(u)
-        return w * 2048 + c * jnp.where(w == 2, 256, 1024) + rb * 256, cb * 512
-
-    def region(u, k, off, n):
-        r0, c0 = base(u)
-        return g_o.at[rows_at(r0 + off, n), pl.ds(pl.multiple_of(c0 + k * BLK, BLK), BLK)]
+        v = jnp.maximum(u - GRAM_UNITS, 0)
+        return v // 16, lax.rem(v, 16)
+
+    def of_weight(u, w):
+        return (u >= GRAM_UNITS) & (grad_unit(u)[0] == w)
+
+    def region(u, w, k, off, n):
+        q = grad_unit(u)[1]
+        if w == 2:
+            r0, c0 = c * 256, q * 512 + k * BLK
+        else:
+            r0, c0 = c * 1024 + lax.rem(q, 2) * 512 + k * BLK, (q // 2) * BLK
+        return rows_at(r0 + off, n), cols_at(c0)
+
+    grads = (g3_o, g2v, g1v)
 
     def keep_copy(u, k):
-        return pltpu.make_async_copy(part.at[lax.rem(u, SLOTS), k, rows_at(me.keep[k][4], 16)],
-                                     region(u, k, me.keep[k][4], 16), lsem.at[k, lax.rem(u, RING)])
-
-    def spread(u, s, k):
+        own = region(u, 0, k, me.keep[k][4], 16)
+        return pltpu.make_async_copy(stage.at[lax.rem(u, RING), k], g3_o.at[own], lsem.at[k, lax.rem(u, RING)])
+
+    def spread(u, w, s, k):
         r = lax.rem(u, RING)
-        dst = region(u, k, me.keep[k][s], BLK >> s)
-        src = part.at[lax.rem(u, SLOTS), k, rows_at(me.keep[k][4], 16)] if s == 4 else dst
+        dst = grads[w].at[region(u, w, k, me.keep[k][s], BLK >> s)]
+        src = stage.at[r, k] if s == 4 and w == 0 else dst
         return rcopy(src, dst, asem.at[s, k, r], bsem.at[s, k, r], me.peers[k][s - 1])
 
-    def cross(u):
+    def cross(u, w):
         r = lax.rem(u, RING)
-        r0, c0 = base(u)
-        reg = g_o.at[rows_at(r0, BLK), pl.ds(pl.multiple_of(c0, 512), 512)]
-        return rcopy(reg, reg, asem.at[0, 0, r], bsem.at[0, 0, r], me.pc)
+        q = grad_unit(u)[1]
+        buf = grads[w].at[unit_region(q, w, c)]
+        return rcopy(buf, buf, asem.at[0, 0, r], bsem.at[0, 0, r], me.pc)
+
+    def unit_region(q, w, core):
+        if w == 2:
+            return rows_at(core * 256, 256), pl.ds(pl.multiple_of(q * 512, 512), 512)
+        return rows_at(core * 1024 + lax.rem(q, 2) * 512, 512), cols(q // 2)
+
+    def put(u, w, own):
+        reg = unit_region(grad_unit(u)[1], w, c if own else 1 - c)
+        out = (None, g2_o, g1_o)[w]
+        return pltpu.make_async_copy(grads[w].at[reg], out.at[reg], psem.at[0 if own else 1, lax.rem(u, RING)])
 
     def spread_gram(u, s, k):
         i, j = block_of(2 * u + k)
@@ -367,11 +401,18 @@
         return rcopy(buf, buf, gasem.at[s - 1, k, r], gbsem.at[s - 1, k, r], me.peers[k][s - 1])
 
     def final(u):
-        @pl.when(u >= GRAM_UNITS)
-        def _():
-            for k in range(2):
-                spread(u, 4, k).start()
-                keep_copy(u, k).start()
+        for w in range(3):
+            @pl.when(of_weight(u, w))
+            def _(w=w):
+                for k in range(2):
+                    piece = part[lax.rem(u, SLOTS), k, rows_at(me.keep[k][4], 16)]
+                    if w == 0:
+                        stage[lax.rem(u, RING), k] = piece
+                        keep_copy(u, k).start()
+                    else:
+                        rr, cc = region(u, w, k, me.keep[k][4], 16)
+                        grads[w][rr, cc] = piece
+                    spread(u, w, 4, k).start()
 
         @pl.when(u < GRAM_UNITS)
         def _():
@@ -379,7 +420,7 @@
                 i, j = block_of(2 * u + k)
                 own = rows_at(me.keep[k][4], 16)
                 row0 = rows_at(i * BLK + me.keep[k][4], 16)
-                mu_r = mut[row0]
+                mu_r = g1v[rows_at(lax.rem(i, 2) * BLK + me.keep[k][4], 16), lanes_at((i // 2) * 128)]
                 mu_c = sv[pl.ds(j, 1)]
                 mm = ALL_ROWS * jnp.concatenate([mu_r, mu_r], axis=1) * mu_c
                 cov = (part[lax.rem(u, SLOTS), k, own] - mm) * (1.0 / (ALL_ROWS - 1))
@@ -394,19 +435,21 @@
                 gw[row0, cols(j)] = jnp.where(diag, -hinge, (2.0 * COV_WEIGHT) * cov).astype(BF16)
                 spread_gram(u, 4, k).start()
 
+    def diff_block(j):
+        diff = zd[0:ROWS, cols(j)].astype(F32) - zod[:, cols(j)].astype(F32)
+        sq = jnp.sum((diff * diff).reshape(ROWS // 8, 8, BLK), axis=0)
+        lacc[...] = lacc[...] + (0.5 * INV_WEIGHT / ALL_ROWS) * sq
+        da[:, cols(j)] = (2.0 * INV_WEIGHT / ALL_ROWS) * diff
+
     def dz_block(j):
         acc = nn(zd[...], gw[:, cols(j)])
         mean = acc[ROWS:ROWS + 1] + acc[ROWS + 1:ROWS + 2] + acc[ROWS + 2:ROWS + 3]
-        diff = zd[0:ROWS, cols(j)].astype(F32) - zod[:, cols(j)].astype(F32)
-        sq = jnp.sum((diff * diff).reshape(ROWS // 8, 8, BLK), axis=0)
-        lacc[...] = lacc[...] + (0.5 * INV_WEIGHT / ALL_ROWS) * sq
-        dz[:, cols(j)] = ((2.0 * INV_WEIGHT / ALL_ROWS) * diff
-                          + (2.0 / (ALL_ROWS - 1)) * (acc[0:ROWS] - mean)).astype(BF16)
+        dz[:, cols(j)] = (da[:, cols(j)] + (2.0 / (ALL_ROWS - 1)) * (acc[0:ROWS] - mean)).astype(BF16)
 
     def back_block(j, grad, st, layer):
         dx = nt(grad[0:ROWS, :], gw[cols(j)])
         nrm = nv[:, cols(j)]
-        act = gb[pl.ds(2 * NB * layer + j, 1)] * nrm + gb[pl.ds(2 * NB * layer + NB + j, 1)]
+        act = gains[layer][:, cols(j)] * nrm + biases[layer][:, cols(j)]
         d_act = jnp.where(act > 0.0, dx, 0.0)
         da[:, cols(j)] = d_act
         st[pl.ds(j, 1)] = jnp.sum(d_act, axis=0, keepdims=True)
@@ -414,7 +457,7 @@
 
     def back_pre(dst, st, layer):
         def step(j, carry):
-            scale = gb[pl.ds(2 * NB * layer + j, 1)] * rs[pl.ds(NB * layer + j, 1)]
+            scale = gains[layer][:, cols(j)] * rs[pl.ds(NB * layer + j, 1)]
             m0 = st[pl.ds(j, 1)] * (1.0 / ALL_ROWS)
             m1 = st[pl.ds(NB + j, 1)] * (1.0 / ALL_ROWS)
             dst[0:ROWS, cols(j)] = (scale * (da[:, cols(j)] - m0 - nv[:, cols(j)] * m1)).astype(BF16)
@@ -424,27 +467,38 @@
     compute(jnp.int32(0))
 
     def slot(t, carry):
+        u, ok = unit_at(t - 9 * LAG - 1)
+        for w in (1, 2):
+            @pl.when(ok & of_weight(u, w))
+            def _(u=u, w=w):
+                put(u, w, False).wait()
+
         u, ok = unit_at(t - 9 * LAG)
-
-        @pl.when(ok & (u >= GRAM_UNITS))
-        def _(u=u):
-            cross(u).wait()
+        for w in range(3):
+            @pl.when(ok & of_weight(u, w))
+            def _(u=u, w=w):
+                cross(u, w).wait()
+                if w > 0:
+                    put(u, w, True).wait()
+                    put(u, w, False).start()
 
         for s in (1, 2, 3, 4):
             u, ok = unit_at(t - LAG * (9 - s))
-
-            @pl.when(ok & (u >= GRAM_UNITS))
-            def _(s=s, u=u):
-                for k in range(2):
-                    cp = spread(u, s, k)
-                    cp.wait_send()
-                    cp.wait_recv()
-                    if s == 4:
-                        keep_copy(u, k).wait()
-                    if s > 1:
-                        spread(u, s - 1, k).start()
-                if s == 1:
-                    cross(u).start()
+            for w in range(3):
+                @pl.when(ok & of_weight(u, w))
+                def _(s=s, u=u, w=w):
+                    for k in range(2):
+                        cp = spread(u, w, s, k)
+                        cp.wait_send()
+                        cp.wait_recv()
+                        if s == 4 and w == 0:
+                            keep_copy(u, k).wait()
+                        if s > 1:
+                            spread(u, w, s - 1, k).start()
+                    if s == 1:
+                        cross(u, w).start()
+                        if w > 0:
+                            put(u, w, True).start()
 
             @pl.when(ok & (u < GRAM_UNITS))
             def _(s=s, u=u):
@@ -462,14 +516,7 @@
                         def _():
                             gw[rows_at(j * BLK, BLK), cols(i)] = gw[rows_at(i * BLK, BLK), cols(j)].T
 
-        sc.advance(t, final)
-        u, ok = unit_at(t)
-
-        @pl.when(ok)
-        def _(u=u):
-            sc.begin(u)
-
-        for first, red in ((3, red0), (PASS_2 + 3, red2), (PASS_1 + 3, red1)):
+        for first, red in ((3, red0), (PASS_2 + 2, red2), (PASS_1 + 2, red1)):
             for ph in range(2):
                 @pl.when(t == first + ph + 1)
                 def _(red=red, ph=ph):
@@ -478,6 +525,33 @@
                 @pl.when(t == first + ph)
                 def _(red=red, ph=ph):
                     red.start(ph)
+
+        for first, st, layer, dst in ((PASS_2, s2, 1, zd), (PASS_1, s1, 0, dz)):
+            @pl.when(t == first + 4)
+            def _(st=st, layer=layer, dst=dst):
+                back_pre(dst, st, layer)
+
+        @pl.when(t == PASS_2 + 2)
+        def _():
+            load_w2.start()
+
+        @pl.when(t == PASS_2 + 4)
+        def _():
+            load_n1.start()
+            swap_du2.start()
+            swap_s2.start()
+
+        @pl.when(t == PASS_1 + 4)
+        def _():
+            swap_du1.start()
+            swap_s1.start()
+
+        sc.advance(t, final)
+        u, ok = unit_at(t)
+
+        @pl.when(ok)
+        def _(u=u):
+            sc.begin(u)
 
         @pl.when(t == 5)
         def _():
@@ -489,8 +563,8 @@
             for j in range(NB):
                 for h in range(2):
                     lanes = slice(128 * h, 128 * h + 128)
-                    dst = slice(j * BLK + 128 * h, j * BLK + 128 * h + 128)
-                    mut[dst] = jnp.broadcast_to(mean[j:j + 1, lanes], (128, 128)).T
+                    r0, c0 = (j % 2) * BLK + 128 * h, (j // 2) * 128
+                    g1v[r0:r0 + 128, c0:c0 + 128] = jnp.broadcast_to(mean[j:j + 1, lanes], (128, 128)).T
                 zd[ROWS:ROWS + 16, j * BLK:(j + 1) * BLK] = jnp.concatenate(
                     [hi[j:j + 1], mid[j:j + 1], low[j:j + 1], jnp.zeros((13, BLK), BF16)], axis=0)
 
@@ -503,28 +577,32 @@
             keep_x1.wait()
             keep_x2.wait()
             swap_x2.wait()
-            swap_h.wait()
             save_n1.wait()
             swap_z.start()
 
-        @pl.when(t == DZ_SLOTS[0] - 1)
+        @pl.when(t == 7)
         def _():
             swap_z.wait()
 
-        for p, first in enumerate(DZ_SLOTS):
+        @pl.when((t >= 8) & (t < 8 + NB))
+        def _():
+            diff_block(t - 8)
+
+        for j, first in enumerate(DZ_SLOTS):
             @pl.when(t == first + 1)
-            def _(p=p):
-                swap_dz(p).wait()
-
-            @pl.when(t == first)
-            def _(p=p):
-                def step(j, carry):
-                    dz_block(2 * p + j)
-                    return carry
-                lax.fori_loop(0, 2, step, 0)
-                swap_dz(p).start()
-
-        @pl.when(t == DZ_SLOTS[3])
+            def _(j=j):
+                swap_dz(j).wait()
+
+        mine_now = jnp.int32(-1)
+        for j, first in enumerate(DZ_SLOTS):
+            mine_now = jnp.where(t == first, j, mine_now)
+
+        @pl.when(mine_now >= 0)
+        def _():
+            dz_block(mine_now)
+            swap_dz(mine_now).start()
+
+        @pl.when(t == DZ_SLOTS[-1])
         def _():
             load_w3.start()
 
@@ -546,33 +624,14 @@
         def _():
             swap_du1.wait()
 
-        for first, grad, st, layer, dst in ((PASS_2, dz, s2, 1, zd), (PASS_1, zd, s1, 0, dz)):
-            @pl.when((t >= first) & (t < first + 3))
+        for first, grad, st, layer in ((PASS_2, dz, s2, 1), (PASS_1, zd, s1, 0)):
+            @pl.when((t >= first) & (t < first + 2))
             def _(first=first, grad=grad, st=st, layer=layer):
                 def step(j, carry):
                     back_block(j, grad, st, layer)
                     return carry
-                lo = 3 * (t - first)
-                lax.fori_loop(lo, jnp.minimum(lo + 3, NB), step, 0)
-
-            @pl.when(t == first + 5)
-            def _(st=st, layer=layer, dst=dst):
-                back_pre(dst, st, layer)
-
-        @pl.when(t == PASS_2 + 3)
-        def _():
-            load_w2.start()
-
-        @pl.when(t == PASS_2 + 5)
-        def _():
-            load_n1.start()
-            swap_du2.start()
-            swap_s2.start()
-
-        @pl.when(t == PASS_1 + 5)
-        def _():
-            swap_du1.start()
-            swap_s1.start()
+                lo = 4 * (t - first)
+                lax.fori_loop(lo, lo + 4, step, 0)
 
         u, ok = unit_at(t + 1)
 
@@ -583,43 +642,47 @@
     lax.fori_loop(0, END, slot, 0)
     swap_s2.wait()
     swap_s1.wait()
-    st2_o[...] = s2[...] + e2[...]
-    st1_o[...] = s1[...] + e1[...]
-
-
-def train_step(ha, hb, w1, w2, w3, gb):
+    sum2, sum1 = s2[...] + e2[...], s1[...] + e1[...]
+    for j in range(NB):
+        lanes = slice(j * BLK, (j + 1) * BLK)
+        st_o[0:1, lanes] = sum1[NB + j:NB + j + 1]
+        st_o[1:2, lanes] = sum1[j:j + 1]
+        st_o[2:3, lanes] = sum2[NB + j:NB + j + 1]
+        st_o[3:4, lanes] = sum2[j:j + 1]
+    total = jnp.sum(jnp.sum(sum2[2 * NB:], axis=0, keepdims=True), axis=1, keepdims=True)
+    st_o[4:5, 0:128] = jnp.broadcast_to(total, (1, 128))
+
+
+def train_step(ha, hb, w1, w2, w3, g1, b1, g2, b2):
     act = pltpu.VMEM((ROWS, DIM), BF16)
     piece = pltpu.VMEM((ROWS, 1024), BF16)
-    wide = pltpu.VMEM((ROWS, DIM), F32)
     dma = pltpu.SemaphoreType.DMA
     return pl.pallas_call(
         step_kernel,
-        out_shape=(sds((2 * DIM + FEAT, DIM), F32), sds((ROWS, DIM), F32), sds((3 * NB, BLK), F32),
-                   sds((2 * NB, BLK), F32)),
-        in_specs=[ANY] * 5 + [INV],
-        out_specs=(ANY, ANY, INV, INV),
+        out_shape=(sds((DIM, DIM), F32), sds((DIM, DIM), F32), sds((FEAT, DIM), F32), sds((ROWS, DIM), F32),
+                   sds((8, DIM), F32)),
+        in_specs=[ANY] * 5 + [INV] * 4,
+        out_specs=(ANY, ANY, ANY, ANY, INV),
         scratch_shapes=[pltpu.VMEM((ROWS + 16, DIM), BF16), act, act, act, pltpu.VMEM((DIM, DIM), BF16),
-                        piece, piece, piece, piece, pltpu.VMEM((ROWS, FEAT), BF16), pltpu.VMEM((ROWS, 256), BF16),
-                        wide, wide, pltpu.VMEM((DIM, 128), F32), pltpu.VMEM((NB, BLK), F32),
-                        pltpu.VMEM((2 * NB, BLK), F32)]
+                        piece, piece, piece, piece, pltpu.VMEM((ROWS, 256), BF16), pltpu.VMEM((ROWS, 256), BF16),
+                        pltpu.VMEM((DIM, DIM), F32), pltpu.VMEM((FEAT, DIM), F32),
+                        pltpu.VMEM((NB, BLK), F32), pltpu.VMEM((2 * NB, BLK), F32),
+                        pltpu.VMEM((RING, 2, 16, BLK), F32)]
         + scatter_scratch(SLOTS) + small_scratch(NB) + small_scratch(2 * NB) + small_scratch(2 * NB)
         + small_scratch(3 * NB) + small_scratch(2 * NB)
         + [pltpu.VMEM((3 * NB, BLK), F32), pltpu.VMEM((2 * NB, BLK), F32),
            dma((4, 2, RING)), dma((4, 2, RING)), dma((5, 2, RING)), dma((5, 2, RING)), dma((2, RING)),
-           dma((10,)), dma((13,)), dma((13,))],
+           dma((2, RING)), dma((10,)), dma((17,)), dma((17,))],
         compiler_params=pltpu.CompilerParams(collective_id=0, has_side_effects=True, vmem_limit_bytes=VMEM_LIMIT),
         name='train_step',
-    )(ha, hb, w1, w2, w3, gb)
+    )(ha, hb, w1, w2, w3, g1, b1, g2, b2)
 
 
 def solution(mesh):
     def local_step(h_a, h_b, w_one, w_two, w_three, gain_one, bias_one, gain_two, bias_two):
-        gb = jnp.stack([gain_one, bias_one, gain_two, bias_two]).reshape(4 * NB, BLK)
-        grads, _, st2, st1 = train_step(h_a, h_b, w_one, w_two, w_three, gb)
-        loss = jnp.sum(st2[2 * NB:])
-        return (loss, grads[2 * DIM:], grads[DIM:2 * DIM], grads[:DIM],
-                st1[NB:2 * NB].reshape(DIM), st1[:NB].reshape(DIM),
-                st2[NB:2 * NB].reshape(DIM), st2[:NB].reshape(DIM))
+        vecs = [v.reshape(1, DIM) for v in (gain_one, bias_one, gain_two, bias_two)]
+        d_three, d_two, d_one, _, st = train_step(h_a, h_b, w_one, w_two, w_three, *vecs)
+        return st[4, 0], d_one, d_two, d_three, st[0], st[1], st[2], st[3]
 
     row_spec = P('data', None)
     return jax.shard_map(local_step, mesh=mesh,

time: 473 us -> 463 us (0.979)
  Pallas kernels: 440 us -> 433 us
    unnamed x5 -> x11, local copies, waits for them, and re-layouts: 3.13 us -> 26.3 us
    slice x2, local copies, waits for them, and re-layouts: 25.9 us -> 2.81 us  [local_step(): return (st[4, 0], d_one, d_two, d_three, st[0], st[1], st[2], st[3])]
    pallas_call x1, Pallas kernels: 440 us -> 433 us  [train_step(): pl.pallas_call(step_kernel, out_shape=(sds((DIM, DIM), F32), sds((DIM, DI...]
where the time goes in v4:
time: 463 us
  Pallas kernels  433 us (94%)
  local copies, waits for them, and re-layouts  29.1 us (6%)
    pallas_call x1, Pallas kernels, train_step(): pl.pallas_call(step_kernel, out_shape=(sds((DIM, DIM), F32), sds((DIM, DI...  433 us
    unnamed x11, local copies, waits for them, and re-layouts  26.3 us

profile of v4, /device:TPU:0, one launch (start us, length us, event | category | flops | bytes accessed | tf_op | source)
XLA Modules:
  0.0 463.2 jit_solution(4274029783810152015)
XLA Ops:
  0.6 433.4 %train_step.1 = (f32[2048,2048]{1,0:T(8,128)}, f32[2048,2048]{1,0:T(8,128)}, f32[512,2048]{1,0:T(8,128)}, f32[1024,2048]{1,0:T(8,128)}, f32[8,2048]{1,0:T(8,128)}) custom-call(bf16[512,512]{1,0:T(8,128)(2,1)} %ha.1, bf16[512,512]{1,0:T(8,128)(2,1)} %hb.1, bf16[512,2048]{1,0:T(8,128)(2,1)} %w1.1, bf16[2048,2048]{1,0:T(8,128)(2,1)} %w2.1, ...), custom_call_target="tpu_custom_call" | custom-call | tf_op jit(solution)/shard_map/train_step/pallas_call | solution.py:660
  434.1 1.2 slice.15
  435.3 1.6 fusion
  436.9 0.0 slice-start
  436.9 4.8 %copy.20 = f32[512,2048]{1,0:T(8,128)} copy(f32[512,2048]{1,0:T(8,128)} %get-tuple-element.29) | data formatting | bytes 8388608
  441.7 0.0 slice-start.1
  441.7 0.0 slice-start.2
  441.7 0.0 slice-start.3
  441.7 13.6 %copy.21 = f32[2048,2048]{1,0:T(8,128)} copy(f32[2048,2048]{1,0:T(8,128)} %get-tuple-element.30) | data formatting | bytes 33554432
  455.3 0.0 slice-done
  455.3 0.0 slice-done.1
  455.3 0.0 slice-done.2
  455.3 1.7 slice-done.3
  457.0 6.2 %copy.22 = f32[2048,2048]{1,0:T(8,128)} copy(f32[2048,2048]{1,0:T(8,128)S(1)} %bitcast.10) | data formatting | bytes 33554432
  (1 shorter events, 0.0 us)
Async XLA Ops:
  436.9 18.4 %slice-start = ((s8[16777216]{0:T(1024)(128)(4,1)}), s8[4194304]{0:T(1024)(128)(4,1)S(1)}, s32[]{:S(2)}) async-start(s8[16777216]{0:T(1024)(128)(4,1)} %bitcast.9), calls=%async_computation | async-start | bytes 8388608
  441.7 13.6 %slice-start.1 = ((s8[16777216]{0:T(1024)(128)(4,1)}), s8[4194304]{0:T(1024)(128)(4,1)S(1)}, s32[]{:S(2)}) async-start(s8[16777216]{0:T(1024)(128)(4,1)} %bitcast.9), calls=%async_computation.1 | async-start | bytes 8388608
  441.7 13.6 %slice-start.2 = ((s8[16777216]{0:T(1024)(128)(4,1)}), s8[4194304]{0:T(1024)(128)(4,1)S(1)}, s32[]{:S(2)}) async-start(s8[16777216]{0:T(1024)(128)(4,1)} %bitcast.9), calls=%async_computation.2 | async-start | bytes 8388608
  441.7 15.3 %slice-start.3 = ((s8[16777216]{0:T(1024)(128)(4,1)}), s8[4194304]{0:T(1024)(128)(4,1)S(1)}, s32[]{:S(2)}) async-start(s8[16777216]{0:T(1024)(128)(4,1)} %bitcast.9), calls=%async_computation.3 | async-start | bytes 8388608

commit v5 on v4

--- a/solution.py
+++ b/solution.py
@@ -25,7 +25,7 @@
 NB = 8
 BLK = 256
 LAG = 2
-RING = 4
+RING = 6
 ALL_ROWS = 16384
 
 
@@ -54,20 +54,15 @@
         pd = px + py - i
         p3 = p1 + p2 - i
         self.phases = ((px, py, pd), (p1, p2, p3))
-        self.bits = ((x, zl, y, zh), (y, zl, x, zh))
-        self.peers = ((px, p1, py, p2), (py, p1, px, p2))
-        self.keep = []
-        self.send = []
-        for k in range(2):
-            keep = [0]
-            send = [None]
-            for s in range(1, 5):
-                n = BLK >> s
-                bit = self.bits[k][s - 1]
-                send.append(keep[-1] + (1 - bit) * n)
-                keep.append(keep[-1] + bit * n)
-            self.keep.append(keep)
-            self.send.append(send)
+        self.end = zl == zh
+        self.p1, self.p3 = p1, p3
+        self.first, self.last = (px, py), (py, px)
+        self.keep = [b * 128 for b in (x, y)]
+        self.send = [(1 - b) * 128 for b in (x, y)]
+        self.near = [k + zh * 64 for k in self.keep]
+        self.far = [k + (1 - zh) * 64 for k in self.keep]
+        self.own = [n + b * 32 for n, b in zip(self.near, (y, x))]
+        self.give = [n + (1 - b) * 32 for n, b in zip(self.near, (y, x))]
 
     def barrier(self):
         sem = pltpu.get_barrier_semaphore()
@@ -111,43 +106,86 @@
 
 class Scatter:
     def __init__(self, place, part, lands, ssem, rsem):
-        self.pl, self.part, self.lands, self.ssem, self.rsem = place, part, lands, ssem, rsem
-
-    def copy(self, u, s, k):
-        n = BLK >> s
-        r = lax.rem(u, RING)
-        return rcopy(self.part.at[lax.rem(u, SLOTS), k, rows_at(self.pl.send[k][s], n)],
-                     self.lands[s - 1].at[r, k], self.ssem.at[s - 1, k, r], self.rsem.at[s - 1, k, r],
-                     self.pl.peers[k][s - 1])
-
-    def begin(self, u):
+        self.pl, self.part, self.ssem, self.rsem = place, part, ssem, rsem
+        self.lands = (lands[0], lands[1], lands[2], lands[1], lands[3])
+
+    def copy(self, u, e, k):
+        me = self.pl
+        off, n, dev = ((me.send[k], 128, me.first[k]), (me.far[k], 64, me.p1), (me.far[k], 64, me.p3),
+                       (me.near[k], 64, me.p1), (me.give[k], 32, me.last[k]))[e]
+        land, r = self.lands[e], lax.rem(u, RING)
+        return rcopy(self.part.at[lax.rem(u, SLOTS), k, rows_at(off, n)],
+                     land.at[lax.rem(u, land.shape[0]), k], self.ssem.at[e, k, r], self.rsem.at[e, k, r], dev)
+
+    def start(self, u, e):
         for k in range(2):
-            self.copy(u, 1, k).start()
+            self.copy(u, e, k).start()
+
+    def sent(self, u, e):
+        for k in range(2):
+            self.copy(u, e, k).wait_send()
+
+    def add(self, u, e, off):
+        p, n = lax.rem(u, SLOTS), (128, 64, 64, 64, 32)[e]
+        land = self.lands[e]
+        for k in range(2):
+            self.copy(u, e, k).wait_recv()
+            rr = rows_at(off[k], n)
+            self.part[p, k, rr] = self.part[p, k, rr] + land[lax.rem(u, land.shape[0]), k]
 
     def advance(self, t, final):
-        for s in (4, 3, 2, 1):
-            u, ok = unit_at(t - LAG * s)
-
-            @pl.when(ok)
-            def _(s=s, u=u):
-                n = BLK >> s
-                p, r = lax.rem(u, SLOTS), lax.rem(u, RING)
-                for k in range(2):
-                    cp = self.copy(u, s, k)
-                    cp.wait_send()
-                    cp.wait_recv()
-                    rr = rows_at(self.pl.keep[k][s], n)
-                    self.part[p, k, rr] = self.part[p, k, rr] + self.lands[s - 1][r, k]
-                    if s < 4:
-                        self.copy(u, s + 1, k).start()
-                if s == 4:
-                    final(u)
+        me = self.pl
+        u5, ok5 = unit_at(t - 5 * LAG)
+        u4, ok4 = unit_at(t - 4 * LAG)
+        u3, ok3 = unit_at(t - 3 * LAG)
+        u2, ok2 = unit_at(t - 2 * LAG)
+        u1, ok1 = unit_at(t - LAG)
+        inner = jnp.logical_not(me.end)
+
+        @pl.when(ok5 & me.end)
+        def _():
+            self.sent(u5, 4)
+            self.add(u5, 4, me.own)
+            final(u5)
+
+        @pl.when(ok4 & me.end)
+        def _():
+            self.add(u4, 3, me.near)
+            self.start(u4, 4)
+
+        @pl.when(ok4 & inner)
+        def _():
+            self.sent(u4, 3)
+
+        @pl.when(ok3 & inner)
+        def _():
+            self.sent(u3, 2)
+            self.add(u3, 2, me.near)
+            self.start(u3, 3)
+
+        @pl.when(ok2 & inner)
+        def _():
+            self.add(u2, 1, me.far)
+            self.start(u2, 2)
+
+        @pl.when(ok2 & me.end)
+        def _():
+            self.sent(u2, 1)
+
+        @pl.when(ok1)
+        def _():
+            self.sent(u1, 0)
+            self.add(u1, 0, me.keep)
+
+        @pl.when(ok1 & me.end)
+        def _():
+            self.start(u1, 1)
 
 
 def scatter_scratch(slots):
-    return [pltpu.VMEM((slots, 2, BLK, BLK), F32)] + \
-        [pltpu.VMEM((RING, 2, BLK >> s, BLK), F32) for s in range(1, 5)] + \
-        [pltpu.SemaphoreType.DMA((4, 2, RING)), pltpu.SemaphoreType.DMA((4, 2, RING))]
+    return [pltpu.VMEM((slots, 2, BLK, BLK), F32), pltpu.VMEM((4, 2, 128, BLK), F32),
+            pltpu.VMEM((6, 2, 64, BLK), F32), pltpu.VMEM((4, 2, 64, BLK), F32), pltpu.VMEM((4, 2, 32, BLK), F32),
+            pltpu.SemaphoreType.DMA((5, 2, RING)), pltpu.SemaphoreType.DMA((5, 2, RING))]
 
 
 class SmallReduce:
@@ -179,14 +217,16 @@
 
 
 GRAM_UNITS = 18
+GRAM = 3
 UNITS = 54
-SLOTS = 4 * LAG + 1
-START_3 = 24
-START_2 = 41
-END = START_2 + 21 + 9 * LAG
-DZ_SLOTS = (20, 23, 26, 28, 30, 32, 33, 34)
-PASS_2 = 35
-PASS_1 = 42
+SLOTS = 5 * LAG + 1
+START_3 = 28
+START_2 = 44
+END = START_2 + 21 + 11 * LAG
+DZ_SLOTS = (23, 27, 30, 32, 34, 36, 37, 38)
+PASS_2 = 39
+PASS_1 = 45
+SPAN_2, SPAN_1 = 3, 4
 
 
 def block_of(q):
@@ -202,11 +242,11 @@
     return jnp.where(ok, u, 0), ok
 
 
-def step_kernel(ha, hb, w1, w2, w3, g1, b1, g2, b2, g3_o, g2_o, g1_o, n1_o, st_o,
-                zd, zod, dz, dzo, gw, x2h, x2o, x1h, x1o, hh, ho, g2v, g1v, lacc, rs, stage,
+def step_kernel(ha, hb, w1, w2, w3, g1, b1, g2, b2, g3_o, g2_o, g1_o, n1_o, h_o, ho_o, st_o,
+                zd, zod, dz, dzo, gw, x2h, x2o, x1h, x1o, g2v, g1v, lacc, rs, stage,
                 part, r1, r2, r3, r4, ssem, rsem, sv, sl, sa, sb, f1, fl1, fa1, fb1, f2, fl2, fa2, fb2,
                 s2, l2, sa2, sb2, s1, l1, sa1, sb1, e2, e1,
-                gasem, gbsem, asem, bsem, lsem, psem, csem, dsem, esem):
+                asem, bsem, lsem, psem, csem, dsem, esem, wsem):
     me = Place()
     c = me.c
     nv, da = g2v.at[pl.ds(0, ROWS)], g2v.at[pl.ds(ROWS, ROWS)]
@@ -222,18 +262,18 @@
     load_w1 = pltpu.make_async_copy(w1, w1v, csem.at[0])
     load_w2a = pltpu.make_async_copy(w2, gw, csem.at[1])
     load_w3a = pltpu.make_async_copy(w3, gw, csem.at[2])
-    load_w3 = pltpu.make_async_copy(w3, gw, csem.at[2])
     load_w2 = pltpu.make_async_copy(w2, gw, csem.at[6])
     load_n1 = pltpu.make_async_copy(n1_o, nv, csem.at[7])
     save_n1 = pltpu.make_async_copy(da, n1_o, csem.at[8])
     keep_x1 = pltpu.make_async_copy(dzo.at[:, half], x1h, csem.at[3])
-    keep_h = pltpu.make_async_copy(hv.at[:, hhalf], hh, csem.at[5])
+    keep_h = pltpu.make_async_copy(hv.at[:, hhalf], h_o, csem.at[5])
+    hh, ho = x2h.at[:, pl.ds(0, 256)], x2o.at[:, pl.ds(0, 256)]
+    load_h2 = [pltpu.make_async_copy(h_o, hh, csem.at[5]), pltpu.make_async_copy(ho_o, ho, csem.at[2])]
     keep_x2 = pltpu.make_async_copy(dz.at[:, half], x2h, csem.at[4])
     swap_z = rcopy(zd.at[body], zod, dsem.at[0], esem.at[0], me.pc)
     swap_x2 = rcopy(dz.at[:, ohalf], x2o, dsem.at[1], esem.at[1], me.pc)
     swap_x1 = rcopy(dzo.at[:, ohalf], x1o, dsem.at[2], esem.at[2], me.pc)
-    swap_h = rcopy(hv.at[:, hohalf], ho, dsem.at[3], esem.at[3], me.pc)
-    swap_du2 = rcopy(zd.at[body], zod, dsem.at[4], esem.at[4], me.pc)
+    swap_h = rcopy(hv.at[:, hohalf], ho_o, dsem.at[3], esem.at[3], me.pc)
     swap_du1 = rcopy(dz, dzo, dsem.at[5], esem.at[5], me.pc)
     swap_s2 = rcopy(s2, e2, dsem.at[6], esem.at[6], me.pc)
     swap_s1 = rcopy(s1, e1, dsem.at[7], esem.at[7], me.pc)
@@ -243,6 +283,12 @@
 
     def give_h(src):
         return rcopy(src, hv.at[mine], dsem.at[16], esem.at[16], me.pc)
+
+    def load_w3(j):
+        return pltpu.make_async_copy(w3.at[cols(j)], gw.at[cols(j)], wsem.at[j])
+
+    def swap_du2(j):
+        return rcopy(zd.at[body, cols(j)], zod.at[:, cols(j)], dsem.at[17 + j], esem.at[17 + j], me.pc)
 
     def swap_dz(j):
         return rcopy(dz.at[:, cols(j)], dzo.at[:, cols(j)], dsem.at[8 + j], esem.at[8 + j], me.pc)
@@ -356,6 +402,8 @@
         return v // 16, lax.rem(v, 16)
 
     def of_weight(u, w):
+        if w == GRAM:
+            return u < GRAM_UNITS
         return (u >= GRAM_UNITS) & (grad_unit(u)[0] == w)
 
     def region(u, w, k, off, n):
@@ -369,20 +417,30 @@
     grads = (g3_o, g2v, g1v)
 
     def keep_copy(u, k):
-        own = region(u, 0, k, me.keep[k][4], 16)
-        return pltpu.make_async_copy(stage.at[lax.rem(u, RING), k], g3_o.at[own], lsem.at[k, lax.rem(u, RING)])
-
-    def spread(u, w, s, k):
+        own = region(u, 0, k, me.own[k], 32)
+        return pltpu.make_async_copy(stage.at[lax.rem(u, 4), k], g3_o.at[own], lsem.at[k, lax.rem(u, RING)])
+
+    def hop(e, k):
+        return ((me.own[k], 32, me.last[k]), (me.near[k], 64, me.p1), (me.near[k], 64, me.p3),
+                (me.far[k], 64, me.p1), (me.keep[k], 128, me.first[k]))[e]
+
+    def spread(u, w, e, k):
         r = lax.rem(u, RING)
-        dst = grads[w].at[region(u, w, k, me.keep[k][s], BLK >> s)]
-        src = stage.at[r, k] if s == 4 and w == 0 else dst
-        return rcopy(src, dst, asem.at[s, k, r], bsem.at[s, k, r], me.peers[k][s - 1])
+        off, n, dev = hop(e, k)
+        if w == GRAM:
+            i, j = block_of(2 * u + k)
+            src = dst = gw.at[rows_at(i * BLK + off, n), cols(j)]
+        else:
+            dst = grads[w].at[region(u, w, k, off, n)]
+            src = stage.at[lax.rem(u, 4), k] if e == 0 and w == 0 else dst
+        g = 0 if w == GRAM else 1
+        return rcopy(src, dst, asem.at[g, e, k, r], bsem.at[g, e, k, r], dev)
 
     def cross(u, w):
         r = lax.rem(u, RING)
         q = grad_unit(u)[1]
         buf = grads[w].at[unit_region(q, w, c)]
-        return rcopy(buf, buf, asem.at[0, 0, r], bsem.at[0, 0, r], me.pc)
+        return rcopy(buf, buf, asem.at[1, 5, 0, r], bsem.at[1, 5, 0, r], me.pc)
 
     def unit_region(q, w, core):
         if w == 2:
@@ -393,47 +451,41 @@
         reg = unit_region(grad_unit(u)[1], w, c if own else 1 - c)
         out = (None, g2_o, g1_o)[w]
         return pltpu.make_async_copy(grads[w].at[reg], out.at[reg], psem.at[0 if own else 1, lax.rem(u, RING)])
-
-    def spread_gram(u, s, k):
-        i, j = block_of(2 * u + k)
-        r = lax.rem(u, RING)
-        buf = gw.at[rows_at(i * BLK + me.keep[k][s], BLK >> s), cols(j)]
-        return rcopy(buf, buf, gasem.at[s - 1, k, r], gbsem.at[s - 1, k, r], me.peers[k][s - 1])
 
     def final(u):
         for w in range(3):
             @pl.when(of_weight(u, w))
             def _(w=w):
                 for k in range(2):
-                    piece = part[lax.rem(u, SLOTS), k, rows_at(me.keep[k][4], 16)]
+                    piece = part[lax.rem(u, SLOTS), k, rows_at(me.own[k], 32)]
                     if w == 0:
-                        stage[lax.rem(u, RING), k] = piece
+                        stage[lax.rem(u, 4), k] = piece
                         keep_copy(u, k).start()
                     else:
-                        rr, cc = region(u, w, k, me.keep[k][4], 16)
+                        rr, cc = region(u, w, k, me.own[k], 32)
                         grads[w][rr, cc] = piece
-                    spread(u, w, 4, k).start()
+                    spread(u, w, 0, k).start()
 
         @pl.when(u < GRAM_UNITS)
         def _():
             for k in range(2):
                 i, j = block_of(2 * u + k)
-                own = rows_at(me.keep[k][4], 16)
-                row0 = rows_at(i * BLK + me.keep[k][4], 16)
-                mu_r = g1v[rows_at(lax.rem(i, 2) * BLK + me.keep[k][4], 16), lanes_at((i // 2) * 128)]
+                own = rows_at(me.own[k], 32)
+                row0 = rows_at(i * BLK + me.own[k], 32)
+                mu_r = g1v[rows_at(lax.rem(i, 2) * BLK + me.own[k], 32), lanes_at((i // 2) * 128)]
                 mu_c = sv[pl.ds(j, 1)]
                 mm = ALL_ROWS * jnp.concatenate([mu_r, mu_r], axis=1) * mu_c
                 cov = (part[lax.rem(u, SLOTS), k, own] - mm) * (1.0 / (ALL_ROWS - 1))
-                row = lax.broadcasted_iota(jnp.int32, (16, BLK), 0) + (i * BLK + me.keep[k][4])
-                col = lax.broadcasted_iota(jnp.int32, (16, BLK), 1) + j * BLK
+                row = lax.broadcasted_iota(jnp.int32, (32, BLK), 0) + (i * BLK + me.own[k])
+                col = lax.broadcasted_iota(jnp.int32, (32, BLK), 1) + j * BLK
                 diag = row == col
                 std = jnp.sqrt(jnp.where(diag, cov, 1.0) + STD_EPS)
                 hinge = jnp.where(std < 1.0, VAR_WEIGHT / (2.0 * std), 0.0)
                 weight = jnp.where(i == j, COV_WEIGHT, 2.0 * COV_WEIGHT)
                 term = jnp.where(diag, VAR_WEIGHT * jnp.maximum(1.0 - std, 0.0), weight * cov * cov)
-                lacc[...] = lacc[...] + term[0:8] + term[8:16]
+                lacc[...] = lacc[...] + ((term[0:8] + term[8:16]) + (term[16:24] + term[24:32]))
                 gw[row0, cols(j)] = jnp.where(diag, -hinge, (2.0 * COV_WEIGHT) * cov).astype(BF16)
-                spread_gram(u, 4, k).start()
+                spread(u, GRAM, 0, k).start()
 
     def diff_block(j):
         diff = zd[0:ROWS, cols(j)].astype(F32) - zod[:, cols(j)].astype(F32)
@@ -455,25 +507,76 @@
         st[pl.ds(j, 1)] = jnp.sum(d_act, axis=0, keepdims=True)
         st[pl.ds(NB + j, 1)] = jnp.sum(d_act * nrm, axis=0, keepdims=True)
 
-    def back_pre(dst, st, layer):
+    def back_pre(dst, st, layer, after):
         def step(j, carry):
             scale = gains[layer][:, cols(j)] * rs[pl.ds(NB * layer + j, 1)]
             m0 = st[pl.ds(j, 1)] * (1.0 / ALL_ROWS)
             m1 = st[pl.ds(NB + j, 1)] * (1.0 / ALL_ROWS)
             dst[0:ROWS, cols(j)] = (scale * (da[:, cols(j)] - m0 - nv[:, cols(j)] * m1)).astype(BF16)
+            after(j)
             return carry
         lax.fori_loop(0, NB, step, 0)
 
+    def gather_step(e, u, w):
+        def each(f):
+            for k in range(2):
+                f(k)
+
+        def wait_send(k):
+            spread(u, w, e - 1, k).wait_send()
+
+        def wait_recv(k):
+            spread(u, w, e - 1, k).wait_recv()
+
+        def begin(k):
+            spread(u, w, e, k).start()
+
+        def at_end():
+            if e == 1 and w == 0:
+                each(lambda k: keep_copy(u, k).wait())
+            if e in (1, 2, 5):
+                each(wait_send)
+            if e in (1, 4, 5):
+                each(wait_recv)
+            if e in (1, 4):
+                each(begin)
+
+        def at_inner():
+            if e in (3, 4, 5):
+                each(wait_send)
+            if e in (2, 3, 5):
+                each(wait_recv)
+            if e in (2, 3, 4):
+                each(begin)
+
+        if e == 5:
+            at_end()
+        else:
+            pl.when(me.end)(at_end)
+            if e > 1:
+                pl.when(jnp.logical_not(me.end))(at_inner)
+        if e == 5 and w < 3:
+            cross(u, w).start()
+            if w > 0:
+                put(u, w, True).start()
+        if e == 5 and w == GRAM:
+            for k in range(2):
+                i, j = block_of(2 * u + k)
+
+                @pl.when(i != j)
+                def _():
+                    gw[rows_at(j * BLK, BLK), cols(i)] = gw[rows_at(i * BLK, BLK), cols(j)].T
+
     compute(jnp.int32(0))
 
     def slot(t, carry):
-        u, ok = unit_at(t - 9 * LAG - 1)
+        u, ok = unit_at(t - 11 * LAG - 1)
         for w in (1, 2):
             @pl.when(ok & of_weight(u, w))
             def _(u=u, w=w):
                 put(u, w, False).wait()
 
-        u, ok = unit_at(t - 9 * LAG)
+        u, ok = unit_at(t - 11 * LAG)
         for w in range(3):
             @pl.when(ok & of_weight(u, w))
             def _(u=u, w=w):
@@ -482,66 +585,38 @@
                     put(u, w, True).wait()
                     put(u, w, False).start()
 
-        for s in (1, 2, 3, 4):
-            u, ok = unit_at(t - LAG * (9 - s))
-            for w in range(3):
+        for e in (5, 4, 3, 2, 1):
+            u, ok = unit_at(t - (5 + e) * LAG)
+            for w in range(4):
                 @pl.when(ok & of_weight(u, w))
-                def _(s=s, u=u, w=w):
-                    for k in range(2):
-                        cp = spread(u, w, s, k)
-                        cp.wait_send()
-                        cp.wait_recv()
-                        if s == 4 and w == 0:
-                            keep_copy(u, k).wait()
-                        if s > 1:
-                            spread(u, w, s - 1, k).start()
-                    if s == 1:
-                        cross(u, w).start()
-                        if w > 0:
-                            put(u, w, True).start()
-
-            @pl.when(ok & (u < GRAM_UNITS))
-            def _(s=s, u=u):
-                for k in range(2):
-                    cp = spread_gram(u, s, k)
-                    cp.wait_send()
-                    cp.wait_recv()
-                    if s > 1:
-                        spread_gram(u, s - 1, k).start()
-                if s == 1:
-                    for k in range(2):
-                        i, j = block_of(2 * u + k)
-
-                        @pl.when(i != j)
-                        def _():
-                            gw[rows_at(j * BLK, BLK), cols(i)] = gw[rows_at(i * BLK, BLK), cols(j)].T
-
-        for first, red in ((3, red0), (PASS_2 + 2, red2), (PASS_1 + 2, red1)):
-            for ph in range(2):
-                @pl.when(t == first + ph + 1)
-                def _(red=red, ph=ph):
-                    red.finish(ph)
-
-                @pl.when(t == first + ph)
-                def _(red=red, ph=ph):
-                    red.start(ph)
-
-        for first, st, layer, dst in ((PASS_2, s2, 1, zd), (PASS_1, s1, 0, dz)):
-            @pl.when(t == first + 4)
+                def _(e=e, u=u, w=w):
+                    gather_step(e, u, w)
+
+        for first, red in ((2, red0), (PASS_2 + SPAN_2 - 1, red2), (PASS_1 + SPAN_1 - 1, red1)):
+            @pl.when(t == first + 1)
+            def _(red=red):
+                red.finish(0)
+                red.start(1)
+
+            @pl.when(t == first + 2)
+            def _(red=red):
+                red.finish(1)
+
+        for first, st, layer, dst in ((PASS_2 + SPAN_2 + 1, s2, 1, zd), (PASS_1 + SPAN_1 + 1, s1, 0, dz)):
+            @pl.when(t == first)
             def _(st=st, layer=layer, dst=dst):
-                back_pre(dst, st, layer)
-
-        @pl.when(t == PASS_2 + 2)
+                back_pre(dst, st, layer, (lambda j: swap_du2(j).start()) if layer == 1 else (lambda j: None))
+
+        @pl.when(t == PASS_2 + SPAN_2)
         def _():
             load_w2.start()
 
-        @pl.when(t == PASS_2 + 4)
+        @pl.when(t == PASS_2 + SPAN_2 + 1)
         def _():
             load_n1.start()
-            swap_du2.start()
             swap_s2.start()
 
-        @pl.when(t == PASS_1 + 4)
+        @pl.when(t == PASS_1 + SPAN_1 + 1)
         def _():
             swap_du1.start()
             swap_s1.start()
@@ -551,9 +626,9 @@
 
         @pl.when(ok)
         def _(u=u):
-            sc.begin(u)
-
-        @pl.when(t == 5)
+            sc.start(u, 0)
+
+        @pl.when(t == 4)
         def _():
             mean = sv[...] * (1.0 / ALL_ROWS)
             sv[...] = mean
@@ -604,34 +679,50 @@
 
         @pl.when(t == DZ_SLOTS[-1])
         def _():
-            load_w3.start()
+            for j in range(NB):
+                load_w3(j).start()
 
         @pl.when(t == PASS_2)
         def _():
             s2[2 * NB:3 * NB] = lacc[...]
-            load_w3.wait()
 
         @pl.when(t == PASS_1)
         def _():
             load_w2.wait()
             load_n1.wait()
 
-        @pl.when(t == START_2 - 1)
-        def _():
-            swap_du2.wait()
+        block = (t - (START_2 - 1)) // 2
+
+        @pl.when((t >= START_2 - 1) & (t < START_2 + 15) & (t == START_2 - 1 + 2 * block))
+        def _():
+            swap_du2(block).wait()
+
+        @pl.when(t == START_2 + 8)
+        def _():
+            for cp in load_h2:
+                cp.start()
 
         @pl.when(t == START_2 + 14)
         def _():
             swap_du1.wait()
-
-        for first, grad, st, layer in ((PASS_2, dz, s2, 1), (PASS_1, zd, s1, 0)):
-            @pl.when((t >= first) & (t < first + 2))
-            def _(first=first, grad=grad, st=st, layer=layer):
+            for cp in load_h2:
+                cp.wait()
+
+        for first, span, grad, st, layer in ((PASS_2, SPAN_2, dz, s2, 1), (PASS_1, SPAN_1, zd, s1, 0)):
+            @pl.when((t >= first) & (t < first + span))
+            def _(first=first, n=-(-NB // span), grad=grad, st=st, layer=layer):
                 def step(j, carry):
+                    if layer == 1:
+                        load_w3(j).wait()
                     back_block(j, grad, st, layer)
                     return carry
-                lo = 4 * (t - first)
-                lax.fori_loop(lo, lo + 4, step, 0)
+                lo = n * (t - first)
+                lax.fori_loop(lo, jnp.minimum(lo + n, NB), step, 0)
+
+        for last, red in ((2, red0), (PASS_2 + SPAN_2 - 1, red2), (PASS_1 + SPAN_1 - 1, red1)):
+            @pl.when(t == last)
+            def _(red=red):
+                red.start(0)
 
         u, ok = unit_at(t + 1)
 
@@ -660,19 +751,19 @@
     return pl.pallas_call(
         step_kernel,
         out_shape=(sds((DIM, DIM), F32), sds((DIM, DIM), F32), sds((FEAT, DIM), F32), sds((ROWS, DIM), F32),
-                   sds((8, DIM), F32)),
+                   sds((ROWS, 256), BF16), sds((ROWS, 256), BF16), sds((8, DIM), F32)),
         in_specs=[ANY] * 5 + [INV] * 4,
-        out_specs=(ANY, ANY, ANY, ANY, INV),
+        out_specs=(ANY,) * 6 + (INV,),
         scratch_shapes=[pltpu.VMEM((ROWS + 16, DIM), BF16), act, act, act, pltpu.VMEM((DIM, DIM), BF16),
-                        piece, piece, piece, piece, pltpu.VMEM((ROWS, 256), BF16), pltpu.VMEM((ROWS, 256), BF16),
+                        piece, piece, piece, piece,
                         pltpu.VMEM((DIM, DIM), F32), pltpu.VMEM((FEAT, DIM), F32),
                         pltpu.VMEM((NB, BLK), F32), pltpu.VMEM((2 * NB, BLK), F32),
-                        pltpu.VMEM((RING, 2, 16, BLK), F32)]
+                        pltpu.VMEM((4, 2, 32, BLK), F32)]
         + scatter_scratch(SLOTS) + small_scratch(NB) + small_scratch(2 * NB) + small_scratch(2 * NB)
         + small_scratch(3 * NB) + small_scratch(2 * NB)
         + [pltpu.VMEM((3 * NB, BLK), F32), pltpu.VMEM((2 * NB, BLK), F32),
-           dma((4, 2, RING)), dma((4, 2, RING)), dma((5, 2, RING)), dma((5, 2, RING)), dma((2, RING)),
-           dma((2, RING)), dma((10,)), dma((17,)), dma((17,))],
+           dma((2, 6, 2, RING)), dma((2, 6, 2, RING)), dma((2, RING)),
+           dma((2, RING)), dma((10,)), dma((25,)), dma((25,)), dma((NB,))],
         compiler_params=pltpu.CompilerParams(collective_id=0, has_side_effects=True, vmem_limit_bytes=VMEM_LIMIT),
         name='train_step',
     )(ha, hb, w1, w2, w3, g1, b1, g2, b2)
@@ -681,7 +772,7 @@
 def solution(mesh):
     def local_step(h_a, h_b, w_one, w_two, w_three, gain_one, bias_one, gain_two, bias_two):
         vecs = [v.reshape(1, DIM) for v in (gain_one, bias_one, gain_two, bias_two)]
-        d_three, d_two, d_one, _, st = train_step(h_a, h_b, w_one, w_two, w_three, *vecs)
+        d_three, d_two, d_one, _, _, _, st = train_step(h_a, h_b, w_one, w_two, w_three, *vecs)
         return st[4, 0], d_one, d_two, d_three, st[0], st[1], st[2], st[3]
 
     row_spec = P('data', None)

time: 463 us -> 448 us (0.968)
  Pallas kernels: 433 us -> 418 us
    pallas_call x1, Pallas kernels: 433 us -> 418 us  [train_step(): pl.pallas_call(step_kernel, out_shape=(sds((DIM, DIM), F32), sds((DIM, DI...]
where the time goes in v5:
time: 448 us
  Pallas kernels  418 us (93%)
  local copies, waits for them, and re-layouts  29.1 us (6%)
    pallas_call x1, Pallas kernels, train_step(): pl.pallas_call(step_kernel, out_shape=(sds((DIM, DIM), F32), sds((DIM, DI...  418 us
    unnamed x11, local copies, waits for them, and re-layouts  26.3 us

profile of v5, /device:TPU:0, one launch (start us, length us, event | category | flops | bytes accessed | tf_op | source)
XLA Modules:
  0.0 448.0 jit_solution(14726739081559614890)
XLA Ops:
  0.6 418.2 %train_step.1 = (f32[2048,2048]{1,0:T(8,128)}, f32[2048,2048]{1,0:T(8,128)}, f32[512,2048]{1,0:T(8,128)}, f32[1024,2048]{1,0:T(8,128)}, bf16[1024,256]{1,0:T(8,1...) custom-call(bf16[512,512]{1,0:T(8,128)(2,1)} %ha.1, bf16[512,512]{1,0:T(8,128)(2,1)} %hb.1, bf16[512,2048]{1,0:T(8,128)(2,1)} %w1.1, ...), custom_call_target="tpu_custom_call" | custom-call | tf_op jit(solution)/shard_map/train_step/pallas_call | solution.py:751
  418.9 1.2 slice.15
  420.0 1.6 fusion
  421.6 0.0 slice-start
  421.7 4.8 %copy.20 = f32[512,2048]{1,0:T(8,128)} copy(f32[512,2048]{1,0:T(8,128)} %get-tuple-element.29) | data formatting | bytes 8388608
  426.5 0.0 slice-start.1
  426.5 0.0 slice-start.2
  426.5 0.0 slice-start.3
  426.5 13.6 %copy.21 = f32[2048,2048]{1,0:T(8,128)} copy(f32[2048,2048]{1,0:T(8,128)} %get-tuple-element.30) | data formatting | bytes 33554432
  440.1 0.0 slice-done
  440.1 0.0 slice-done.1
  440.1 0.0 slice-done.2
  440.1 1.7 slice-done.3
  441.8 6.2 %copy.22 = f32[2048,2048]{1,0:T(8,128)} copy(f32[2048,2048]{1,0:T(8,128)S(1)} %bitcast.10) | data formatting | bytes 33554432
  (1 shorter events, 0.0 us)
Async XLA Ops:
  421.6 18.4 %slice-start = ((s8[16777216]{0:T(1024)(128)(4,1)}), s8[4194304]{0:T(1024)(128)(4,1)S(1)}, s32[]{:S(2)}) async-start(s8[16777216]{0:T(1024)(128)(4,1)} %bitcast.9), calls=%async_computation | async-start | bytes 8388608
  426.5 13.6 %slice-start.1 = ((s8[16777216]{0:T(1024)(128)(4,1)}), s8[4194304]{0:T(1024)(128)(4,1)S(1)}, s32[]{:S(2)}) async-start(s8[16777216]{0:T(1024)(128)(4,1)} %bitcast.9), calls=%async_computation.1 | async-start | bytes 8388608
  426.5 13.6 %slice-start.2 = ((s8[16777216]{0:T(1024)(128)(4,1)}), s8[4194304]{0:T(1024)(128)(4,1)S(1)}, s32[]{:S(2)}) async-start(s8[16777216]{0:T(1024)(128)(4,1)} %bitcast.9), calls=%async_computation.2 | async-start | bytes 8388608
  426.5 15.3 %slice-start.3 = ((s8[16777216]{0:T(1024)(128)(4,1)}), s8[4194304]{0:T(1024)(128)(4,1)S(1)}, s32[]{:S(2)}) async-start(s8[16777216]{0:T(1024)(128)(4,1)} %bitcast.9), calls=%async_computation.3 | async-start | bytes 8388608

commit v6 on v5

--- a/solution.py
+++ b/solution.py
@@ -25,7 +25,7 @@
 NB = 8
 BLK = 256
 LAG = 2
-RING = 6
+RING = 8
 ALL_ROWS = 16384
 
 
@@ -104,34 +104,50 @@
     return pl.ds(pl.multiple_of(j * BLK, BLK), BLK)
 
 
+def is_inward(u):
+    return (u >= GRAM_UNITS) & (lax.rem(jnp.maximum(u - GRAM_UNITS, 0), 4) == 0)
+
+
 class Scatter:
     def __init__(self, place, part, lands, ssem, rsem):
-        self.pl, self.part, self.ssem, self.rsem = place, part, ssem, rsem
-        self.lands = (lands[0], lands[1], lands[2], lands[1], lands[3])
-
-    def copy(self, u, e, k):
+        self.pl, self.part, self.lands, self.ssem, self.rsem = place, part, lands, ssem, rsem
+
+    def landing(self, u, e, k, n):
+        v = jnp.maximum(u - GRAM_UNITS, 0)
+        q, r = v // 4, lax.rem(v, 4)
+        gram = u < GRAM_UNITS
+        if e in (0, 2):
+            return self.lands[e].at[lax.rem(u, 4), k]
+        if e == 4:
+            turn = jnp.where(gram, u, jnp.where(r == 0, q, v - 1 - q))
+            return self.lands[3].at[lax.rem(turn, 4), k]
+        off = jnp.where(gram, lax.rem(u, 8) * 64, lax.rem(q, 2) * 320 + jnp.where(r == 0, 0, 64 + r * 64))
+        return self.lands[1].at[k, pl.ds(pl.multiple_of(off, 64), n)]
+
+    def copy(self, u, e, k, inward=False):
         me = self.pl
         off, n, dev = ((me.send[k], 128, me.first[k]), (me.far[k], 64, me.p1), (me.far[k], 64, me.p3),
                        (me.near[k], 64, me.p1), (me.give[k], 32, me.last[k]))[e]
-        land, r = self.lands[e], lax.rem(u, RING)
-        return rcopy(self.part.at[lax.rem(u, SLOTS), k, rows_at(off, n)],
-                     land.at[lax.rem(u, land.shape[0]), k], self.ssem.at[e, k, r], self.rsem.at[e, k, r], dev)
-
-    def start(self, u, e):
+        if e == 1 and inward:
+            off, n = me.keep[k], 128
+        r = lax.rem(u, RING)
+        return rcopy(self.part.at[lax.rem(u, SLOTS), k, pl.ds(pl.multiple_of(off, 32), n)], self.landing(u, e, k, n),
+                     self.ssem.at[e, k, r], self.rsem.at[e, k, r], dev)
+
+    def start(self, u, e, inward=False):
         for k in range(2):
-            self.copy(u, e, k).start()
-
-    def sent(self, u, e):
+            self.copy(u, e, k, inward).start()
+
+    def sent(self, u, e, inward=False):
         for k in range(2):
-            self.copy(u, e, k).wait_send()
-
-    def add(self, u, e, off):
-        p, n = lax.rem(u, SLOTS), (128, 64, 64, 64, 32)[e]
-        land = self.lands[e]
+            self.copy(u, e, k, inward).wait_send()
+
+    def add(self, u, e, off, inward=False):
+        p, n = lax.rem(u, SLOTS), 128 if inward else (128, 64, 64, 64, 32)[e]
         for k in range(2):
-            self.copy(u, e, k).wait_recv()
-            rr = rows_at(off[k], n)
-            self.part[p, k, rr] = self.part[p, k, rr] + land[lax.rem(u, land.shape[0]), k]
+            self.copy(u, e, k, inward).wait_recv()
+            rr = pl.ds(pl.multiple_of(off[k], 32), n)
+            self.part[p, k, rr] = self.part[p, k, rr] + self.landing(u, e, k, n)[...]
 
     def advance(self, t, final):
         me = self.pl
@@ -140,20 +156,27 @@
         u3, ok3 = unit_at(t - 3 * LAG)
         u2, ok2 = unit_at(t - 2 * LAG)
         u1, ok1 = unit_at(t - LAG)
-        inner = jnp.logical_not(me.end)
-
-        @pl.when(ok5 & me.end)
+        end, inner = me.end, jnp.logical_not(me.end)
+        in5, in4, in3, in2, in1 = (is_inward(u) for u in (u5, u4, u3, u2, u1))
+
+        def out(flag):
+            return jnp.logical_not(flag)
+
+        @pl.when(ok5 & ((end & out(in5)) | (inner & in5)))
         def _():
             self.sent(u5, 4)
             self.add(u5, 4, me.own)
             final(u5)
 
-        @pl.when(ok4 & me.end)
+        @pl.when(ok4 & end & out(in4))
         def _():
             self.add(u4, 3, me.near)
+
+        @pl.when(ok4 & ((end & out(in4)) | (inner & in4)))
+        def _():
             self.start(u4, 4)
 
-        @pl.when(ok4 & inner)
+        @pl.when(ok4 & inner & out(in4))
         def _():
             self.sent(u4, 3)
 
@@ -161,36 +184,45 @@
         def _():
             self.sent(u3, 2)
             self.add(u3, 2, me.near)
+
+        @pl.when(ok3 & inner & out(in3))
+        def _():
             self.start(u3, 3)
 
+        for inward, flag2, flag1 in ((False, out(in2), out(in1)), (True, in2, in1)):
+            @pl.when(ok2 & inner & flag2)
+            def _(inward=inward):
+                self.add(u2, 1, me.keep if inward else me.far, inward)
+
+            @pl.when(ok2 & end & flag2)
+            def _(inward=inward):
+                self.sent(u2, 1, inward)
+
         @pl.when(ok2 & inner)
         def _():
-            self.add(u2, 1, me.far)
             self.start(u2, 2)
-
-        @pl.when(ok2 & me.end)
-        def _():
-            self.sent(u2, 1)
 
         @pl.when(ok1)
         def _():
             self.sent(u1, 0)
             self.add(u1, 0, me.keep)
 
-        @pl.when(ok1 & me.end)
-        def _():
-            self.start(u1, 1)
+        for inward, flag1 in ((False, out(in1)), (True, in1)):
+            @pl.when(ok1 & end & flag1)
+            def _(inward=inward):
+                self.start(u1, 1, inward)
 
 
 def scatter_scratch(slots):
     return [pltpu.VMEM((slots, 2, BLK, BLK), F32), pltpu.VMEM((4, 2, 128, BLK), F32),
-            pltpu.VMEM((6, 2, 64, BLK), F32), pltpu.VMEM((4, 2, 64, BLK), F32), pltpu.VMEM((4, 2, 32, BLK), F32),
+            pltpu.VMEM((2, 640, BLK), F32), pltpu.VMEM((4, 2, 64, BLK), F32), pltpu.VMEM((4, 2, 32, BLK), F32),
             pltpu.SemaphoreType.DMA((5, 2, RING)), pltpu.SemaphoreType.DMA((5, 2, RING))]
 
 
 class SmallReduce:
     def __init__(self, place, val, land, ssem, rsem):
-        self.pl, self.val, self.land, self.ssem, self.rsem = place, val, land, ssem, rsem
+        self.pl, self.val, self.ssem, self.rsem = place, val, ssem, rsem
+        self.land = land.at[:, :, pl.ds(0, val.shape[0])]
 
     def copies(self, ph):
         return [rcopy(self.val, self.land.at[ph, k], self.ssem.at[ph, k], self.rsem.at[ph, k], p)
@@ -203,7 +235,8 @@
     def finish(self, ph):
         for cp in self.copies(ph):
             cp.wait()
-        self.val[...] = (self.val[...] + self.land[ph, 0]) + (self.land[ph, 1] + self.land[ph, 2])
+        land = self.land
+        self.val[...] = (self.val[...] + land[ph, 0]) + (land[ph, 1] + land[ph, 2])
 
     def run(self):
         for ph in range(2):
@@ -212,8 +245,7 @@
 
 
 def small_scratch(n):
-    return [pltpu.VMEM((n, BLK), F32), pltpu.VMEM((2, 3, n, BLK), F32),
-            pltpu.SemaphoreType.DMA((2, 3)), pltpu.SemaphoreType.DMA((2, 3))]
+    return [pltpu.VMEM((n, BLK), F32), pltpu.SemaphoreType.DMA((2, 3)), pltpu.SemaphoreType.DMA((2, 3))]
 
 
 GRAM_UNITS = 18
@@ -242,15 +274,16 @@
     return jnp.where(ok, u, 0), ok
 
 
-def step_kernel(ha, hb, w1, w2, w3, g1, b1, g2, b2, g3_o, g2_o, g1_o, n1_o, h_o, ho_o, st_o,
+def step_kernel(ha, hb, w1, w2, w3, g1, b1, g2, b2, g3_o, g2_o, g1_o, n1_o, h_o, ho_o, st_o, loss_o,
                 zd, zod, dz, dzo, gw, x2h, x2o, x1h, x1o, g2v, g1v, lacc, rs, stage,
-                part, r1, r2, r3, r4, ssem, rsem, sv, sl, sa, sb, f1, fl1, fa1, fb1, f2, fl2, fa2, fb2,
-                s2, l2, sa2, sb2, s1, l1, sa1, sb1, e2, e1,
+                part, r1, r2, r3, r4, ssem, rsem, sv, sa, sb, fa1, fb1, fa2, fb2,
+                s2, sa2, sb2, s1, sa1, sb1, odd_land, even_land, e2, e1,
                 asem, bsem, lsem, psem, csem, dsem, esem, wsem):
     me = Place()
     c = me.c
     nv, da = g2v.at[pl.ds(0, ROWS)], g2v.at[pl.ds(ROWS, ROWS)]
     hv = x2o.at[:, pl.ds(0, FEAT)]
+    f1, f2 = s1, s2.at[pl.ds(0, 2 * NB)]
     gains, biases = (g1, g2), (b1, b2)
     half = pl.ds(pl.multiple_of(c * 1024, 1024), 1024)
     ohalf = pl.ds(pl.multiple_of((1 - c) * 1024, 1024), 1024)
@@ -337,7 +370,7 @@
     swap_h.start()
     keep_h.start()
     matmul(hv, w1v, da, f1)
-    SmallReduce(me, f1, fl1, fa1, fb1).run()
+    SmallReduce(me, f1, odd_land, fa1, fb1).run()
     norm(da, dzo, f1, 0)
     save_n1.start()
     keep_h.wait()
@@ -347,7 +380,7 @@
     load_w2a.wait()
     matmul(dzo, gw, nv, f2)
     load_w3a.start()
-    SmallReduce(me, f2, fl2, fa2, fb2).run()
+    SmallReduce(me, f2, even_land, fa2, fb2).run()
     norm(nv, dz, f2, 1)
     swap_x1.wait()
     swap_x2.start()
@@ -366,9 +399,9 @@
         lax.fori_loop(0, 2, step, 0)
 
     z_blocks(0)
-    red0 = SmallReduce(me, sv, sl, sa, sb)
-    red2 = SmallReduce(me, s2, l2, sa2, sb2)
-    red1 = SmallReduce(me, s1, l1, sa1, sb1)
+    red0 = SmallReduce(me, sv, odd_land, sa, sb)
+    red2 = SmallReduce(me, s2, even_land, sa2, sb2)
+    red1 = SmallReduce(me, s1, odd_land, sa1, sb1)
     sc = Scatter(me, part, (r1, r2, r3, r4), ssem, rsem)
 
     def compute(u):
@@ -418,21 +451,23 @@
 
     def keep_copy(u, k):
         own = region(u, 0, k, me.own[k], 32)
-        return pltpu.make_async_copy(stage.at[lax.rem(u, 4), k], g3_o.at[own], lsem.at[k, lax.rem(u, RING)])
-
-    def hop(e, k):
+        return pltpu.make_async_copy(stage.at[lax.rem(u, 3), k], g3_o.at[own], lsem.at[k, lax.rem(u, RING)])
+
+    def hop(e, k, inward):
+        if e == 3 and inward:
+            return me.keep[k], 128, me.p1
         return ((me.own[k], 32, me.last[k]), (me.near[k], 64, me.p1), (me.near[k], 64, me.p3),
                 (me.far[k], 64, me.p1), (me.keep[k], 128, me.first[k]))[e]
 
-    def spread(u, w, e, k):
+    def spread(u, w, e, k, inward=False):
         r = lax.rem(u, RING)
-        off, n, dev = hop(e, k)
+        off, n, dev = hop(e, k, inward)
         if w == GRAM:
             i, j = block_of(2 * u + k)
             src = dst = gw.at[rows_at(i * BLK + off, n), cols(j)]
         else:
             dst = grads[w].at[region(u, w, k, off, n)]
-            src = stage.at[lax.rem(u, 4), k] if e == 0 and w == 0 else dst
+            src = stage.at[lax.rem(u, 3), k] if e == 0 and w == 0 else dst
         g = 0 if w == GRAM else 1
         return rcopy(src, dst, asem.at[g, e, k, r], bsem.at[g, e, k, r], dev)
 
@@ -459,7 +494,7 @@
                 for k in range(2):
                     piece = part[lax.rem(u, SLOTS), k, rows_at(me.own[k], 32)]
                     if w == 0:
-                        stage[lax.rem(u, 4), k] = piece
+                        stage[lax.rem(u, 3), k] = piece
                         keep_copy(u, k).start()
                     else:
                         rr, cc = region(u, w, k, me.own[k], 32)
@@ -517,43 +552,48 @@
             return carry
         lax.fori_loop(0, NB, step, 0)
 
-    def gather_step(e, u, w):
+    def gather_step(e, u, w, inward):
         def each(f):
             for k in range(2):
                 f(k)
 
         def wait_send(k):
-            spread(u, w, e - 1, k).wait_send()
+            spread(u, w, e - 1, k, inward).wait_send()
 
         def wait_recv(k):
-            spread(u, w, e - 1, k).wait_recv()
+            spread(u, w, e - 1, k, inward).wait_recv()
 
         def begin(k):
-            spread(u, w, e, k).start()
-
-        def at_end():
+            spread(u, w, e, k, inward).start()
+
+        def run(sends, recvs, begins):
             if e == 1 and w == 0:
                 each(lambda k: keep_copy(u, k).wait())
-            if e in (1, 2, 5):
+            if e in sends:
                 each(wait_send)
-            if e in (1, 4, 5):
+            if e in recvs:
                 each(wait_recv)
-            if e in (1, 4):
+            if e in begins:
                 each(begin)
 
+        def at_end():
+            if inward:
+                run((), (4,), (4,))
+            else:
+                run((1, 2, 5), (1, 4, 5), (1, 4))
+
         def at_inner():
-            if e in (3, 4, 5):
-                each(wait_send)
-            if e in (2, 3, 5):
-                each(wait_recv)
-            if e in (2, 3, 4):
-                each(begin)
+            if inward:
+                run((1, 3, 4), (1, 3), (2, 3, 4))
+            else:
+                run((3, 4), (2, 3), (2, 3, 4))
 
         if e == 5:
             at_end()
         else:
-            pl.when(me.end)(at_end)
-            if e > 1:
+            if e == 4 or not inward:
+                pl.when(me.end)(at_end)
+            if e > 1 or inward:
                 pl.when(jnp.logical_not(me.end))(at_inner)
         if e == 5 and w < 3:
             cross(u, w).start()
@@ -587,10 +627,16 @@
 
         for e in (5, 4, 3, 2, 1):
             u, ok = unit_at(t - (5 + e) * LAG)
+            flag = is_inward(u)
             for w in range(4):
-                @pl.when(ok & of_weight(u, w))
-                def _(e=e, u=u, w=w):
-                    gather_step(e, u, w)
+                for inward in ((False,) if w == GRAM or e == 5 else (False, True)):
+                    hit = ok & of_weight(u, w)
+                    if w != GRAM and e < 5:
+                        hit = hit & (flag if inward else jnp.logical_not(flag))
+
+                    @pl.when(hit)
+                    def _(e=e, u=u, w=w, inward=inward):
+                        gather_step(e, u, w, inward)
 
         for first, red in ((2, red0), (PASS_2 + SPAN_2 - 1, red2), (PASS_1 + SPAN_1 - 1, red1)):
             @pl.when(t == first + 1)
@@ -640,8 +686,8 @@
                     lanes = slice(128 * h, 128 * h + 128)
                     r0, c0 = (j % 2) * BLK + 128 * h, (j // 2) * 128
                     g1v[r0:r0 + 128, c0:c0 + 128] = jnp.broadcast_to(mean[j:j + 1, lanes], (128, 128)).T
-                zd[ROWS:ROWS + 16, j * BLK:(j + 1) * BLK] = jnp.concatenate(
-                    [hi[j:j + 1], mid[j:j + 1], low[j:j + 1], jnp.zeros((13, BLK), BF16)], axis=0)
+                zd[ROWS:ROWS + 8, j * BLK:(j + 1) * BLK] = jnp.concatenate(
+                    [hi[j:j + 1], mid[j:j + 1], low[j:j + 1], jnp.zeros((5, BLK), BF16)], axis=0)
 
         @pl.when(t < 3)
         def _():
@@ -740,8 +786,7 @@
         st_o[1:2, lanes] = sum1[j:j + 1]
         st_o[2:3, lanes] = sum2[NB + j:NB + j + 1]
         st_o[3:4, lanes] = sum2[j:j + 1]
-    total = jnp.sum(jnp.sum(sum2[2 * NB:], axis=0, keepdims=True), axis=1, keepdims=True)
-    st_o[4:5, 0:128] = jnp.broadcast_to(total, (1, 128))
+    loss_o[0, 0] = jnp.sum(sum2[2 * NB:])
 
 
 def train_step(ha, hb, w1, w2, w3, g1, b1, g2, b2):
@@ -751,17 +796,18 @@
     return pl.pallas_call(
         step_kernel,
         out_shape=(sds((DIM, DIM), F32), sds((DIM, DIM), F32), sds((FEAT, DIM), F32), sds((ROWS, DIM), F32),
-                   sds((ROWS, 256), BF16), sds((ROWS, 256), BF16), sds((8, DIM), F32)),
+                   sds((ROWS, 256), BF16), sds((ROWS, 256), BF16), sds((4, DIM), F32), sds((1, 1), F32)),
         in_specs=[ANY] * 5 + [INV] * 4,
-        out_specs=(ANY,) * 6 + (INV,),
-        scratch_shapes=[pltpu.VMEM((ROWS + 16, DIM), BF16), act, act, act, pltpu.VMEM((DIM, DIM), BF16),
+        out_specs=(ANY,) * 6 + (INV, pl.BlockSpec(memory_space=pltpu.SMEM)),
+        scratch_shapes=[pltpu.VMEM((ROWS + 8, DIM), BF16), act, act, act, pltpu.VMEM((DIM, DIM), BF16),
                         piece, piece, piece, piece,
                         pltpu.VMEM((DIM, DIM), F32), pltpu.VMEM((FEAT, DIM), F32),
                         pltpu.VMEM((NB, BLK), F32), pltpu.VMEM((2 * NB, BLK), F32),
-                        pltpu.VMEM((4, 2, 32, BLK), F32)]
-        + scatter_scratch(SLOTS) + small_scratch(NB) + small_scratch(2 * NB) + small_scratch(2 * NB)
+                        pltpu.VMEM((3, 2, 32, BLK), F32)]
+        + scatter_scratch(SLOTS) + small_scratch(NB) + [dma((2, 3))] * 4
         + small_scratch(3 * NB) + small_scratch(2 * NB)
-        + [pltpu.VMEM((3 * NB, BLK), F32), pltpu.VMEM((2 * NB, BLK), F32),
+        + [pltpu.VMEM((2, 3, 2 * NB, BLK), F32), pltpu.VMEM((2, 3, 3 * NB, BLK), F32),
+           pltpu.VMEM((3 * NB, BLK), F32), pltpu.VMEM((2 * NB, BLK), F32),
            dma((2, 6, 2, RING)), dma((2, 6, 2, RING)), dma((2, RING)),
            dma((2, RING)), dma((10,)), dma((25,)), dma((25,)), dma((NB,))],
         compiler_params=pltpu.CompilerParams(collective_id=0, has_side_effects=True, vmem_limit_bytes=VMEM_LIMIT),
@@ -772,8 +818,8 @@
 def solution(mesh):
     def local_step(h_a, h_b, w_one, w_two, w_three, gain_one, bias_one, gain_two, bias_two):
         vecs = [v.reshape(1, DIM) for v in (gain_one, bias_one, gain_two, bias_two)]
-        d_three, d_two, d_one, _, _, _, st = train_step(h_a, h_b, w_one, w_two, w_three, *vecs)
-        return st[4, 0], d_one, d_two, d_three, st[0], st[1], st[2], st[3]
+        d_three, d_two, d_one, _, _, _, st, loss = train_step(h_a, h_b, w_one, w_two, w_three, *vecs)
+        return loss.reshape(()), d_one, d_two, d_three, st[0], st[1], st[2], st[3]
 
     row_spec = P('data', None)
     return jax.shard_map(local_step, mesh=mesh,

time: 448 us -> 442 us (0.987)
  Pallas kernels: 418 us -> 411 us
    pallas_call x1, Pallas kernels: 418 us -> 411 us  [train_step(): pl.pallas_call(step_kernel, out_shape=(sds((DIM, DIM), F32), sds((DIM, DI...]
where the time goes in v6:
time: 442 us; the launch traced here: 441 us
  Pallas kernels  411 us (93%)
  local copies, waits for them, and re-layouts  27.9 us (6%)
    pallas_call x1, Pallas kernels, train_step(): pl.pallas_call(step_kernel, out_shape=(sds((DIM, DIM), F32), sds((DIM, DI...  411 us
    unnamed x11, local copies, waits for them, and re-layouts  26.3 us

profile of v6, /device:TPU:0, one launch (start us, length us, event | category | flops | bytes accessed | tf_op | source)
XLA Modules:
  0.0 441.3 jit_solution(13862058329265248270)
XLA Ops:
  0.6 411.1 %train_step.1 = (f32[2048,2048]{1,0:T(8,128)}, f32[2048,2048]{1,0:T(8,128)}, f32[512,2048]{1,0:T(8,128)}, f32[1024,2048]{1,0:T(8,128)}, bf16[1024,256]{1,0:T(8,1...) custom-call(bf16[512,512]{1,0:T(8,128)(2,1)} %ha.1, bf16[512,512]{1,0:T(8,128)(2,1)} %hb.1, ...), custom_call_target="tpu_custom_call" | custom-call | tf_op jit(solution)/shard_map/train_step/pallas_call | solution.py:796
  411.7 1.5 fusion
  413.8 0.0 slice-start
  413.8 4.8 %copy.22 = f32[512,2048]{1,0:T(8,128)} copy(f32[512,2048]{1,0:T(8,128)} %get-tuple-element.31) | data formatting | bytes 8388608
  418.7 0.0 slice-start.1
  418.7 0.0 slice-start.2
  418.7 0.0 slice-start.3
  418.7 13.6 %copy.23 = f32[2048,2048]{1,0:T(8,128)} copy(f32[2048,2048]{1,0:T(8,128)} %get-tuple-element.32) | data formatting | bytes 33554432
  432.2 0.0 slice-done
  432.3 0.0 slice-done.1
  432.3 0.0 slice-done.2
  432.3 1.7 slice-done.3
  434.0 6.2 %copy.24 = f32[2048,2048]{1,0:T(8,128)} copy(f32[2048,2048]{1,0:T(8,128)S(1)} %bitcast.10) | data formatting | bytes 33554432
  (1 shorter events, 0.0 us)
Async XLA Ops:
  413.8 18.4 %slice-start = ((s8[16777216]{0:T(1024)(128)(4,1)}), s8[4194304]{0:T(1024)(128)(4,1)S(1)}, s32[]{:S(2)}) async-start(s8[16777216]{0:T(1024)(128)(4,1)} %bitcast.9), calls=%async_computation | async-start | bytes 8388608
  418.7 13.6 %slice-start.1 = ((s8[16777216]{0:T(1024)(128)(4,1)}), s8[4194304]{0:T(1024)(128)(4,1)S(1)}, s32[]{:S(2)}) async-start(s8[16777216]{0:T(1024)(128)(4,1)} %bitcast.9), calls=%async_computation.1 | async-start | bytes 8388608
  418.7 13.6 %slice-start.2 = ((s8[16777216]{0:T(1024)(128)(4,1)}), s8[4194304]{0:T(1024)(128)(4,1)S(1)}, s32[]{:S(2)}) async-start(s8[16777216]{0:T(1024)(128)(4,1)} %bitcast.9), calls=%async_computation.2 | async-start | bytes 8388608
  418.7 15.3 %slice-start.3 = ((s8[16777216]{0:T(1024)(128)(4,1)}), s8[4194304]{0:T(1024)(128)(4,1)S(1)}, s32[]{:S(2)}) async-start(s8[16777216]{0:T(1024)(128)(4,1)} %bitcast.9), calls=%async_computation.3 | async-start | bytes 8388608

commit v7 on v6

--- a/solution.py
+++ b/solution.py
@@ -64,11 +64,13 @@
         self.own = [n + b * 32 for n, b in zip(self.near, (y, x))]
         self.give = [n + (1 - b) * 32 for n, b in zip(self.near, (y, x))]
 
-    def barrier(self):
+    def announce(self):
         sem = pltpu.get_barrier_semaphore()
         for p in (self.pc,) + self.phases[0] + self.phases[1]:
             pl.semaphore_signal(sem, inc=1, device_id=(p,), device_id_type=MESH)
-        pl.semaphore_wait(sem, 7)
+
+    def await_all(self):
+        pl.semaphore_wait(pltpu.get_barrier_semaphore(), 7)
 
 
 def rcopy(src, dst, ssem, rsem, dev):
@@ -149,68 +151,78 @@
             rr = pl.ds(pl.multiple_of(off[k], 32), n)
             self.part[p, k, rr] = self.part[p, k, rr] + self.landing(u, e, k, n)[...]
 
-    def advance(self, t, final):
+    def step(self, e, u, gram, final):
         me = self.pl
-        u5, ok5 = unit_at(t - 5 * LAG)
-        u4, ok4 = unit_at(t - 4 * LAG)
-        u3, ok3 = unit_at(t - 3 * LAG)
-        u2, ok2 = unit_at(t - 2 * LAG)
-        u1, ok1 = unit_at(t - LAG)
-        end, inner = me.end, jnp.logical_not(me.end)
-        in5, in4, in3, in2, in1 = (is_inward(u) for u in (u5, u4, u3, u2, u1))
-
-        def out(flag):
-            return jnp.logical_not(flag)
-
-        @pl.when(ok5 & ((end & out(in5)) | (inner & in5)))
-        def _():
-            self.sent(u5, 4)
-            self.add(u5, 4, me.own)
-            final(u5)
-
-        @pl.when(ok4 & end & out(in4))
-        def _():
-            self.add(u4, 3, me.near)
-
-        @pl.when(ok4 & ((end & out(in4)) | (inner & in4)))
-        def _():
-            self.start(u4, 4)
-
-        @pl.when(ok4 & inner & out(in4))
-        def _():
-            self.sent(u4, 3)
-
-        @pl.when(ok3 & inner)
-        def _():
-            self.sent(u3, 2)
-            self.add(u3, 2, me.near)
-
-        @pl.when(ok3 & inner & out(in3))
-        def _():
-            self.start(u3, 3)
-
-        for inward, flag2, flag1 in ((False, out(in2), out(in1)), (True, in2, in1)):
-            @pl.when(ok2 & inner & flag2)
-            def _(inward=inward):
-                self.add(u2, 1, me.keep if inward else me.far, inward)
-
-            @pl.when(ok2 & end & flag2)
-            def _(inward=inward):
-                self.sent(u2, 1, inward)
-
-        @pl.when(ok2 & inner)
-        def _():
-            self.start(u2, 2)
-
-        @pl.when(ok1)
-        def _():
-            self.sent(u1, 0)
-            self.add(u1, 0, me.keep)
-
-        for inward, flag1 in ((False, out(in1)), (True, in1)):
-            @pl.when(ok1 & end & flag1)
-            def _(inward=inward):
-                self.start(u1, 1, inward)
+        if gram:
+            owner, passes = me.end, jnp.logical_not(me.end)
+        else:
+            inward = is_inward(u)
+            owner, passes = me.end != inward, jnp.logical_not(me.end) & jnp.logical_not(inward)
+        variants = (False,) if gram else (False, True)
+
+        def of(variant):
+            return me.end if gram else me.end & (inward if variant else jnp.logical_not(inward))
+
+        if e == 1:
+            self.sent(u, 0)
+            self.add(u, 0, me.keep)
+            for v in variants:
+                pl.when(of(v))(functools.partial(self.start, u, 1, v))
+        if e == 2:
+            for v in variants:
+                pl.when(of(v))(functools.partial(self.sent, u, 1, v))
+
+            @pl.when(jnp.logical_not(me.end))
+            def _():
+                for v in variants:
+                    def gather(v=v):
+                        self.add(u, 1, me.keep if v else me.far, v)
+                    if gram:
+                        gather()
+                    else:
+                        pl.when(inward if v else jnp.logical_not(inward))(gather)
+                self.start(u, 2)
+        if e == 3:
+            @pl.when(jnp.logical_not(me.end))
+            def _():
+                self.sent(u, 2)
+                self.add(u, 2, me.near)
+
+            pl.when(passes)(functools.partial(self.start, u, 3))
+        if e == 4:
+            pl.when(of(False))(functools.partial(self.add, u, 3, me.near))
+            pl.when(owner)(functools.partial(self.start, u, 4))
+            pl.when(passes)(functools.partial(self.sent, u, 3))
+        if e == 5:
+            @pl.when(owner)
+            def _():
+                self.sent(u, 4)
+                self.add(u, 4, me.own)
+                final(u)
+
+
+class Span:
+    def __init__(self, lo, hi, t):
+        self.lo, self.hi, self.t = lo, hi, t
+
+    def at(self, slot, f):
+        if self.lo <= slot < self.hi:
+            pl.when(self.t == slot)(f)
+
+    def within(self, first, stop, f):
+        if max(first, self.lo) >= min(stop, self.hi):
+            return
+        conds = ([] if first <= self.lo else [self.t >= first]) + ([] if stop >= self.hi else [self.t < stop])
+        if not conds:
+            f()
+        else:
+            pl.when(conds[0] if len(conds) == 1 else conds[0] & conds[1])(f)
+
+    def units(self, lag, f):
+        for w, first, stop, base in ((GRAM, 0, GRAM_UNITS, 0), (0, START_3, START_3 + 16, 18),
+                                     (1, START_2, START_2 + 16, 34), (2, START_2 + 16, START_2 + 20, 50)):
+            u = self.t - (lag + first - base)
+            self.within(first + lag, stop + lag, functools.partial(f, u, w))
 
 
 def scatter_scratch(slots):
@@ -255,6 +267,7 @@
 START_3 = 28
 START_2 = 44
 END = START_2 + 21 + 11 * LAG
+LOOPS = (0, 18, 39, 54, 66, END)
 DZ_SLOTS = (23, 27, 30, 32, 34, 36, 37, 38)
 PASS_2 = 39
 PASS_1 = 45
@@ -266,12 +279,6 @@
     for first in (8, 15, 21, 26, 30, 33, 35):
         i = i + jnp.where(q >= first, 1, 0)
     return i, i + q - (17 * i - i * i) // 2
-
-
-def unit_at(t):
-    u = jnp.where(t < START_3, t, jnp.where(t < START_2, t - (START_3 - 18), t - (START_2 - 34)))
-    ok = ((t >= 0) & (t < 18)) | ((t >= START_3) & (t < START_3 + 16)) | ((t >= START_2) & (t < START_2 + 20))
-    return jnp.where(ok, u, 0), ok
 
 
 def step_kernel(ha, hb, w1, w2, w3, g1, b1, g2, b2, g3_o, g2_o, g1_o, n1_o, h_o, ho_o, st_o, loss_o,
@@ -280,6 +287,7 @@
                 s2, sa2, sb2, s1, sa1, sb1, odd_land, even_land, e2, e1,
                 asem, bsem, lsem, psem, csem, dsem, esem, wsem):
     me = Place()
+    me.announce()
     c = me.c
     nv, da = g2v.at[pl.ds(0, ROWS)], g2v.at[pl.ds(ROWS, ROWS)]
     hv = x2o.at[:, pl.ds(0, FEAT)]
@@ -290,6 +298,7 @@
     hhalf = pl.ds(pl.multiple_of(c * 256, 256), 256)
     hohalf = pl.ds(pl.multiple_of((1 - c) * 256, 256), 256)
     mine = pl.ds(pl.multiple_of(c * HALF, HALF), HALF)
+    theirs = pl.ds(pl.multiple_of((1 - c) * HALF, HALF), HALF)
     body = pl.ds(0, ROWS)
     w1v = zod.at[pl.ds(0, FEAT)]
     load_w1 = pltpu.make_async_copy(w1, w1v, csem.at[0])
@@ -331,20 +340,25 @@
         def _(own=own):
             load_h(own).start()
     load_w1.start()
-    load_w2a.start()
-    me.barrier()
+    me.await_all()
     for k, other in ((0, hb), (1, ha)):
         @pl.when(c == k)
         def _(other=other):
             give_h(other).start()
+    load_w2a.start()
     lacc[...] = jnp.zeros_like(lacc)
 
-    def matmul(src, w, dst, st):
+    def matmul(src, w, dst, st, rows, add):
         def step(j, carry):
-            res = nn(src[...], w[:, cols(j)])
-            dst[:, cols(j)] = res
-            st[pl.ds(j, 1)] = jnp.sum(res, axis=0, keepdims=True)
-            st[pl.ds(NB + j, 1)] = jnp.sum(res * res, axis=0, keepdims=True)
+            res = nn(src[rows, :], w[:, cols(j)])
+            dst[rows, cols(j)] = res
+            one = jnp.sum(res, axis=0, keepdims=True)
+            two = jnp.sum(res * res, axis=0, keepdims=True)
+            if add:
+                one = one + st[pl.ds(j, 1)]
+                two = two + st[pl.ds(NB + j, 1)]
+            st[pl.ds(j, 1)] = one
+            st[pl.ds(NB + j, 1)] = two
             return carry
         lax.fori_loop(0, NB, step, 0)
 
@@ -366,10 +380,11 @@
 
     load_w1.wait()
     load_h(ha).wait()
+    matmul(hv, w1v, da, f1, mine, False)
     give_h(ha).wait()
     swap_h.start()
     keep_h.start()
-    matmul(hv, w1v, da, f1)
+    matmul(hv, w1v, da, f1, theirs, True)
     SmallReduce(me, f1, odd_land, fa1, fb1).run()
     norm(da, dzo, f1, 0)
     save_n1.start()
@@ -378,7 +393,7 @@
     swap_x1.start()
     keep_x1.start()
     load_w2a.wait()
-    matmul(dzo, gw, nv, f2)
+    matmul(dzo, gw, nv, f2, body, False)
     load_w3a.start()
     SmallReduce(me, f2, even_land, fa2, fb2).run()
     norm(nv, dz, f2, 1)
@@ -404,40 +419,30 @@
     red1 = SmallReduce(me, s1, odd_land, sa1, sb1)
     sc = Scatter(me, part, (r1, r2, r3, r4), ssem, rsem)
 
-    def compute(u):
+    def compute(u, w):
         p = lax.rem(u, SLOTS)
-
-        @pl.when(u < GRAM_UNITS)
-        def _():
+        if w == GRAM:
             for k in range(2):
                 i, j = block_of(2 * u + k)
                 part[p, k] = tn(zd[0:ROWS, cols(i)], zd[0:ROWS, cols(j)])
-
-        w, q = grad_unit(u)
-        for w_, la, lb, ra, rb in ((0, x2h, x2o, dz, dzo), (1, x1h, x1o, zd, zod)):
-            @pl.when((u >= GRAM_UNITS) & (w == w_))
-            def _(la=la, lb=lb, ra=ra, rb=rb):
-                lc = pl.ds(pl.multiple_of(lax.rem(q, 2) * 512, 512), 512)
-                rc = cols(q // 2)
-                res = tn(la[:, lc], ra[0:ROWS, rc]) + tn(lb[:, lc], rb[:, rc])
-                part[p, 0] = res[0:BLK]
-                part[p, 1] = res[BLK:2 * BLK]
-
-        @pl.when((u >= GRAM_UNITS) & (w == 2))
-        def _():
+            return
+        q = grad_unit(u)[1]
+        if w == 2:
             rc = pl.ds(pl.multiple_of(q * 512, 512), 512)
             res = tn(hh[...], dz[:, rc]) + tn(ho[...], dzo[:, rc])
             part[p, 0] = res[:, 0:BLK]
             part[p, 1] = res[:, BLK:2 * BLK]
+            return
+        la, lb, ra, rb = ((x2h, x2o, dz, dzo), (x1h, x1o, zd, zod))[w]
+        lc = pl.ds(pl.multiple_of(lax.rem(q, 2) * 512, 512), 512)
+        rc = cols(q // 2)
+        res = tn(la[:, lc], ra[0:ROWS, rc]) + tn(lb[:, lc], rb[:, rc])
+        part[p, 0] = res[0:BLK]
+        part[p, 1] = res[BLK:2 * BLK]
 
     def grad_unit(u):
         v = jnp.maximum(u - GRAM_UNITS, 0)
         return v // 16, lax.rem(v, 16)
-
-    def of_weight(u, w):
-        if w == GRAM:
-            return u < GRAM_UNITS
-        return (u >= GRAM_UNITS) & (grad_unit(u)[0] == w)
 
     def region(u, w, k, off, n):
         q = grad_unit(u)[1]
@@ -487,40 +492,36 @@
         out = (None, g2_o, g1_o)[w]
         return pltpu.make_async_copy(grads[w].at[reg], out.at[reg], psem.at[0 if own else 1, lax.rem(u, RING)])
 
-    def final(u):
-        for w in range(3):
-            @pl.when(of_weight(u, w))
-            def _(w=w):
-                for k in range(2):
-                    piece = part[lax.rem(u, SLOTS), k, rows_at(me.own[k], 32)]
-                    if w == 0:
-                        stage[lax.rem(u, 3), k] = piece
-                        keep_copy(u, k).start()
-                    else:
-                        rr, cc = region(u, w, k, me.own[k], 32)
-                        grads[w][rr, cc] = piece
-                    spread(u, w, 0, k).start()
-
-        @pl.when(u < GRAM_UNITS)
-        def _():
+    def final(u, w):
+        if w < 3:
             for k in range(2):
-                i, j = block_of(2 * u + k)
-                own = rows_at(me.own[k], 32)
-                row0 = rows_at(i * BLK + me.own[k], 32)
-                mu_r = g1v[rows_at(lax.rem(i, 2) * BLK + me.own[k], 32), lanes_at((i // 2) * 128)]
-                mu_c = sv[pl.ds(j, 1)]
-                mm = ALL_ROWS * jnp.concatenate([mu_r, mu_r], axis=1) * mu_c
-                cov = (part[lax.rem(u, SLOTS), k, own] - mm) * (1.0 / (ALL_ROWS - 1))
-                row = lax.broadcasted_iota(jnp.int32, (32, BLK), 0) + (i * BLK + me.own[k])
-                col = lax.broadcasted_iota(jnp.int32, (32, BLK), 1) + j * BLK
-                diag = row == col
-                std = jnp.sqrt(jnp.where(diag, cov, 1.0) + STD_EPS)
-                hinge = jnp.where(std < 1.0, VAR_WEIGHT / (2.0 * std), 0.0)
-                weight = jnp.where(i == j, COV_WEIGHT, 2.0 * COV_WEIGHT)
-                term = jnp.where(diag, VAR_WEIGHT * jnp.maximum(1.0 - std, 0.0), weight * cov * cov)
-                lacc[...] = lacc[...] + ((term[0:8] + term[8:16]) + (term[16:24] + term[24:32]))
-                gw[row0, cols(j)] = jnp.where(diag, -hinge, (2.0 * COV_WEIGHT) * cov).astype(BF16)
-                spread(u, GRAM, 0, k).start()
+                piece = part[lax.rem(u, SLOTS), k, rows_at(me.own[k], 32)]
+                if w == 0:
+                    stage[lax.rem(u, 3), k] = piece
+                    keep_copy(u, k).start()
+                else:
+                    rr, cc = region(u, w, k, me.own[k], 32)
+                    grads[w][rr, cc] = piece
+                spread(u, w, 0, k).start()
+            return
+        for k in range(2):
+            i, j = block_of(2 * u + k)
+            own = rows_at(me.own[k], 32)
+            row0 = rows_at(i * BLK + me.own[k], 32)
+            mu_r = g1v[rows_at(lax.rem(i, 2) * BLK + me.own[k], 32), lanes_at((i // 2) * 128)]
+            mu_c = sv[pl.ds(j, 1)]
+            mm = ALL_ROWS * jnp.concatenate([mu_r, mu_r], axis=1) * mu_c
+            cov = (part[lax.rem(u, SLOTS), k, own] - mm) * (1.0 / (ALL_ROWS - 1))
+            row = lax.broadcasted_iota(jnp.int32, (32, BLK), 0) + (i * BLK + me.own[k])
+            col = lax.broadcasted_iota(jnp.int32, (32, BLK), 1) + j * BLK
+            diag = row == col
+            std = jnp.sqrt(jnp.where(diag, cov, 1.0) + STD_EPS)
+            hinge = jnp.where(std < 1.0, VAR_WEIGHT / (2.0 * std), 0.0)
+            weight = jnp.where(i == j, COV_WEIGHT, 2.0 * COV_WEIGHT)
+            term = jnp.where(diag, VAR_WEIGHT * jnp.maximum(1.0 - std, 0.0), weight * cov * cov)
+            lacc[...] = lacc[...] + ((term[0:8] + term[8:16]) + (term[16:24] + term[24:32]))
+            gw[row0, cols(j)] = jnp.where(diag, -hinge, (2.0 * COV_WEIGHT) * cov).astype(BF16)
+            spread(u, GRAM, 0, k).start()
 
     def diff_block(j):
         diff = zd[0:ROWS, cols(j)].astype(F32) - zod[:, cols(j)].astype(F32)
@@ -607,93 +608,86 @@
                 def _():
                     gw[rows_at(j * BLK, BLK), cols(i)] = gw[rows_at(i * BLK, BLK), cols(j)].T
 
-    compute(jnp.int32(0))
-
-    def slot(t, carry):
-        u, ok = unit_at(t - 11 * LAG - 1)
-        for w in (1, 2):
-            @pl.when(ok & of_weight(u, w))
-            def _(u=u, w=w):
-                put(u, w, False).wait()
-
-        u, ok = unit_at(t - 11 * LAG)
-        for w in range(3):
-            @pl.when(ok & of_weight(u, w))
-            def _(u=u, w=w):
-                cross(u, w).wait()
-                if w > 0:
-                    put(u, w, True).wait()
-                    put(u, w, False).start()
-
+    compute(jnp.int32(0), GRAM)
+
+    def gather(e, u, w):
+        if w == GRAM or e == 5:
+            gather_step(e, u, w, False)
+            return
+        inward = is_inward(u)
+        pl.when(jnp.logical_not(inward))(lambda: gather_step(e, u, w, False))
+        pl.when(inward)(lambda: gather_step(e, u, w, True))
+
+    def put_end(u, w):
+        if w in (1, 2):
+            put(u, w, False).wait()
+
+    def cross_end(u, w):
+        if w < 3:
+            cross(u, w).wait()
+        if w in (1, 2):
+            put(u, w, True).wait()
+            put(u, w, False).start()
+
+    def means():
+        mean = sv[...] * (1.0 / ALL_ROWS)
+        sv[...] = mean
+        hi = mean.astype(BF16)
+        mid = (mean - hi.astype(F32)).astype(BF16)
+        low = (mean - hi.astype(F32) - mid.astype(F32)).astype(BF16)
+        for j in range(NB):
+            for h in range(2):
+                lanes = slice(128 * h, 128 * h + 128)
+                r0, c0 = (j % 2) * BLK + 128 * h, (j // 2) * 128
+                g1v[r0:r0 + 128, c0:c0 + 128] = jnp.broadcast_to(mean[j:j + 1, lanes], (128, 128)).T
+            zd[ROWS:ROWS + 8, j * BLK:(j + 1) * BLK] = jnp.concatenate(
+                [hi[j:j + 1], mid[j:j + 1], low[j:j + 1], jnp.zeros((5, BLK), BF16)], axis=0)
+
+    def slots(lo, hi):
+        def slot(t, carry):
+            run_slot(Span(lo, hi, t), t)
+            return carry
+        lax.fori_loop(lo, hi, slot, 0)
+
+    def run_slot(span, t):
+        span.units(11 * LAG + 1, put_end)
+        span.units(11 * LAG, cross_end)
         for e in (5, 4, 3, 2, 1):
-            u, ok = unit_at(t - (5 + e) * LAG)
-            flag = is_inward(u)
-            for w in range(4):
-                for inward in ((False,) if w == GRAM or e == 5 else (False, True)):
-                    hit = ok & of_weight(u, w)
-                    if w != GRAM and e < 5:
-                        hit = hit & (flag if inward else jnp.logical_not(flag))
-
-                    @pl.when(hit)
-                    def _(e=e, u=u, w=w, inward=inward):
-                        gather_step(e, u, w, inward)
-
-        for first, red in ((2, red0), (PASS_2 + SPAN_2 - 1, red2), (PASS_1 + SPAN_1 - 1, red1)):
-            @pl.when(t == first + 1)
+            span.units((5 + e) * LAG, functools.partial(gather, e))
+        reds = ((2, red0), (PASS_2 + SPAN_2 - 1, red2), (PASS_1 + SPAN_1 - 1, red1))
+        for first, red in reds:
+            @functools.partial(span.at, first + 1)
             def _(red=red):
                 red.finish(0)
                 red.start(1)
 
-            @pl.when(t == first + 2)
+            @functools.partial(span.at, first + 2)
             def _(red=red):
                 red.finish(1)
 
-        for first, st, layer, dst in ((PASS_2 + SPAN_2 + 1, s2, 1, zd), (PASS_1 + SPAN_1 + 1, s1, 0, dz)):
-            @pl.when(t == first)
-            def _(st=st, layer=layer, dst=dst):
-                back_pre(dst, st, layer, (lambda j: swap_du2(j).start()) if layer == 1 else (lambda j: None))
-
-        @pl.when(t == PASS_2 + SPAN_2)
+        @functools.partial(span.at, PASS_2 + SPAN_2)
         def _():
             load_w2.start()
 
-        @pl.when(t == PASS_2 + SPAN_2 + 1)
-        def _():
+        @functools.partial(span.at, PASS_2 + SPAN_2 + 1)
+        def _():
+            back_pre(zd, s2, 1, lambda j: swap_du2(j).start())
             load_n1.start()
             swap_s2.start()
 
-        @pl.when(t == PASS_1 + SPAN_1 + 1)
-        def _():
+        @functools.partial(span.at, PASS_1 + SPAN_1 + 1)
+        def _():
+            back_pre(dz, s1, 0, lambda j: None)
             swap_du1.start()
             swap_s1.start()
 
-        sc.advance(t, final)
-        u, ok = unit_at(t)
-
-        @pl.when(ok)
-        def _(u=u):
-            sc.start(u, 0)
-
-        @pl.when(t == 4)
-        def _():
-            mean = sv[...] * (1.0 / ALL_ROWS)
-            sv[...] = mean
-            hi = mean.astype(BF16)
-            mid = (mean - hi.astype(F32)).astype(BF16)
-            low = (mean - hi.astype(F32) - mid.astype(F32)).astype(BF16)
-            for j in range(NB):
-                for h in range(2):
-                    lanes = slice(128 * h, 128 * h + 128)
-                    r0, c0 = (j % 2) * BLK + 128 * h, (j // 2) * 128
-                    g1v[r0:r0 + 128, c0:c0 + 128] = jnp.broadcast_to(mean[j:j + 1, lanes], (128, 128)).T
-                zd[ROWS:ROWS + 8, j * BLK:(j + 1) * BLK] = jnp.concatenate(
-                    [hi[j:j + 1], mid[j:j + 1], low[j:j + 1], jnp.zeros((5, BLK), BF16)], axis=0)
-
-        @pl.when(t < 3)
-        def _():
-            z_blocks(2 * t + 2)
-
-        @pl.when(t == 3)
+        for e in (5, 4, 3, 2, 1):
+            span.units(e * LAG, lambda u, w, e=e: sc.step(e, u, w == GRAM, lambda v: final(v, w)))
+        span.units(0, lambda u, w: sc.start(u, 0))
+        span.at(4, means)
+        span.within(0, 3, lambda: z_blocks(2 * t + 2))
+
+        @functools.partial(span.at, 3)
         def _():
             keep_x1.wait()
             keep_x2.wait()
@@ -701,62 +695,56 @@
             save_n1.wait()
             swap_z.start()
 
-        @pl.when(t == 7)
-        def _():
-            swap_z.wait()
-
-        @pl.when((t >= 8) & (t < 8 + NB))
-        def _():
-            diff_block(t - 8)
-
+        span.at(7, swap_z.wait)
+        span.within(8, 8 + NB, lambda: diff_block(t - 8))
         for j, first in enumerate(DZ_SLOTS):
-            @pl.when(t == first + 1)
-            def _(j=j):
-                swap_dz(j).wait()
-
+            span.at(first + 1, lambda j=j: swap_dz(j).wait())
         mine_now = jnp.int32(-1)
         for j, first in enumerate(DZ_SLOTS):
-            mine_now = jnp.where(t == first, j, mine_now)
-
-        @pl.when(mine_now >= 0)
-        def _():
-            dz_block(mine_now)
-            swap_dz(mine_now).start()
-
-        @pl.when(t == DZ_SLOTS[-1])
+            if span.lo <= first < span.hi:
+                mine_now = jnp.where(t == first, j, mine_now)
+        if any(span.lo <= first < span.hi for first in DZ_SLOTS):
+            @pl.when(mine_now >= 0)
+            def _():
+                dz_block(mine_now)
+                swap_dz(mine_now).start()
+
+        @functools.partial(span.at, DZ_SLOTS[-1])
         def _():
             for j in range(NB):
                 load_w3(j).start()
 
-        @pl.when(t == PASS_2)
+        @functools.partial(span.at, PASS_2)
         def _():
             s2[2 * NB:3 * NB] = lacc[...]
 
-        @pl.when(t == PASS_1)
+        @functools.partial(span.at, PASS_1)
         def _():
             load_w2.wait()
             load_n1.wait()
 
-        block = (t - (START_2 - 1)) // 2
-
-        @pl.when((t >= START_2 - 1) & (t < START_2 + 15) & (t == START_2 - 1 + 2 * block))
-        def _():
-            swap_du2(block).wait()
-
-        @pl.when(t == START_2 + 8)
+        @functools.partial(span.within, START_2 - 1, START_2 + 15)
+        def _():
+            block = (t - (START_2 - 1)) // 2
+
+            @pl.when(t == START_2 - 1 + 2 * block)
+            def _():
+                swap_du2(block).wait()
+
+        @functools.partial(span.at, START_2 + 8)
         def _():
             for cp in load_h2:
                 cp.start()
 
-        @pl.when(t == START_2 + 14)
+        @functools.partial(span.at, START_2 + 14)
         def _():
             swap_du1.wait()
             for cp in load_h2:
                 cp.wait()
 
-        for first, span, grad, st, layer in ((PASS_2, SPAN_2, dz, s2, 1), (PASS_1, SPAN_1, zd, s1, 0)):
-            @pl.when((t >= first) & (t < first + span))
-            def _(first=first, n=-(-NB // span), grad=grad, st=st, layer=layer):
+        for first, width, grad, st, layer in ((PASS_2, SPAN_2, dz, s2, 1), (PASS_1, SPAN_1, zd, s1, 0)):
+            @functools.partial(span.within, first, first + width)
+            def _(first=first, n=-(-NB // width), grad=grad, st=st, layer=layer):
                 def step(j, carry):
                     if layer == 1:
                         load_w3(j).wait()
@@ -765,18 +753,12 @@
                 lo = n * (t - first)
                 lax.fori_loop(lo, jnp.minimum(lo + n, NB), step, 0)
 
-        for last, red in ((2, red0), (PASS_2 + SPAN_2 - 1, red2), (PASS_1 + SPAN_1 - 1, red1)):
-            @pl.when(t == last)
-            def _(red=red):
-                red.start(0)
-
-        u, ok = unit_at(t + 1)
-
-        @pl.when(ok)
-        def _(u=u):
-            compute(u)
-        return carry
-    lax.fori_loop(0, END, slot, 0)
+        for last, red in reds:
+            span.at(last, lambda red=red: red.start(0))
+        span.units(-1, compute)
+
+    for lo, hi in zip(LOOPS, LOOPS[1:]):
+        slots(lo, hi)
     swap_s2.wait()
     swap_s1.wait()
     sum2, sum1 = s2[...] + e2[...], s1[...] + e1[...]

time: 442 us -> 436 us (0.986)
  Pallas kernels: 411 us -> 405 us
    pallas_call x1, Pallas kernels: 411 us -> 405 us  [train_step(): pl.pallas_call(step_kernel, out_shape=(sds((DIM, DIM), F32), sds((DIM, DI...]
where the time goes in v7:
time: 436 us; the launch traced here: 435 us
  Pallas kernels  405 us (93%)
  local copies, waits for them, and re-layouts  27.9 us (6%)
    pallas_call x1, Pallas kernels, train_step(): pl.pallas_call(step_kernel, out_shape=(sds((DIM, DIM), F32), sds((DIM, DI...  405 us
    unnamed x11, local copies, waits for them, and re-layouts  26.3 us

profile of v7, /device:TPU:0, one launch (start us, length us, event | category | flops | bytes accessed | tf_op | source)
XLA Modules:
  0.0 435.3 jit_solution(13607164726559725496)
XLA Ops:
  0.6 405.1 %train_step.1 = (f32[2048,2048]{1,0:T(8,128)}, f32[2048,2048]{1,0:T(8,128)}, f32[512,2048]{1,0:T(8,128)}, f32[1024,2048]{1,0:T(8,128)}, bf16[1024,256]{1,0:T(8,1...) custom-call(bf16[512,512]{1,0:T(8,128)(2,1)} %ha.1, bf16[512,512]{1,0:T(8,128)(2,1)} %hb.1, ...), custom_call_target="tpu_custom_call" | custom-call | tf_op jit(solution)/shard_map/train_step/pallas_call | solution.py:778
  405.7 1.5 fusion
  407.8 0.0 slice-start
  407.9 4.8 %copy.22 = f32[512,2048]{1,0:T(8,128)} copy(f32[512,2048]{1,0:T(8,128)} %get-tuple-element.31) | data formatting | bytes 8388608
  412.7 0.0 slice-start.1
  412.7 0.0 slice-start.2
  412.7 0.0 slice-start.3
  412.7 13.6 %copy.23 = f32[2048,2048]{1,0:T(8,128)} copy(f32[2048,2048]{1,0:T(8,128)} %get-tuple-element.32) | data formatting | bytes 33554432
  426.3 0.0 slice-done
  426.3 0.0 slice-done.1
  426.3 0.0 slice-done.2
  426.3 1.7 slice-done.3
  428.0 6.2 %copy.24 = f32[2048,2048]{1,0:T(8,128)} copy(f32[2048,2048]{1,0:T(8,128)S(1)} %bitcast.10) | data formatting | bytes 33554432
  (1 shorter events, 0.0 us)
Async XLA Ops:
  407.8 18.4 %slice-start = ((s8[16777216]{0:T(1024)(128)(4,1)}), s8[4194304]{0:T(1024)(128)(4,1)S(1)}, s32[]{:S(2)}) async-start(s8[16777216]{0:T(1024)(128)(4,1)} %bitcast.9), calls=%async_computation | async-start | bytes 8388608
  412.7 13.6 %slice-start.1 = ((s8[16777216]{0:T(1024)(128)(4,1)}), s8[4194304]{0:T(1024)(128)(4,1)S(1)}, s32[]{:S(2)}) async-start(s8[16777216]{0:T(1024)(128)(4,1)} %bitcast.9), calls=%async_computation.1 | async-start | bytes 8388608
  412.7 13.6 %slice-start.2 = ((s8[16777216]{0:T(1024)(128)(4,1)}), s8[4194304]{0:T(1024)(128)(4,1)S(1)}, s32[]{:S(2)}) async-start(s8[16777216]{0:T(1024)(128)(4,1)} %bitcast.9), calls=%async_computation.2 | async-start | bytes 8388608
  412.7 15.3 %slice-start.3 = ((s8[16777216]{0:T(1024)(128)(4,1)}), s8[4194304]{0:T(1024)(128)(4,1)S(1)}, s32[]{:S(2)}) async-start(s8[16777216]{0:T(1024)(128)(4,1)} %bitcast.9), calls=%async_computation.3 | async-start | bytes 8388608

commit v8 on v7

--- a/solution.py
+++ b/solution.py
@@ -681,22 +681,6 @@
             swap_du1.start()
             swap_s1.start()
 
-        for e in (5, 4, 3, 2, 1):
-            span.units(e * LAG, lambda u, w, e=e: sc.step(e, u, w == GRAM, lambda v: final(v, w)))
-        span.units(0, lambda u, w: sc.start(u, 0))
-        span.at(4, means)
-        span.within(0, 3, lambda: z_blocks(2 * t + 2))
-
-        @functools.partial(span.at, 3)
-        def _():
-            keep_x1.wait()
-            keep_x2.wait()
-            swap_x2.wait()
-            save_n1.wait()
-            swap_z.start()
-
-        span.at(7, swap_z.wait)
-        span.within(8, 8 + NB, lambda: diff_block(t - 8))
         for j, first in enumerate(DZ_SLOTS):
             span.at(first + 1, lambda j=j: swap_dz(j).wait())
         mine_now = jnp.int32(-1)
@@ -714,6 +698,22 @@
             for j in range(NB):
                 load_w3(j).start()
 
+        for e in (5, 4, 3, 2, 1):
+            span.units(e * LAG, lambda u, w, e=e: sc.step(e, u, w == GRAM, lambda v: final(v, w)))
+        span.units(0, lambda u, w: sc.start(u, 0))
+        span.at(4, means)
+        span.within(0, 3, lambda: z_blocks(2 * t + 2))
+
+        @functools.partial(span.at, 3)
+        def _():
+            keep_x1.wait()
+            keep_x2.wait()
+            swap_x2.wait()
+            save_n1.wait()
+            swap_z.start()
+
+        span.at(7, swap_z.wait)
+        span.within(8, 8 + NB, lambda: diff_block(t - 8))
         @functools.partial(span.at, PASS_2)
         def _():
             s2[2 * NB:3 * NB] = lacc[...]
@@ -797,11 +797,61 @@
     )(ha, hb, w1, w2, w3, g1, b1, g2, b2)
 
 
+CHUNK = 128
+BUFS = 8
+
+
+def finish_kernel(g3, g2, g1, st, loss, o3, o2, o1, gain1, bias1, gain2, bias2, loss_o, buf, isem, osem, rsem):
+    jobs = [(src, dst, r) for src, dst, n in ((g3, o3, DIM), (g2, o2, DIM), (g1, o1, FEAT)) for r in range(0, n, CHUNK)]
+
+    def take(i):
+        src, _, r = jobs[i]
+        return pltpu.make_async_copy(src.at[pl.ds(r, CHUNK)], buf.at[i % BUFS], isem.at[i % BUFS])
+
+    def give(i):
+        _, dst, r = jobs[i]
+        return pltpu.make_async_copy(buf.at[i % BUFS], dst.at[pl.ds(r, CHUNK)], osem.at[i % BUFS])
+
+    for i in range(BUFS - 1):
+        take(i).start()
+    rows = [pltpu.make_async_copy(st.at[pl.ds(row, 1)], out, rsem.at[row])
+            for row, out in enumerate((gain1, bias1, gain2, bias2))]
+    for cp in rows:
+        cp.start()
+    loss_o[0, 0] = loss[0, 0]
+    for i in range(len(jobs)):
+        take(i).wait()
+        give(i).start()
+        if i + BUFS - 1 < len(jobs):
+            if i > 0:
+                give(i - 1).wait()
+            take(i + BUFS - 1).start()
+    for i in range(len(jobs) - BUFS, len(jobs)):
+        give(i).wait()
+    for cp in rows:
+        cp.wait()
+
+
+def finish(g3, g2, g1, st, loss):
+    smem = pl.BlockSpec(memory_space=pltpu.SMEM)
+    dma = pltpu.SemaphoreType.DMA
+    return pl.pallas_call(
+        finish_kernel,
+        out_shape=(sds((DIM, DIM), F32), sds((DIM, DIM), F32), sds((FEAT, DIM), F32)) + (sds((1, DIM), F32),) * 4
+        + (sds((1, 1), F32),),
+        in_specs=[ANY] * 4 + [smem],
+        out_specs=(ANY,) * 7 + (smem,),
+        scratch_shapes=[pltpu.VMEM((BUFS, CHUNK, DIM), F32), dma((BUFS,)), dma((BUFS,)), dma((4,))],
+        name='finish',
+    )(g3, g2, g1, st, loss)
+
+
 def solution(mesh):
     def local_step(h_a, h_b, w_one, w_two, w_three, gain_one, bias_one, gain_two, bias_two):
         vecs = [v.reshape(1, DIM) for v in (gain_one, bias_one, gain_two, bias_two)]
-        d_three, d_two, d_one, _, _, _, st, loss = train_step(h_a, h_b, w_one, w_two, w_three, *vecs)
-        return loss.reshape(()), d_one, d_two, d_three, st[0], st[1], st[2], st[3]
+        g_three, g_two, g_one, _, _, _, st, part_loss = train_step(h_a, h_b, w_one, w_two, w_three, *vecs)
+        d_three, d_two, d_one, *small, loss = finish(g_three, g_two, g_one, st, part_loss)
+        return (loss.reshape(()), d_one, d_two, d_three, *[v.reshape(DIM) for v in small])
 
     row_spec = P('data', None)
     return jax.shard_map(local_step, mesh=mesh,

time: 436 us -> 431 us (0.989)
  local copies, waits for them, and re-layouts: 27.9 us -> 0 us
  Pallas kernels: 405 us -> 430 us
    unnamed x11 -> x0, local copies, waits for them, and re-layouts: 26.3 us -> none
    pallas_call x0 -> x1, Pallas kernels: none -> 26.1 us  [finish(): pl.pallas_call(finish_kernel, out_shape=(sds((DIM, DIM), F32), sds((DIM,...]
where the time goes in v8:
time: 431 us; the launch traced here: 430 us
  Pallas kernels  430 us (100%)
    pallas_call x1, Pallas kernels, train_step(): pl.pallas_call(step_kernel, out_shape=(sds((DIM, DIM), F32), sds((DIM, DI...  404 us
    pallas_call x1, Pallas kernels, finish(): pl.pallas_call(finish_kernel, out_shape=(sds((DIM, DIM), F32), sds((DIM,...  26.1 us

profile of v8, /device:TPU:0, one launch (start us, length us, event | category | flops | bytes accessed | tf_op | source)
XLA Modules:
  0.0 430.5 jit_solution(12054283126299452686)
XLA Ops:
  0.6 403.6 %train_step.1 = (f32[2048,2048]{1,0:T(8,128)}, f32[2048,2048]{1,0:T(8,128)}, f32[512,2048]{1,0:T(8,128)}, f32[1024,2048]{1,0:T(8,128)}, bf16[1024,256]{1,0:T(8,1...) custom-call(bf16[512,512]{1,0:T(8,128)(2,1)} %ha.1, bf16[512,512]{1,0:T(8,128)(2,1)} %hb.1, ...), custom_call_target="tpu_custom_call" | custom-call | tf_op jit(solution)/shard_map/train_step/pallas_call | solution.py:778
  404.2 26.1 %finish.1 = (f32[2048,2048]{1,0:T(8,128)}, f32[2048,2048]{1,0:T(8,128)}, f32[512,2048]{1,0:T(8,128)}, f32[1,2048]{1,0:T(1,128)}, f32[1,2048]{1,0:T(1,128)}, /*in...) custom-call(f32[2048,2048]{1,0:T(8,128)} %get-tuple-element.21.g3, f32[2048,2048]{1,0:T(8,128)} %get-tuple-element.22.g2, ...), custom_call_target="tpu_custom_call" | custom-call | tf_op jit(solution)/shard_map/finish/pallas_call | solution.py:838

commit v9 on v8

--- a/solution.py
+++ b/solution.py
@@ -232,9 +232,9 @@
 
 
 class SmallReduce:
-    def __init__(self, place, val, land, ssem, rsem):
+    def __init__(self, place, val, land, ssem, rsem, row=0):
         self.pl, self.val, self.ssem, self.rsem = place, val, ssem, rsem
-        self.land = land.at[:, :, pl.ds(0, val.shape[0])]
+        self.land = land.at[:, :, pl.ds(row, val.shape[0])]
 
     def copies(self, ph):
         return [rcopy(self.val, self.land.at[ph, k], self.ssem.at[ph, k], self.rsem.at[ph, k], p)
@@ -249,11 +249,6 @@
             cp.wait()
         land = self.land
         self.val[...] = (self.val[...] + land[ph, 0]) + (land[ph, 1] + land[ph, 2])
-
-    def run(self):
-        for ph in range(2):
-            self.start(ph)
-            self.finish(ph)
 
 
 def small_scratch(n):
@@ -291,7 +286,7 @@
     c = me.c
     nv, da = g2v.at[pl.ds(0, ROWS)], g2v.at[pl.ds(ROWS, ROWS)]
     hv = x2o.at[:, pl.ds(0, FEAT)]
-    f1, f2 = s1, s2.at[pl.ds(0, 2 * NB)]
+    f1, f2 = [[st.at[pl.ds(h * NB, NB)] for h in range(2)] for st in (s1, s2)]
     gains, biases = (g1, g2), (b1, b2)
     half = pl.ds(pl.multiple_of(c * 1024, 1024), 1024)
     ohalf = pl.ds(pl.multiple_of((1 - c) * 1024, 1024), 1024)
@@ -303,7 +298,8 @@
     w1v = zod.at[pl.ds(0, FEAT)]
     load_w1 = pltpu.make_async_copy(w1, w1v, csem.at[0])
     load_w2a = pltpu.make_async_copy(w2, gw, csem.at[1])
-    load_w3a = pltpu.make_async_copy(w3, gw, csem.at[2])
+    load_w3a = [pltpu.make_async_copy(w3.at[pl.ds(r, 1024)], gw.at[pl.ds(r, 1024)], csem.at[k])
+                for r, k in ((0, 2), (1024, 4))]
     load_w2 = pltpu.make_async_copy(w2, gw, csem.at[6])
     load_n1 = pltpu.make_async_copy(n1_o, nv, csem.at[7])
     save_n1 = pltpu.make_async_copy(da, n1_o, csem.at[8])
@@ -311,7 +307,7 @@
     keep_h = pltpu.make_async_copy(hv.at[:, hhalf], h_o, csem.at[5])
     hh, ho = x2h.at[:, pl.ds(0, 256)], x2o.at[:, pl.ds(0, 256)]
     load_h2 = [pltpu.make_async_copy(h_o, hh, csem.at[5]), pltpu.make_async_copy(ho_o, ho, csem.at[2])]
-    keep_x2 = pltpu.make_async_copy(dz.at[:, half], x2h, csem.at[4])
+    keep_x2 = pltpu.make_async_copy(dz.at[:, half], x2h, csem.at[10])
     swap_z = rcopy(zd.at[body], zod, dsem.at[0], esem.at[0], me.pc)
     swap_x2 = rcopy(dz.at[:, ohalf], x2o, dsem.at[1], esem.at[1], me.pc)
     swap_x1 = rcopy(dzo.at[:, ohalf], x1o, dsem.at[2], esem.at[2], me.pc)
@@ -348,72 +344,105 @@
     load_w2a.start()
     lacc[...] = jnp.zeros_like(lacc)
 
-    def matmul(src, w, dst, st, rows, add):
+    def matmul(src, w, dst, rows, depth, first, stop, st=None, add=False):
         def step(j, carry):
-            res = nn(src[rows, :], w[:, cols(j)])
+            res = nn(src[rows, depth], w[depth, cols(j)])
+            if add == 'depth':
+                res = res + dst[rows, cols(j)]
             dst[rows, cols(j)] = res
-            one = jnp.sum(res, axis=0, keepdims=True)
-            two = jnp.sum(res * res, axis=0, keepdims=True)
-            if add:
-                one = one + st[pl.ds(j, 1)]
-                two = two + st[pl.ds(NB + j, 1)]
-            st[pl.ds(j, 1)] = one
-            st[pl.ds(NB + j, 1)] = two
+            if st is not None:
+                one = jnp.sum(res, axis=0, keepdims=True)
+                two = jnp.sum(res * res, axis=0, keepdims=True)
+                k = lax.rem(j, 4)
+                if add == 'rows':
+                    one = one + st[pl.ds(k, 1)]
+                    two = two + st[pl.ds(4 + k, 1)]
+                st[pl.ds(k, 1)] = one
+                st[pl.ds(4 + k, 1)] = two
             return carry
-        lax.fori_loop(0, NB, step, 0)
-
-    def norm(u, x, st, layer):
-        mean = st[0:NB] * (1.0 / ALL_ROWS)
-        var = st[NB:2 * NB] * (1.0 / ALL_ROWS) - mean * mean
+        lax.fori_loop(first, stop, step, 0)
+
+    def norm(u, x, st, layer, h):
+        mean = st[0:4] * (1.0 / ALL_ROWS)
+        var = st[4:8] * (1.0 / ALL_ROWS) - mean * mean
         inv = lax.rsqrt(var + BN_EPS)
-        st[0:NB] = mean
-        st[NB:2 * NB] = inv
-        rs[NB * layer:NB * layer + NB] = inv
+        st[0:4] = mean
+        st[4:8] = inv
+        rs[NB * layer + 4 * h:NB * layer + 4 * h + 4] = inv
 
         def step(j, carry):
-            nrm = (u[:, cols(j)] - st[pl.ds(j, 1)]) * st[pl.ds(NB + j, 1)]
+            k = j - 4 * h
+            nrm = (u[:, cols(j)] - st[pl.ds(k, 1)]) * st[pl.ds(4 + k, 1)]
             act = gains[layer][:, cols(j)] * nrm + biases[layer][:, cols(j)]
             u[:, cols(j)] = nrm
             x[:, cols(j)] = jnp.maximum(act, 0.0).astype(BF16)
             return carry
-        lax.fori_loop(0, NB, step, 0)
-
+        lax.fori_loop(4 * h, 4 * h + 4, step, 0)
+
+    low, high, full = pl.ds(0, 1024), pl.ds(1024, 1024), pl.ds(0, DIM)
+    all_f = pl.ds(0, FEAT)
+    red_f1 = [SmallReduce(me, f1[h], odd_land, fa1.at[h], fb1.at[h], h * NB) for h in range(2)]
+    red_f2 = [SmallReduce(me, f2[h], even_land, fa2.at[h], fb2.at[h], h * NB) for h in range(2)]
     load_w1.wait()
     load_h(ha).wait()
-    matmul(hv, w1v, da, f1, mine, False)
     give_h(ha).wait()
     swap_h.start()
     keep_h.start()
-    matmul(hv, w1v, da, f1, theirs, True)
-    SmallReduce(me, f1, odd_land, fa1, fb1).run()
-    norm(da, dzo, f1, 0)
+    for h in range(2):
+        matmul(hv, w1v, da, body, all_f, 4 * h, 4 * h + 4, f1[h])
+        red_f1[h].start(0)
+    for h in range(2):
+        red_f1[h].finish(0)
+        red_f1[h].start(1)
+    red_f1[0].finish(1)
+    norm(da, dzo, f1[0], 0, 0)
+    load_w2a.wait()
+    matmul(dzo, gw, nv, body, low, 0, NB)
+    red_f1[1].finish(1)
+    norm(da, dzo, f1[1], 0, 1)
+    matmul(dzo, gw, nv, body, high, 0, 4, f2[0], 'depth')
+    red_f2[0].start(0)
     save_n1.start()
     keep_h.wait()
     swap_h.wait()
     swap_x1.start()
     keep_x1.start()
-    load_w2a.wait()
-    matmul(dzo, gw, nv, f2, body, False)
-    load_w3a.start()
-    SmallReduce(me, f2, even_land, fa2, fb2).run()
-    norm(nv, dz, f2, 1)
+    matmul(dzo, gw, nv, body, high, 4, 6, f2[1], 'depth')
+    red_f2[0].finish(0)
+    red_f2[0].start(1)
+    matmul(dzo, gw, nv, body, high, 6, NB, f2[1], 'depth')
+    red_f2[1].start(0)
+    for cp in load_w3a:
+        cp.start()
+    red_f2[0].finish(1)
+    norm(nv, dz, f2[0], 1, 0)
+    red_f2[1].finish(0)
+    red_f2[1].start(1)
+    save_n1.wait()
+    load_w3a[0].wait()
+    matmul(dz, gw, da, body, low, 0, 4)
+    red_f2[1].finish(1)
+    norm(nv, dz, f2[1], 1, 1)
     swap_x1.wait()
     swap_x2.start()
     keep_x2.start()
-    load_w3a.wait()
-
-    def z_block(j):
-        res = nn(dz[...], gw[:, cols(j)]).astype(BF16)
+    load_w3a[1].wait()
+
+    def z_block(j, part_done):
+        if part_done:
+            res = (da[:, cols(j)] + nn(dz[:, high], gw[high, cols(j)])).astype(BF16)
+        else:
+            res = nn(dz[...], gw[:, cols(j)]).astype(BF16)
         zd[0:ROWS, cols(j)] = res
         sv[pl.ds(j, 1)] = jnp.sum(res.astype(F32), axis=0, keepdims=True)
 
-    def z_blocks(first):
+    def z_blocks(first, part_done):
         def step(j, carry):
-            z_block(first + j)
+            z_block(first + j, part_done)
             return carry
         lax.fori_loop(0, 2, step, 0)
 
-    z_blocks(0)
+    z_blocks(0, True)
     red0 = SmallReduce(me, sv, odd_land, sa, sb)
     red2 = SmallReduce(me, s2, even_land, sa2, sb2)
     red1 = SmallReduce(me, s1, odd_land, sa1, sb1)
@@ -702,14 +731,14 @@
             span.units(e * LAG, lambda u, w, e=e: sc.step(e, u, w == GRAM, lambda v: final(v, w)))
         span.units(0, lambda u, w: sc.start(u, 0))
         span.at(4, means)
-        span.within(0, 3, lambda: z_blocks(2 * t + 2))
+        span.at(0, lambda: z_blocks(2, True))
+        span.within(1, 3, lambda: z_blocks(2 * t + 2, False))
 
         @functools.partial(span.at, 3)
         def _():
             keep_x1.wait()
             keep_x2.wait()
             swap_x2.wait()
-            save_n1.wait()
             swap_z.start()
 
         span.at(7, swap_z.wait)
@@ -786,12 +815,12 @@
                         pltpu.VMEM((DIM, DIM), F32), pltpu.VMEM((FEAT, DIM), F32),
                         pltpu.VMEM((NB, BLK), F32), pltpu.VMEM((2 * NB, BLK), F32),
                         pltpu.VMEM((3, 2, 32, BLK), F32)]
-        + scatter_scratch(SLOTS) + small_scratch(NB) + [dma((2, 3))] * 4
+        + scatter_scratch(SLOTS) + small_scratch(NB) + [dma((2, 2, 3))] * 4
         + small_scratch(3 * NB) + small_scratch(2 * NB)
         + [pltpu.VMEM((2, 3, 2 * NB, BLK), F32), pltpu.VMEM((2, 3, 3 * NB, BLK), F32),
            pltpu.VMEM((3 * NB, BLK), F32), pltpu.VMEM((2 * NB, BLK), F32),
            dma((2, 6, 2, RING)), dma((2, 6, 2, RING)), dma((2, RING)),
-           dma((2, RING)), dma((10,)), dma((25,)), dma((25,)), dma((NB,))],
+           dma((2, RING)), dma((11,)), dma((25,)), dma((25,)), dma((NB,))],
         compiler_params=pltpu.CompilerParams(collective_id=0, has_side_effects=True, vmem_limit_bytes=VMEM_LIMIT),
         name='train_step',
     )(ha, hb, w1, w2, w3, g1, b1, g2, b2)

time: 431 us -> 428 us (level)
  no operation moved by 1% of the time
where the time goes in v9:
time: 428 us
  Pallas kernels  427 us (100%)
    pallas_call x1, Pallas kernels, train_step(): pl.pallas_call(step_kernel, out_shape=(sds((DIM, DIM), F32), sds((DIM, DI...  401 us
    pallas_call x1, Pallas kernels, finish(): pl.pallas_call(finish_kernel, out_shape=(sds((DIM, DIM), F32), sds((DIM,...  26.1 us

profile of v9, /device:TPU:0, one launch (start us, length us, event | category | flops | bytes accessed | tf_op | source)
XLA Modules:
  0.0 427.8 jit_solution(9852727110033208844)
XLA Ops:
  0.6 400.8 %train_step.1 = (f32[2048,2048]{1,0:T(8,128)}, f32[2048,2048]{1,0:T(8,128)}, f32[512,2048]{1,0:T(8,128)}, f32[1024,2048]{1,0:T(8,128)}, bf16[1024,256]{1,0:T(8,1...) custom-call(bf16[512,512]{1,0:T(8,128)(2,1)} %ha.1, bf16[512,512]{1,0:T(8,128)(2,1)} %hb.1, ...), custom_call_target="tpu_custom_call" | custom-call | tf_op jit(solution)/shard_map/train_step/pallas_call | solution.py:807
  401.5 26.1 %finish.1 = (f32[2048,2048]{1,0:T(8,128)}, f32[2048,2048]{1,0:T(8,128)}, f32[512,2048]{1,0:T(8,128)}, f32[1,2048]{1,0:T(1,128)}, f32[1,2048]{1,0:T(1,128)}, /*in...) custom-call(f32[2048,2048]{1,0:T(8,128)} %get-tuple-element.21.g3, f32[2048,2048]{1,0:T(8,128)} %get-tuple-element.22.g2, ...), custom_call_target="tpu_custom_call" | custom-call | tf_op jit(solution)/shard_map/finish/pallas_call | solution.py:867

commit v10 on v9

--- a/solution.py
+++ b/solution.py
@@ -277,7 +277,7 @@
 
 
 def step_kernel(ha, hb, w1, w2, w3, g1, b1, g2, b2, g3_o, g2_o, g1_o, n1_o, h_o, ho_o, st_o, loss_o,
-                zd, zod, dz, dzo, gw, x2h, x2o, x1h, x1o, g2v, g1v, lacc, rs, stage,
+                zd, zod, dz, dzo, gw, x2h, x2o, x1h, x1o, g2v, g1v, lacc, rs, stage, st_v,
                 part, r1, r2, r3, r4, ssem, rsem, sv, sa, sb, fa1, fb1, fa2, fb2,
                 s2, sa2, sb2, s1, sa1, sb1, odd_land, even_land, e2, e1,
                 asem, bsem, lsem, psem, csem, dsem, esem, wsem):
@@ -451,9 +451,19 @@
     def compute(u, w):
         p = lax.rem(u, SLOTS)
         if w == GRAM:
-            for k in range(2):
-                i, j = block_of(2 * u + k)
-                part[p, k] = tn(zd[0:ROWS, cols(i)], zd[0:ROWS, cols(j)])
+            i, j = block_of(2 * u)
+            i1, j1 = block_of(2 * u + 1)
+
+            @pl.when(i == i1)
+            def _():
+                res = tn(zd[0:ROWS, cols(i)], zd[0:ROWS, pl.ds(pl.multiple_of(j * BLK, BLK), 2 * BLK)])
+                part[p, 0] = res[:, 0:BLK]
+                part[p, 1] = res[:, BLK:2 * BLK]
+
+            @pl.when(i != i1)
+            def _():
+                part[p, 0] = tn(zd[0:ROWS, cols(i)], zd[0:ROWS, cols(j)])
+                part[p, 1] = tn(zd[0:ROWS, cols(i1)], zd[0:ROWS, cols(j1)])
             return
         q = grad_unit(u)[1]
         if w == 2:
@@ -678,6 +688,21 @@
             return carry
         lax.fori_loop(lo, hi, slot, 0)
 
+    out_st = pltpu.make_async_copy(st_v, st_o, csem.at[9])
+
+    def small_results():
+        swap_s2.wait()
+        swap_s1.wait()
+        sum2, sum1 = s2[...] + e2[...], s1[...] + e1[...]
+        for j in range(NB):
+            lanes = slice(j * BLK, (j + 1) * BLK)
+            st_v[0:1, lanes] = sum1[NB + j:NB + j + 1]
+            st_v[1:2, lanes] = sum1[j:j + 1]
+            st_v[2:3, lanes] = sum2[NB + j:NB + j + 1]
+            st_v[3:4, lanes] = sum2[j:j + 1]
+        loss_o[0, 0] = jnp.sum(sum2[2 * NB:])
+        out_st.start()
+
     def run_slot(span, t):
         span.units(11 * LAG + 1, put_end)
         span.units(11 * LAG, cross_end)
@@ -727,6 +752,7 @@
             for j in range(NB):
                 load_w3(j).start()
 
+        span.at(START_2 + 24, small_results)
         for e in (5, 4, 3, 2, 1):
             span.units(e * LAG, lambda u, w, e=e: sc.step(e, u, w == GRAM, lambda v: final(v, w)))
         span.units(0, lambda u, w: sc.start(u, 0))
@@ -788,16 +814,7 @@
 
     for lo, hi in zip(LOOPS, LOOPS[1:]):
         slots(lo, hi)
-    swap_s2.wait()
-    swap_s1.wait()
-    sum2, sum1 = s2[...] + e2[...], s1[...] + e1[...]
-    for j in range(NB):
-        lanes = slice(j * BLK, (j + 1) * BLK)
-        st_o[0:1, lanes] = sum1[NB + j:NB + j + 1]
-        st_o[1:2, lanes] = sum1[j:j + 1]
-        st_o[2:3, lanes] = sum2[NB + j:NB + j + 1]
-        st_o[3:4, lanes] = sum2[j:j + 1]
-    loss_o[0, 0] = jnp.sum(sum2[2 * NB:])
+    out_st.wait()
 
 
 def train_step(ha, hb, w1, w2, w3, g1, b1, g2, b2):
@@ -809,12 +826,12 @@
         out_shape=(sds((DIM, DIM), F32), sds((DIM, DIM), F32), sds((FEAT, DIM), F32), sds((ROWS, DIM), F32),
                    sds((ROWS, 256), BF16), sds((ROWS, 256), BF16), sds((4, DIM), F32), sds((1, 1), F32)),
         in_specs=[ANY] * 5 + [INV] * 4,
-        out_specs=(ANY,) * 6 + (INV, pl.BlockSpec(memory_space=pltpu.SMEM)),
+        out_specs=(ANY,) * 7 + (pl.BlockSpec(memory_space=pltpu.SMEM),),
         scratch_shapes=[pltpu.VMEM((ROWS + 8, DIM), BF16), act, act, act, pltpu.VMEM((DIM, DIM), BF16),
                         piece, piece, piece, piece,
                         pltpu.VMEM((DIM, DIM), F32), pltpu.VMEM((FEAT, DIM), F32),
                         pltpu.VMEM((NB, BLK), F32), pltpu.VMEM((2 * NB, BLK), F32),
-                        pltpu.VMEM((3, 2, 32, BLK), F32)]
+                        pltpu.VMEM((3, 2, 32, BLK), F32), pltpu.VMEM((4, DIM), F32)]
         + scatter_scratch(SLOTS) + small_scratch(NB) + [dma((2, 2, 3))] * 4
         + small_scratch(3 * NB) + small_scratch(2 * NB)
         + [pltpu.VMEM((2, 3, 2 * NB, BLK), F32), pltpu.VMEM((2, 3, 3 * NB, BLK), F32),

time: 428 us -> 428 us (level)
  no operation moved by 1% of the time
where the time goes in v10:
time: 428 us; the launch traced here: 427 us
  Pallas kernels  427 us (100%)
    pallas_call x1, Pallas kernels, train_step(): pl.pallas_call(step_kernel, out_shape=(sds((DIM, DIM), F32), sds((DIM, DI...  401 us
    pallas_call x1, Pallas kernels, finish(): pl.pallas_call(finish_kernel, out_shape=(sds((DIM, DIM), F32), sds((DIM,...  26.1 us

profile of v10, /device:TPU:0, one launch (start us, length us, event | category | flops | bytes accessed | tf_op | source)
XLA Modules:
  0.0 427.5 jit_solution(15374649909332350214)
XLA Ops:
  0.6 400.6 %train_step.1 = (f32[2048,2048]{1,0:T(8,128)}, f32[2048,2048]{1,0:T(8,128)}, f32[512,2048]{1,0:T(8,128)}, f32[1024,2048]{1,0:T(8,128)}, bf16[1024,256]{1,0:T(8,1...) custom-call(bf16[512,512]{1,0:T(8,128)(2,1)} %ha.1, bf16[512,512]{1,0:T(8,128)(2,1)} %hb.1, ...), custom_call_target="tpu_custom_call" | custom-call | tf_op jit(solution)/shard_map/train_step/pallas_call | solution.py:824
  401.2 26.1 %finish.1 = (f32[2048,2048]{1,0:T(8,128)}, f32[2048,2048]{1,0:T(8,128)}, f32[512,2048]{1,0:T(8,128)}, f32[1,2048]{1,0:T(1,128)}, f32[1,2048]{1,0:T(1,128)}, /*in...) custom-call(f32[2048,2048]{1,0:T(8,128)} %get-tuple-element.21.g3, f32[2048,2048]{1,0:T(8,128)} %get-tuple-element.22.g2, ...), custom_call_target="tpu_custom_call" | custom-call | tf_op jit(solution)/shard_map/finish/pallas_call | solution.py:884

commit v11 on v10

--- a/solution.py
+++ b/solution.py
@@ -709,7 +709,7 @@
         for e in (5, 4, 3, 2, 1):
             span.units((5 + e) * LAG, functools.partial(gather, e))
         reds = ((2, red0), (PASS_2 + SPAN_2 - 1, red2), (PASS_1 + SPAN_1 - 1, red1))
-        for first, red in reds:
+        for first, red in reds[:2]:
             @functools.partial(span.at, first + 1)
             def _(red=red):
                 red.finish(0)
@@ -728,12 +728,6 @@
             back_pre(zd, s2, 1, lambda j: swap_du2(j).start())
             load_n1.start()
             swap_s2.start()
-
-        @functools.partial(span.at, PASS_1 + SPAN_1 + 1)
-        def _():
-            back_pre(dz, s1, 0, lambda j: None)
-            swap_du1.start()
-            swap_s1.start()
 
         for j, first in enumerate(DZ_SLOTS):
             span.at(first + 1, lambda j=j: swap_dz(j).wait())
@@ -756,6 +750,21 @@
         for e in (5, 4, 3, 2, 1):
             span.units(e * LAG, lambda u, w, e=e: sc.step(e, u, w == GRAM, lambda v: final(v, w)))
         span.units(0, lambda u, w: sc.start(u, 0))
+        first, red = reds[2]
+
+        @functools.partial(span.at, first + 1)
+        def _():
+            red.finish(0)
+            red.start(1)
+
+        span.at(first + 2, lambda: red.finish(1))
+
+        @functools.partial(span.at, PASS_1 + SPAN_1 + 1)
+        def _():
+            back_pre(dz, s1, 0, lambda j: None)
+            swap_du1.start()
+            swap_s1.start()
+
         span.at(4, means)
         span.at(0, lambda: z_blocks(2, True))
         span.within(1, 3, lambda: z_blocks(2 * t + 2, False))

time: 428 us -> 428 us (level)
  no operation moved by 1% of the time
where the time goes in v11:
time: 428 us
  Pallas kernels  427 us (100%)
    pallas_call x1, Pallas kernels, train_step(): pl.pallas_call(step_kernel, out_shape=(sds((DIM, DIM), F32), sds((DIM, DI...  401 us
    pallas_call x1, Pallas kernels, finish(): pl.pallas_call(finish_kernel, out_shape=(sds((DIM, DIM), F32), sds((DIM,...  26.1 us

profile of v11, /device:TPU:0, one launch (start us, length us, event | category | flops | bytes accessed | tf_op | source)
XLA Modules:
  0.0 427.6 jit_solution(3781905233988967779)
XLA Ops:
  0.6 400.7 %train_step.1 = (f32[2048,2048]{1,0:T(8,128)}, f32[2048,2048]{1,0:T(8,128)}, f32[512,2048]{1,0:T(8,128)}, f32[1024,2048]{1,0:T(8,128)}, bf16[1024,256]{1,0:T(8,1...) custom-call(bf16[512,512]{1,0:T(8,128)(2,1)} %ha.1, bf16[512,512]{1,0:T(8,128)(2,1)} %hb.1, ...), custom_call_target="tpu_custom_call" | custom-call | tf_op jit(solution)/shard_map/train_step/pallas_call | solution.py:833
  401.3 26.1 %finish.1 = (f32[2048,2048]{1,0:T(8,128)}, f32[2048,2048]{1,0:T(8,128)}, f32[512,2048]{1,0:T(8,128)}, f32[1,2048]{1,0:T(1,128)}, f32[1,2048]{1,0:T(1,128)}, /*in...) custom-call(f32[2048,2048]{1,0:T(8,128)} %get-tuple-element.21.g3, f32[2048,2048]{1,0:T(8,128)} %get-tuple-element.22.g2, ...), custom_call_target="tpu_custom_call" | custom-call | tf_op jit(solution)/shard_map/finish/pallas_call | solution.py:893
